TPU v7x, 32 devices: a whole 2x2x4 slice. The times are simulated.
32 devices in a mesh: dp: 8 (over z, core), section: 4 (over y, x).
Axes of the slice: x: 2, y: 2, z: 4, core: 2. Of those that a mesh axis runs over, the one named last changes fastest.
Arguments:
- layer_inputs: bfloat16 [4, 2, 16, 32, 4096], P('section', None, 'dp'), may hold values from -6 to 6
- saved_queries: bfloat16 [4, 2, 16, 32, 128], P('section', None, 'dp'), may hold values from -16 to 16
- saved_keys: bfloat16 [4, 2, 16, 32, 128], P('section', None, 'dp'), may hold values from -16 to 16
- held_weights: bfloat16 [4, 2, 2, 4096, 128], P('section'), may hold values from -0.15625 to 0.15625
- cotangent: bfloat16 [2, 16, 32, 4096], P(None, 'dp'), may hold values from -6 to 6
- valid_lengths: int32 [2, 16], P(None, 'dp'), may hold values from 2 to 32, as said below
Outputs:
- input_grads: bfloat16 [4, 2, 16, 32, 4096], P('section', None, 'dp')
- weight_grads: float32 [4, 2, 4096, 128], P('section', None, 'dp')
Inputs may be any that keep to these rules, and one draw needn't show every extreme that they name: `valid_lengths`: some sequence has 32 valid tokens.
All inputs are finite; a program needn't handle non-finite values.
Results may differ from a plain program's by a relative error of at most 0.014.
Values may be sent and summed in bfloat16 or wider, within the bound.
No kernel may reach another device: no remote copies, remote signals or barrier semaphores. Data moves between devices by JAX's collectives and lax.ppermute only.
A program may use at most 64 MiB of HBM per device.

v0:
```python
import functools
import math

import jax
import jax.numpy as jnp
from jax import lax
from jax.experimental import pallas as pl
from jax.experimental.pallas import tpu as pltpu
from jax.sharding import PartitionSpec as P


def passed_along(block, axis, distance):
    devices = range(lax.axis_size(axis))
    route = [(i - distance, i) for i in devices if i - distance in devices]
    return lax.ppermute(block, axis, route)


def from_partner(block, axis, bit):
    count = lax.axis_size(axis)
    route = []
    for low in range(count):
        high = low | 1 << bit
        if high != low and high < count:
            route += [(low, high), (high, low)]
    return lax.ppermute(block, axis, route)


def attention_weights(queries, key_vectors, valid_lengths):
    length = queries.shape[-2]
    scores = jnp.einsum(
        "nmth,nmsh->nmts", queries, key_vectors, preferred_element_type=jnp.float32
    ) / math.sqrt(queries.shape[-1])
    row_pos = lax.broadcasted_iota(jnp.int32, (length, length), 0)
    col_pos = lax.broadcasted_iota(jnp.int32, (length, length), 1)
    allowed = (col_pos <= row_pos)[None, None] & (
        col_pos[None, None] < valid_lengths[:, :, None, None]
    )
    scores = jnp.where(allowed, scores, -jnp.inf)
    row_max = jnp.max(scores, axis=-1, keepdims=True)
    raised = jnp.where(allowed, jnp.exp(scores - row_max), 0.0)
    return (raised / jnp.sum(raised, axis=-1, keepdims=True)).astype(jnp.bfloat16)


def reduced(layer_inputs, saved_queries, saved_keys, held_weights, cotangent, valid_lengths):
    sections = lax.axis_size("section")
    position = lax.axis_index("section")
    inputs = layer_inputs[0]
    value_w = held_weights[0, :, 0]
    output_w = held_weights[0, :, 1]
    attend = attention_weights(saved_queries[0], saved_keys[0], valid_lengths)
    micro_count = inputs.shape[1]
    length = inputs.shape[2]
    model_width = inputs.shape[3]
    head_size = value_w.shape[2]
    values = jnp.einsum(
        "nmld,ndh->nmlh", inputs, value_w, preferred_element_type=jnp.float32
    ).astype(jnp.bfloat16)
    mixtures = jnp.einsum(
        "nmts,nmsh->nmth", attend, values, preferred_element_type=jnp.float32
    ).astype(jnp.bfloat16)
    is_end = [position == sections - 1, position == 0]
    starts = [sections - 1 - position, position]

    def make_compute(direction):

        def compute(operands):
            grads, uppers, vgrads, incoming, index = operands
            fresh = lax.dynamic_index_in_dim(cotangent[direction], index, 0, keepdims=False)
            upstream = jnp.where(is_end[direction], fresh, incoming)
            weights_now = lax.dynamic_index_in_dim(attend[direction], index, 0, keepdims=False)
            out_grad = jnp.dot(
                upstream, output_w[direction], preferred_element_type=jnp.float32
            ).astype(jnp.bfloat16)
            val_grad = jnp.einsum(
                "ts,th->sh", weights_now, out_grad, preferred_element_type=jnp.float32
            ).astype(jnp.bfloat16)
            branch = jnp.einsum(
                "lh,dh->ld", val_grad, value_w[direction], preferred_element_type=jnp.float32
            )
            grad_input = (upstream.astype(jnp.float32) + branch).astype(jnp.bfloat16)
            grads = lax.dynamic_update_index_in_dim(grads, grad_input, index, 0)
            uppers = lax.dynamic_update_index_in_dim(uppers, upstream, index, 0)
            vgrads = lax.dynamic_update_index_in_dim(vgrads, val_grad, index, 0)
            return (grad_input, (grads, uppers, vgrads))

        return compute

    def skip(operands):
        grads, uppers, vgrads, incoming, _ = operands
        return (jnp.zeros_like(incoming), (grads, uppers, vgrads))

    def advance(moment, received, buffers):
        outgoing = []
        updated = []
        for direction in range(2):
            micro_id = moment - starts[direction]
            active = (micro_id >= 0) & (micro_id < micro_count)
            clipped = jnp.clip(micro_id, 0, micro_count - 1)
            grads, uppers, vgrads = buffers[direction]
            sent_now, fresh_buffers = lax.cond(
                active,
                make_compute(direction),
                skip,
                (grads, uppers, vgrads, received[direction], clipped),
            )
            outgoing.append(sent_now)
            updated.append(fresh_buffers)
        return (jnp.stack(outgoing), tuple(updated))

    big_zero = jnp.zeros((micro_count, length, model_width), jnp.bfloat16)
    small_zero = jnp.zeros((micro_count, length, head_size), jnp.bfloat16)
    buffers = ((big_zero, big_zero, small_zero), (big_zero, big_zero, small_zero))
    sent, buffers = advance(
        jnp.int32(0), jnp.zeros((2, length, model_width), jnp.bfloat16), buffers
    )

    def loop_body(moment, carried):
        outgoing, held = carried
        from_next = passed_along(outgoing[0], "section", -1)
        from_prev = passed_along(outgoing[1], "section", 1)
        return advance(moment, jnp.stack([from_next, from_prev]), held)

    sent, buffers = lax.fori_loop(1, sections + micro_count - 1, loop_body, (sent, buffers))
    grads_in = jnp.stack([buffers[0][0], buffers[1][0]])
    upstreams = jnp.stack([buffers[0][1], buffers[1][1]])
    val_grads = jnp.stack([buffers[0][2], buffers[1][2]])
    flat_in = inputs.reshape(2, micro_count * length, model_width)
    flat_up = upstreams.reshape(2, micro_count * length, model_width)
    flat_mix = mixtures.reshape(2, micro_count * length, head_size)
    flat_vg = val_grads.reshape(2, micro_count * length, head_size)
    grad_value = jnp.einsum("ntd,nth->dnh", flat_in, flat_vg, preferred_element_type=jnp.float32)
    grad_output = jnp.einsum("ntd,nth->dnh", flat_up, flat_mix, preferred_element_type=jnp.float32)
    summed = lax.psum_scatter(
        jnp.stack([grad_value, grad_output], axis=2).reshape(
            model_width // lax.axis_size("dp") * lax.axis_size("dp"), 4 * head_size
        ),
        "dp",
        scatter_dimension=0,
        tiled=True,
    )
    summed = summed.reshape(-1, 2, 2, head_size)
    own_part = summed[:, 0]
    mirror_part = summed[:, 1]
    for bit_no in range(sections.bit_length() - 1):
        mirror_part = from_partner(mirror_part.astype(jnp.bfloat16), "section", bit_no).astype(
            mirror_part.dtype
        )
    combined = own_part + mirror_part
    weight_grads = jnp.transpose(combined, (1, 0, 2))[None]
    return (grads_in[None], weight_grads)


def swapped(block, axis, mask):
    return lax.ppermute(block, axis, [(i, i ^ mask) for i in range(lax.axis_size(axis))])


def shifted(block, distance):
    count = lax.axis_size("dp")
    return lax.ppermute(block, "dp", [(i, (i + 2 * distance) % count) for i in range(count)])


def contract(left, right, left_dim, right_dim):
    return lax.dot_general(
        left, right, (((left_dim,), (right_dim,)), ((), ())), preferred_element_type=jnp.float32
    )


def block_attention(queries, key_vectors, valid_lengths):
    ways, seqs, length, head = queries.shape
    tokens = seqs * length
    scores = jnp.einsum(
        "nth,nsh->nts",
        queries.reshape(ways, tokens, head),
        key_vectors.reshape(ways, tokens, head),
        preferred_element_type=jnp.float32,
    ) / math.sqrt(head)
    row = lax.broadcasted_iota(jnp.int32, (tokens, tokens), 0)
    col = lax.broadcasted_iota(jnp.int32, (tokens, tokens), 1)
    bound = jnp.repeat(valid_lengths, length, axis=1)[:, None, :]
    allowed = ((row // length == col // length) & (col <= row))[None] & (
        (col % length)[None] < bound
    )
    scores = jnp.where(allowed, scores, -jnp.inf)
    row_max = jnp.max(scores, axis=-1, keepdims=True)
    raised = jnp.where(allowed, jnp.exp(scores - row_max), 0.0)
    return (raised / jnp.sum(raised, axis=-1, keepdims=True)).astype(jnp.bfloat16)


def chain_kernel(sections, tokens, head, place, *refs):
    parts = refs[:sections]
    gathered, steer, own = refs[sections:]
    products = (sections - 1) * head

    def at(here):
        mine = [[None] * sections, [None] * sections]
        for way in range(2):
            order = range(sections - 1, -1, -1) if way == 0 else range(sections)
            done = []
            for holder in order:
                part = parts[here ^ holder]
                first = products + way * tokens
                total = part[first : first + tokens, :].astype(jnp.float32)
                for other in done:
                    block = (other ^ holder) - 1
                    total += contract(
                        mine[way][other], part[block * head : (block + 1) * head, :], 1, 0
                    )
                base = products + 2 * tokens
                weights = part[base : base + tokens, way * tokens : (way + 1) * tokens]
                mine[way][holder] = contract(weights, total.astype(jnp.bfloat16), 0, 0).astype(
                    jnp.bfloat16
                )
                done.append(holder)
        zero = jnp.zeros((tokens, head), jnp.bfloat16)
        for far in range(sections):
            inside = here + far < sections
            gathered[0, far] = mine[0][here + far] if inside else zero
            gathered[1, far] = mine[1][sections - 1 - here - far] if inside else zero
        mirror = here ^ (sections - 1)
        base = products + 2 * tokens + tokens
        gathered[0, sections] = parts[0][base : base + tokens, :]
        gathered[1, sections] = parts[here ^ mirror][base + tokens : base + 2 * tokens, :]
        for way in range(2):
            own[way] = mine[way][here]
        for mask in range(1, sections):
            other = here ^ mask
            way = 0 if other > here else 1
            lanes = slice((mask - 1) * head, mask * head)
            steer[way * tokens : (way + 1) * tokens, lanes] = mine[way][other]
            steer[(1 - way) * tokens : (2 - way) * tokens, lanes] = zero

    for here in range(sections):

        @pl.when(place[0] == here)
        def _():
            at(here)


def input_kernel(sections, tokens, place, cot, steer, own, held, *refs):
    near, far = refs[: sections - 1], refs[sections - 1 : 2 * sections - 2]
    out = refs[2 * sections - 2]
    width = near[0].shape[1]
    core = place[1]
    for which, fetched in ((core, near), (1 - core, far)):
        start = pl.multiple_of(which * width, 128)
        weights = jnp.concatenate([block[0] for block in fetched], axis=1)
        total = contract(steer[...], weights, 1, 1)
        for way in range(2):
            branch = contract(own[way], held[way, 0, pl.ds(start, width), :], 1, 1)
            branch += total[way * tokens : (way + 1) * tokens]
            base = cot[way, :, pl.ds(start, width)].astype(jnp.float32)
            out[way, :, pl.ds(start, width)] = (base + branch).astype(jnp.bfloat16)


def pick_weights(sections, place, halved, *refs):
    outs, sems = refs[: sections - 1], refs[sections - 1]
    here, core = place[0], place[1]
    copies = []
    for mask in range(sections - 1, 0, -1):
        way = jnp.where((here ^ mask) < here, 0, 1)
        copy = pltpu.make_async_copy(
            halved.at[way, 0, :, core], outs[mask - 1], sems.at[mask - 1]
        )
        copy.start()
        copies.append(copy)
    for copy in copies:
        copy.wait()


def carried_out(copies):
    for copy in copies:
        copy.start()
    for copy in copies:
        copy.wait()


def pick_outputs(place, halved, out, sem):
    carried_out([pltpu.make_async_copy(halved.at[:, 1, :, place[1]], out, sem)])


def pick_columns(steps, width, place, inputs, cot, *refs):
    outs, sems = refs[:steps], refs[steps]
    copies = []
    for distance in range(steps):
        start = pl.multiple_of((place[2] + distance) % steps * 2 * width, 128)
        copies.append(
            pltpu.make_async_copy(
                inputs.at[:, :, pl.ds(start, 2 * width)],
                outs[distance].at[0:2],
                sems.at[3 * distance],
            )
        )
        for way in range(2):
            half = pl.multiple_of(start + place[3 + way] * width, 128)
            copies.append(
                pltpu.make_async_copy(
                    cot.at[way, :, pl.ds(half, width)],
                    outs[distance].at[2, :, way * width : (way + 1) * width],
                    sems.at[3 * distance + 1 + way],
                )
            )
    carried_out(copies)


def pick_moving(steps, *refs):
    sources, upward, sems = refs[:steps], refs[steps], refs[steps + 3]
    width = upward.shape[-1] // 2
    copies = []
    for step, source in enumerate(sources):
        copies.append(pltpu.make_async_copy(source.at[1], upward.at[step], sems.at[3 * step]))
        for way in range(2):
            half = source.at[2, :, way * width : (way + 1) * width]
            copies.append(
                pltpu.make_async_copy(
                    half, refs[steps + 1 + way].at[step], sems.at[3 * step + 1 + way]
                )
            )
    carried_out(copies)


def product_kernel(sections, steps, place, outputs, *refs):
    fetched, out = refs[: sections - 1], refs[sections - 1]
    for mask in range(1, sections):
        way = jnp.where((place[0] ^ mask) > place[0], 0, 1)
        total = None
        for step in range(steps):
            term = contract(fetched[mask - 1][step], outputs[way, step], 0, 0)
            total = term if total is None else total + term
        out[mask - 1] = total


def weight_kernel(sections, steps, tokens, place, *refs):
    columns = refs[: 2 * steps]
    mirrored, lent = refs[2 * steps : 2 * steps + 2], refs[2 * steps + 2 : 2 * steps + 6]
    sent = refs[2 * steps + 6 : 4 * steps + 6]
    held, out, lefts, rights, steers = refs[4 * steps + 6 :]
    width, head = out.shape[1:]
    every = 2 * steps * tokens
    lanes = pl.ds(pl.multiple_of(place[1] * width, 128), width)
    for index in range(2 * steps):
        rows = slice(index * tokens, (index + 1) * tokens)
        for way in range(2):
            for far in range(1, sections):
                steers[way, rows, (far - 1) * head : far * head] = sent[index][way, far]
            both = slice(way * every + index * tokens, way * every + (index + 1) * tokens)
            lefts[0, both, :] = sent[index][way, 0]
            lefts[1, both, :] = sent[index][way, sections]
        rights[rows, :] = columns[index][0, :, lanes]
        rows = slice(every + index * tokens, every + (index + 1) * tokens)
        rights[rows, :] = mirrored[index // steps][index % steps, :, lanes]
    out[0] = contract(lefts[0], rights[...], 0, 0).T
    for index in range(2 * steps):
        for way in range(2):
            both = slice(way * every + index * tokens, way * every + (index + 1) * tokens)
            half = slice(way * width, (way + 1) * width)

            @pl.when(place[3 + way] == place[1])
            def _():
                rights[both, :] = columns[index][2, :, half]

            @pl.when(place[3 + way] != place[1])
            def _():
                rights[both, :] = lent[2 * (index // steps) + way][index % steps]

    for way in range(2):
        rows = slice(way * every, (way + 1) * every)
        total = contract(steers[way], held[way], 1, 1)
        rights[rows, :] = (rights[rows, :].astype(jnp.float32) + total).astype(jnp.bfloat16)
    out[1] = contract(lefts[1], rights[...], 0, 0).T


def gathered(layer_inputs, saved_queries, saved_keys, held_weights, cotangent, valid_lengths):
    sections = lax.axis_size("section")
    replicas = lax.axis_size("dp")
    steps = replicas // 2
    here = lax.axis_index("section")
    core = lax.axis_index("dp") % 2
    depth = lax.axis_index("dp") // 2
    inputs = layer_inputs[0]
    held = held_weights[0]
    seqs, length, model_width = inputs.shape[1:]
    tokens = seqs * length
    head = held.shape[-1]
    width = model_width // replicas
    inputs = inputs.reshape(2, tokens, model_width)
    cot = cotangent.reshape(2, tokens, model_width)
    halved = held.reshape(2, 2, steps, 2, width, head)
    asides = (sections // 2, 1)
    place = jnp.stack([here, core, depth] + [jnp.where(here & aside, 1, 0) for aside in asides])
    memory = pl.BlockSpec(memory_space=pltpu.VMEM)
    scalars = pl.BlockSpec(memory_space=pltpu.SMEM)
    anywhere = pl.BlockSpec(memory_space=pl.ANY)
    hbm = pl.BlockSpec(memory_space=pltpu.HBM)

    picked = pl.pallas_call(
        functools.partial(pick_weights, sections),
        in_specs=[scalars, hbm],
        out_specs=[memory] * (sections - 1),
        out_shape=[jax.ShapeDtypeStruct((steps, width, head), jnp.bfloat16)] * (sections - 1),
        scratch_shapes=[pltpu.SemaphoreType.DMA((sections - 1,))],
        name="pick_weights",
        compiler_params=pltpu.CompilerParams(vmem_limit_bytes=61 << 20),
    )(place, halved)
    fetched = [None] * sections
    for mask in range(sections - 1, 0, -1):
        fetched[mask] = swapped(picked[mask - 1], "section", mask)

    picked = pl.pallas_call(
        functools.partial(pick_columns, steps, width),
        in_specs=[scalars] + [hbm] * 2,
        out_specs=[memory] * steps,
        out_shape=[jax.ShapeDtypeStruct((3, tokens, 2 * width), jnp.bfloat16)] * steps,
        scratch_shapes=[pltpu.SemaphoreType.DMA((3 * steps,))],
        name="pick_columns",
        compiler_params=pltpu.CompilerParams(vmem_limit_bytes=8 << 20),
    )(place, inputs, cot)
    near_columns = [picked[0]]
    for distance in range(1, steps):
        near_columns.append(shifted(picked[distance], distance))

    attend = block_attention(saved_queries[0], saved_keys[0], valid_lengths)
    values = jnp.einsum(
        "ntd,ndh->nth", inputs, held[:, 0], preferred_element_type=jnp.float32
    ).astype(jnp.bfloat16)
    mixtures = jnp.einsum(
        "nts,nsh->nth", attend, values, preferred_element_type=jnp.float32
    ).astype(jnp.bfloat16)
    first_grad = jnp.einsum(
        "ntd,ndh->nth", cot, held[:, 1], preferred_element_type=jnp.float32
    ).astype(jnp.bfloat16)

    outputs = pl.pallas_call(
        pick_outputs,
        in_specs=[scalars, hbm],
        out_specs=memory,
        out_shape=jax.ShapeDtypeStruct((2, steps, width, head), jnp.bfloat16),
        scratch_shapes=[pltpu.SemaphoreType.DMA],
        name="pick_outputs",
        compiler_params=pltpu.CompilerParams(vmem_limit_bytes=58 << 20),
    )(place, halved)
    products = pl.pallas_call(
        functools.partial(product_kernel, sections, steps),
        in_specs=[scalars] + [memory] * sections,
        out_specs=memory,
        out_shape=jax.ShapeDtypeStruct((sections - 1, head, head), jnp.float32),
        name="products",
        compiler_params=pltpu.CompilerParams(vmem_limit_bytes=8 << 20),
    )(place, outputs, *fetched[1:])
    products = (products + swapped(products, "dp", 1)).astype(jnp.bfloat16)
    lent_back = [None] * sections
    for mask in range(1, sections):
        lent_back[mask] = swapped(fetched[mask], "dp", 1)

    part = jnp.concatenate(
        [
            products.reshape(-1, head),
            first_grad.reshape(-1, head),
            jnp.pad(
                jnp.concatenate([attend[0], attend[1]], axis=1), ((0, 0), (0, head - 2 * tokens))
            ),
            mixtures.reshape(-1, head),
        ]
    )
    rows = part.shape[0] - 2 * tokens
    parts = [part]
    for mask in range(1, sections):
        parts.append(swapped(part if mask == sections - 1 else part[:rows], "section", mask))

    upward, *sideways = pl.pallas_call(
        functools.partial(pick_moving, steps),
        in_specs=[anywhere] * steps,
        out_specs=[memory] * 3,
        out_shape=[jax.ShapeDtypeStruct((steps, tokens, 2 * width), jnp.bfloat16)]
        + [jax.ShapeDtypeStruct((steps, tokens, width), jnp.bfloat16)] * 2,
        scratch_shapes=[pltpu.SemaphoreType.DMA((3 * steps,))],
        name="pick_moving",
        compiler_params=pltpu.CompilerParams(vmem_limit_bytes=8 << 20),
    )(*near_columns)
    near_mirror = swapped(upward, "section", sections - 1)
    near_aside, far_aside = [], []
    for way in range(2):
        near_aside.append(swapped(sideways[way], "section", asides[way]))
    far_mirror = swapped(near_mirror, "dp", 1)
    for way in range(2):
        far_aside.append(swapped(near_aside[way], "dp", 1))
    far_columns = []
    for distance in range(steps):
        far_columns.append(swapped(near_columns[distance], "dp", 1))
    own_slice = lax.dynamic_slice(
        halved, (1, 0, depth, core, 0, 0), (1, 1, 1, 1, width, head)
    ).reshape(width, head)
    lent = [own_slice]
    for mask in range(1, sections):
        route = [
            (i, i ^ mask) for i in range(sections) if i ^ mask < i < sections - 1 - (i ^ mask)
        ]
        lent.append(lax.ppermute(own_slice, "section", route) if route else None)

    sent, steer, own = pl.pallas_call(
        functools.partial(chain_kernel, sections, tokens, head),
        in_specs=[scalars] + [memory] * sections,
        out_specs=(memory, memory, memory),
        out_shape=(
            jax.ShapeDtypeStruct((2, sections + 1, tokens, head), jnp.bfloat16),
            jax.ShapeDtypeStruct((2 * tokens, (sections - 1) * head), jnp.bfloat16),
            jax.ShapeDtypeStruct((2, tokens, head), jnp.bfloat16),
        ),
        name="chain",
        compiler_params=pltpu.CompilerParams(vmem_limit_bytes=8 << 20),
    )(place, *parts)

    near_sent = [sent]
    for distance in range(1, steps):
        near_sent.append(shifted(sent, distance))
    far_sent = []
    for distance in range(steps):
        far_sent.append(swapped(near_sent[distance], "dp", 1))

    grads_in = pl.pallas_call(
        functools.partial(input_kernel, sections, tokens),
        grid=(steps,),
        in_specs=[
            scalars,
            pl.BlockSpec((2, tokens, 2 * width), lambda i: (0, 0, i)),
            pl.BlockSpec((2 * tokens, (sections - 1) * head), lambda i: (0, 0)),
            pl.BlockSpec((2, tokens, head), lambda i: (0, 0, 0)),
            pl.BlockSpec((2, 1, 2 * width, head), lambda i: (0, 0, i, 0)),
        ]
        + [pl.BlockSpec((1, width, head), lambda i: (i, 0, 0))] * (2 * sections - 2),
        out_specs=pl.BlockSpec((2, tokens, 2 * width), lambda i: (0, 0, i)),
        out_shape=jax.ShapeDtypeStruct((2, tokens, model_width), jnp.bfloat16),
        name="input_side",
        compiler_params=pltpu.CompilerParams(vmem_limit_bytes=61 << 20),
    )(place, cot, steer, own, held, *fetched[1:], *lent_back[1:])

    sliced = [own_slice] + [
        lax.dynamic_index_in_dim(block, depth, 0, keepdims=False) for block in fetched[1:]
    ]
    down = jnp.stack(sliced)
    up = jnp.stack(
        [own_slice]
        + [
            sliced[mask]
            if lent[mask] is None
            else jnp.where((here ^ mask) < here, sliced[mask], lent[mask])
            for mask in range(1, sections)
        ]
    )
    nearby = []
    for distance in range(1, sections):
        inside = here + distance < sections
        below = jnp.where(inside, here ^ (here + distance), 0)
        above = jnp.where(inside, here ^ (sections - 1 - here - distance), 0)
        nearby.append(
            jnp.stack(
                [
                    lax.dynamic_index_in_dim(down, below, 0, keepdims=False),
                    lax.dynamic_index_in_dim(up, above, 0, keepdims=False),
                ]
            )
        )
    nearby = jnp.concatenate(nearby, axis=2)

    every = replicas * tokens
    weight_grads = pl.pallas_call(
        functools.partial(weight_kernel, sections, steps, tokens),
        in_specs=[scalars] + [memory] * (4 * steps + 7),
        out_specs=memory,
        out_shape=jax.ShapeDtypeStruct((2, width, head), jnp.float32),
        scratch_shapes=[
            pltpu.VMEM((2, 2 * every, head), jnp.bfloat16),
            pltpu.VMEM((2 * every, width), jnp.bfloat16),
            pltpu.VMEM((2, every, (sections - 1) * head), jnp.bfloat16),
        ],
        name="weight_side",
        compiler_params=pltpu.CompilerParams(vmem_limit_bytes=20 << 20),
    )(
        place,
        *near_columns,
        *far_columns,
        near_mirror,
        far_mirror,
        *near_aside,
        *far_aside,
        *near_sent,
        *far_sent,
        nearby,
    )
    shape = (1, 2, seqs, length, model_width)
    return (grads_in.reshape(shape), weight_grads[None])


def shards(*operands):
    layer_inputs, held_weights = operands[0], operands[3]
    sections = lax.axis_size("section")
    replicas = lax.axis_size("dp")
    seqs, length, model_width = layer_inputs.shape[2:]
    head = held_weights.shape[-1]
    every_token = replicas * seqs * length
    moved = 2 * every_token * ((sections + 1) * head + 2 * model_width // replicas) * 2
    partial_sums = 4 * model_width * head * 4
    even = replicas % 2 == 0 and sections > 1 and sections & (sections - 1) == 0
    if even and moved < partial_sums and 2 * seqs * length <= head:
        return gathered(*operands)
    return reduced(*operands)


def solution(mesh):
    return jax.shard_map(
        shards,
        mesh=mesh,
        in_specs=(
            P("section", None, "dp", None, None),
            P("section", None, "dp", None, None),
            P("section", None, "dp", None, None),
            P("section", None, None, None, None),
            P(None, "dp", None, None),
            P(None, "dp"),
        ),
        out_specs=(P("section", None, "dp", None, None), P("section", None, "dp", None)),
        check_vma=False,
    )
```

profile of v0, /device:TPU:9, one launch (start us, length us, event | category | flops | bytes accessed | tf_op | source)
XLA Modules:
  0.0 142.4 jit_solution(787449156149364345)
XLA Ops:
  1.3 3.6 %pick_weights.1 = (bf16[4,512,128]{2,1,0:T(8,128)(2,1)}, bf16[4,512,128]{2,1,0:T(8,128)(2,1)}, bf16[4,512,128]{2,1,0:T(8,128)(2,1)}) custom-call(s32[5]{0:T(128)} %stack.54.place, bf16[2,2,4,2,512,128]{5,4,3,2,1,0:T(8,128)(2,1)} %bitcast.59), custom_call_target="tpu_custom_call" | custom-call | tf_op jit(solution)/shard_map/pick_weights/pallas_call | solution.py:395
  6.0 1.3 collective-permute-start.1
  8.8 1.8 %pick_columns.1 = (bf16[3,64,1024]{2,1,0:T(8,128)(2,1)S(1)}, bf16[3,64,1024]{2,1,0:T(8,128)(2,1)}, bf16[3,64,1024]{2,1,0:T(8,128)(2,1)}, bf16[3,64,1024]{2,1,0:T(8,128)(2,1)S(1)}) custom-call(s32[5]{0:T(128)S(1)} %copy-done.29, bf16[2,64,4096]{2,1,0:T(8,128)(2,1)S(1)} %bitcast.58, bf16[2,64,4096]{2,1,0:T(8,128)(2,1)S(1)} %bitcast.55), custom_call_target="tpu_custom_call" | custom-call | tf_op jit(solution)/shard_map/pick_columns/pallas_call | solution.py:408
  11.3 1.3 collective-permute-start.10
  13.9 1.6 %fusion.14 = (f32[2,64]{1,0:T(2,128)S(1)}, f32[2,64,64]{2,1,0:T(8,128)}) fusion(s32[2,64]{1,0:T(2,128)S(1)} %lt.74, s32[64,64]{1,0:T(8,128)S(1)} %broadcast_select_fusion, pred[64,64]{1,0:T(8,128)(4,1)S(1)} %fusion.13, bf16[2,64,128]{2,1,0:T(8,128)(2,1)S(1)} %bitcast.53, bf16[2,64,128]{2,1,0:T(8,128)(2,1)} %bitcast.72), kind=kOutput, calls=%fused_computation.53 | convolution fusion | flops 2170943 | bytes 119808 | tf_op jit(solution)/shard_map/sub | solution.py:185
  16.5 4.3 %collective-permute-done.10.refs_1_ = bf16[3,64,1024]{2,1,0:T(8,128)(2,1)S(1)} collective-permute-done((bf16[3,64,1024]{2,1,0:T(8,128)(2,1)}, bf16[3,64,1024]{2,1,0:T(8,128)(2,1)S(1)}, u32[]{:S(2)}, u32[]{:S(2)}) %collective-permute-start.10) | collective-permute-done | bytes 393248 | tf_op jit(solution)/shard_map/ppermute | solution.py:159
  20.8 2.4 %collective-permute-start.12 = (bf16[3,64,1024]{2,1,0:T(8,128)(2,1)}, bf16[3,64,1024]{2,1,0:T(8,128)(2,1)}, u32[]{:S(2)}, u32[]{:S(2)}) collective-permute-start(bf16[3,64,1024]{2,1,0:T(8,128)(2,1)} %copy-done.32), channel_id=1, source_target_pairs={{0,24},{4,28},{8,0},{12,4},{16,8},{20,12},{24,16},{28,20},{1,25},{... | collective-permute-start | bytes 1179656 | tf_op jit(solution)/shard_map/ppermute | solution.py:159
  23.2 3.1 %convolution_convert_fusion = bf16[2,64,128]{2,1,0:T(8,128)(2,1)} fusion(bf16[2,64,64]{2,1,0:T(8,128)(2,1)S(1)} %divide_convert_fusion, bf16[2,64,4096]{2,1,0:T(8,128)(2,1)} %bitcast.57, bf16[2,2,4096,128]{3,2,1,0:T(8,128)(2,1)} %bitcast.60), kind=kOutput, calls=%fused_computation.12 | convolution fusion | flops 136347648 | bytes 3194880 | tf_op jit(solution)/shard_map/nts,nsh->nth/dot_general | solution.py:425
  26.3 19.0 %collective-permute-done.11.refs_2_ = bf16[3,64,1024]{2,1,0:T(8,128)(2,1)} collective-permute-done((bf16[3,64,1024]{2,1,0:T(8,128)(2,1)}, bf16[3,64,1024]{2,1,0:T(8,128)(2,1)}, u32[]{:S(2)}, u32[]{:S(2)}) %collective-permute-start.11) | collective-permute-done | bytes 393248 | tf_op jit(solution)/shard_map/ppermute | solution.py:159
  45.3 2.3 %collective-permute-start.13 = (bf16[3,64,1024]{2,1,0:T(8,128)(2,1)S(1)}, bf16[3,64,1024]{2,1,0:T(8,128)(2,1)}, u32[]{:S(2)}, u32[]{:S(2)}) collective-permute-start(bf16[3,64,1024]{2,1,0:T(8,128)(2,1)S(1)} %get-tuple-element.20.refs_0_), channel_id=1, source_target_pairs={{0,4},{4,0},{8,12},{12,8},{16,20},{20,16},{24,28},{28,24},{1,5},{5... | collective-permute-start | bytes 1179656 | tf_op jit(solution)/shard_map/ppermute | solution.py:154
  47.5 2.1 %fusion.7 = bf16[2,64,128]{2,1,0:T(8,128)(2,1)S(1)} fusion(bf16[2,64,4096]{2,1,0:T(8,128)(2,1)S(1)} %bitcast.56, bf16[2,2,4096,128]{3,2,1,0:T(8,128)(2,1)} %bitcast.61), kind=kOutput, calls=%fused_computation.10 | convolution fusion | flops 134234112 | bytes 3178496 | tf_op jit(solution)/shard_map/ntd,ndh->nth/dot_general | solution.py:428
  49.7 2.4 %pick_moving.1 = (bf16[4,64,1024]{2,1,0:T(8,128)(2,1)}, bf16[4,64,512]{2,1,0:T(8,128)(2,1)S(1)}, bf16[4,64,512]{2,1,0:T(8,128)(2,1)S(1)}) custom-call(bf16[3,64,1024]{2,1,0:T(8,128)(2,1)S(1)} %get-tuple-element.20.refs_0_, bf16[3,64,1024]{2,1,0:T(8,128)(2,1)S(1)} %collective-permute-done.10.refs_1_, bf16[3,64,1024]{2,1,0:T(8,128)(2,1)} %collective-permute-done.11.refs_2_, ...), custom_call_target="tpu_custom_call" | custom-call | tf_op jit(solution)/shard_map/pick_moving/pallas_call | solution.py:469
  53.1 1.6 %dynamic-slice_bitcast_fusion = (bf16[512,128]{1,0:T(8,128)(2,1)S(1)}, bf16[1,512,128]{2,1,0:T(8,128)(2,1)}) fusion(bf16[2,2,4,2,512,128]{5,4,3,2,1,0:T(8,128)(2,1)} %bitcast.62, s32[]{:T(128)S(6)} %select_n.121, s32[]{:T(128)S(6)} %select_n.122), kind=kLoop, calls=%fused_computation.27 | loop fusion | bytes 393224 | tf_op jit(solution)/shard_map/reshape | solution.py:491
  54.8 3.0 %pick_outputs.1.outputs = bf16[2,4,512,128]{3,2,1,0:T(8,128)(2,1)} custom-call(s32[5]{0:T(128)} %stack.54.place, bf16[2,2,4,2,512,128]{5,4,3,2,1,0:T(8,128)(2,1)} %bitcast.63), custom_call_target="tpu_custom_call" | custom-call | tf_op jit(solution)/shard_map/pick_outputs/pallas_call | solution.py:432
  57.8 1.3 collective-permute-start.31
  59.1 1.3 collective-permute-start.30
  64.5 1.3 collective-permute-done.30
  68.2 15.8 %collective-permute-done.20.refs_11_ = bf16[4,64,512]{2,1,0:T(8,128)(2,1)S(1)} collective-permute-done((bf16[4,64,512]{2,1,0:T(8,128)(2,1)S(1)}, bf16[4,64,512]{2,1,0:T(8,128)(2,1)S(1)}, u32[]{:S(2)}, u32[]{:S(2)}) %collective-permute-start.20) | collective-permute-done | bytes 262176 | tf_op jit(solution)/shard_map/ppermute | solution.py:154
  84.1 1.9 %collective-permute-start.6 = (bf16[704,128]{1,0:T(8,128)(2,1)S(1)}, bf16[704,128]{1,0:T(8,128)(2,1)}, u32[]{:S(2)}, u32[]{:S(2)}) collective-permute-start(bf16[704,128]{1,0:T(8,128)(2,1)S(1)} %pad_maximum_fusion.4.refs_0_), channel_id=1, source_target_pairs={{0,3},{1,2},{2,1},{3,0},{4,7},{5,6},{6,5},{7,4},{8,11},{9,10},{10,... | collective-permute-start | bytes 540680 | tf_op jit(solution)/shard_map/ppermute | solution.py:154
  88.3 1.7 %collective-permute-start.7 = (bf16[4,512,128]{2,1,0:T(8,128)(2,1)S(1)}, bf16[4,512,128]{2,1,0:T(8,128)(2,1)}, u32[]{:S(2)}, u32[]{:S(2)}) collective-permute-start(bf16[4,512,128]{2,1,0:T(8,128)(2,1)S(1)} %collective-permute-done.refs_0_), channel_id=1, source_target_pairs={{0,4},{4,0},{8,12},{12,8},{16,20},{20,16},{24,28},{28,24},{1,5},{5... | collective-permute-start | bytes 1572872 | tf_op jit(solution)/shard_map/ppermute | solution.py:154
  90.7 1.4 collective-permute-start.8
  92.1 2.8 %collective-permute-done.5.refs_2_ = bf16[576,128]{1,0:T(8,128)(2,1)S(1)} collective-permute-done((bf16[576,128]{1,0:T(8,128)(2,1)S(1)}, bf16[576,128]{1,0:T(8,128)(2,1)S(1)}, u32[]{:S(2)}, u32[]{:S(2)}) %collective-permute-start.5) | collective-permute-done | bytes 147488 | tf_op jit(solution)/shard_map/ppermute | solution.py:154
  95.5 1.5 %collective-permute-start.21 = (bf16[4,64,512]{2,1,0:T(8,128)(2,1)}, bf16[4,64,512]{2,1,0:T(8,128)(2,1)S(1)}, u32[]{:S(2)}, u32[]{:S(2)}) collective-permute-start(bf16[4,64,512]{2,1,0:T(8,128)(2,1)} %collective-permute-done.19.refs_10_), channel_id=1, source_target_pairs={{0,4},{4,0},{8,12},{12,8},{16,20},{20,16},{24,28},{28,24},{1,5},{5... | collective-permute-start | bytes 786440 | tf_op jit(solution)/shard_map/ppermute | solution.py:154
  101.6 3.2 %chain.1 = (bf16[2,5,64,128]{3,2,1,0:T(8,128)(2,1)}, bf16[128,384]{1,0:T(8,128)(2,1)S(1)}, bf16[2,64,128]{2,1,0:T(8,128)(2,1)S(1)}) custom-call(s32[5]{0:T(128)S(1)} %copy-done.30, bf16[704,128]{1,0:T(8,128)(2,1)S(1)} %pad_maximum_fusion.4.refs_0_, bf16[576,128]{1,0:T(8,128)(2,1)S(1)} %copy-done.24, bf16[576,128]{1,0:T(8,128)(2,1)S(1)} %copy-done.26, ...), custom_call_target="tpu_custom_call" | custom-call | tf_op jit(solution)/shard_map/chain/pallas_call | solution.py:499
  106.1 1.9 %collective-permute-start.23 = (bf16[2,5,64,128]{3,2,1,0:T(8,128)(2,1)}, bf16[2,5,64,128]{3,2,1,0:T(8,128)(2,1)}, u32[]{:S(2)}, u32[]{:S(2)}) collective-permute-start(bf16[2,5,64,128]{3,2,1,0:T(8,128)(2,1)} %get-tuple-element.27.refs_14_), channel_id=1, source_target_pairs={{0,8},{4,12},{8,16},{12,20},{16,24},{20,28},{24,0},{28,4},{1,9},{5... | collective-permute-start | bytes 491528 | tf_op jit(solution)/shard_map/ppermute | solution.py:159
  107.9 1.3 collective-permute-start.24
  109.2 1.4 collective-permute-start.25
  112.9 7.5 %collective-permute-start.27 = (bf16[2,5,64,128]{3,2,1,0:T(8,128)(2,1)}, bf16[2,5,64,128]{3,2,1,0:T(8,128)(2,1)}, u32[]{:S(2)}, u32[]{:S(2)}) collective-permute-start(bf16[2,5,64,128]{3,2,1,0:T(8,128)(2,1)} %collective-permute-done.23.refs_15_), channel_id=1, source_target_pairs={{0,4},{4,0},{8,12},{12,8},{16,20},{20,16},{24,28},{28,24},{1,5},{5... | collective-permute-start | bytes 491528 | tf_op jit(solution)/shard_map/ppermute | solution.py:154
  120.4 1.6 %collective-permute-done.24.refs_16_ = bf16[2,5,64,128]{3,2,1,0:T(8,128)(2,1)} collective-permute-done((bf16[2,5,64,128]{3,2,1,0:T(8,128)(2,1)}, bf16[2,5,64,128]{3,2,1,0:T(8,128)(2,1)}, u32[]{:S(2)}, u32[]{:S(2)}) %collective-permute-start.24) | collective-permute-done | bytes 163872 | tf_op jit(solution)/shard_map/ppermute | solution.py:159
  123.2 1.4 collective-permute-done.25.refs_17_
  125.3 5.3 %input_side.1 = bf16[2,64,4096]{2,1,0:T(8,128)(2,1)} custom-call(s32[5]{0:T(128)} %stack.54.place, bf16[2,64,4096]{2,1,0:T(8,128)(2,1)} %bitcast.54, bf16[128,384]{1,0:T(8,128)(2,1)} %copy-done.27, bf16[2,64,128]{2,1,0:T(8,128)(2,1)} %copy-done.28, bf16[2,2,4096,128]{3,2,1,0:T(8,128)(2,1)} %bitcast.64, bf16[4,512,128]{2,1,0:T(8,128)(2,1)} %copy-done.4, ...), custom_call_target="tpu_custom_call" | custom-call | tf_op jit(solution)/shard_map/input_side/pallas_call | solution.py:519
  138.0 4.4 %weight_side.1 = f32[2,512,128]{2,1,0:T(8,128)} custom-call(s32[5]{0:T(128)S(1)} %copy-done.31, bf16[3,64,1024]{2,1,0:T(8,128)(2,1)S(1)} %get-tuple-element.20.refs_0_, bf16[3,64,1024]{2,1,0:T(8,128)(2,1)S(1)} %copy-done.7, bf16[3,64,1024]{2,1,0:T(8,128)(2,1)} %collective-permute-done.11.refs_2_, bf16[3,64,1024]{2,1,0:T(8,128)(2,1)} %collective-permute-done.12.refs_3_, ...), custom_call_target="tpu_custom_call" | custom-call | tf_op jit(solution)/shard_map/weight_side/pallas_call | solution.py:565
  (143 shorter events, 34.6 us)
Async XLA Ops:
  4.9 52.9 %collective-permute-start = (bf16[4,512,128]{2,1,0:T(8,128)(2,1)}, bf16[4,512,128]{2,1,0:T(8,128)(2,1)S(1)}, u32[]{:S(2)}, u32[]{:S(2)}) collective-permute-start(bf16[4,512,128]{2,1,0:T(8,128)(2,1)} %get-tuple-element.15), channel_id=1, source_target_pairs={{0,1},{1,0},{2,3},{3,2},{4,5},{5,4},{6,7},{7,6},{8,9},{9,8},{10,11... | collective-permute-start | bytes 1572872 | tf_op jit(solution)/shard_map/ppermute | solution.py:154
  6.0 53.1 %collective-permute-start.1 = (bf16[4,512,128]{2,1,0:T(8,128)(2,1)}, bf16[4,512,128]{2,1,0:T(8,128)(2,1)S(1)}, u32[]{:S(2)}, u32[]{:S(2)}) collective-permute-start(bf16[4,512,128]{2,1,0:T(8,128)(2,1)} %get-tuple-element.16), channel_id=1, source_target_pairs={{0,2},{1,3},{2,0},{3,1},{4,6},{5,7},{6,4},{7,5},{8,10},{9,11},{10,... | collective-permute-start | bytes 1572872 | tf_op jit(solution)/shard_map/ppermute | solution.py:154
  7.3 53.1 %collective-permute-start.2 = (bf16[4,512,128]{2,1,0:T(8,128)(2,1)}, bf16[4,512,128]{2,1,0:T(8,128)(2,1)S(1)}, u32[]{:S(2)}, u32[]{:S(2)}) collective-permute-start(bf16[4,512,128]{2,1,0:T(8,128)(2,1)} %get-tuple-element.17), channel_id=1, source_target_pairs={{0,3},{1,2},{2,1},{3,0},{4,7},{5,6},{6,5},{7,4},{8,11},{9,10},{10,... | collective-permute-start | bytes 1572872 | tf_op jit(solution)/shard_map/ppermute | solution.py:154
  11.3 9.5 %collective-permute-start.10 = (bf16[3,64,1024]{2,1,0:T(8,128)(2,1)}, bf16[3,64,1024]{2,1,0:T(8,128)(2,1)S(1)}, u32[]{:S(2)}, u32[]{:S(2)}) collective-permute-start(bf16[3,64,1024]{2,1,0:T(8,128)(2,1)} %get-tuple-element.21), channel_id=1, source_target_pairs={{0,8},{4,12},{8,16},{12,20},{16,24},{20,28},{24,0},{28,4},{1,9},{5... | collective-permute-start | bytes 1179656 | tf_op jit(solution)/shard_map/ppermute | solution.py:159
  12.6 32.7 %collective-permute-start.11 = (bf16[3,64,1024]{2,1,0:T(8,128)(2,1)}, bf16[3,64,1024]{2,1,0:T(8,128)(2,1)}, u32[]{:S(2)}, u32[]{:S(2)}) collective-permute-start(bf16[3,64,1024]{2,1,0:T(8,128)(2,1)} %get-tuple-element.22), channel_id=1, source_target_pairs={{0,16},{4,20},{8,24},{12,28},{16,0},{20,4},{24,8},{28,12},{1,17},{... | collective-permute-start | bytes 1179656 | tf_op jit(solution)/shard_map/ppermute | solution.py:159
  20.8 28.9 %collective-permute-start.12 = (bf16[3,64,1024]{2,1,0:T(8,128)(2,1)}, bf16[3,64,1024]{2,1,0:T(8,128)(2,1)}, u32[]{:S(2)}, u32[]{:S(2)}) collective-permute-start(bf16[3,64,1024]{2,1,0:T(8,128)(2,1)} %copy-done.32), channel_id=1, source_target_pairs={{0,24},{4,28},{8,0},{12,4},{16,8},{20,12},{24,16},{28,20},{1,25},{... | collective-permute-start | bytes 1179656 | tf_op jit(solution)/shard_map/ppermute | solution.py:159
  45.3 21.2 %collective-permute-start.13 = (bf16[3,64,1024]{2,1,0:T(8,128)(2,1)S(1)}, bf16[3,64,1024]{2,1,0:T(8,128)(2,1)}, u32[]{:S(2)}, u32[]{:S(2)}) collective-permute-start(bf16[3,64,1024]{2,1,0:T(8,128)(2,1)S(1)} %get-tuple-element.20.refs_0_), channel_id=1, source_target_pairs={{0,4},{4,0},{8,12},{12,8},{16,20},{20,16},{24,28},{28,24},{1,5},{5... | collective-permute-start | bytes 1179656 | tf_op jit(solution)/shard_map/ppermute | solution.py:154
  52.0 15.5 %collective-permute-start.19 = (bf16[4,64,512]{2,1,0:T(8,128)(2,1)S(1)}, bf16[4,64,512]{2,1,0:T(8,128)(2,1)}, u32[]{:S(2)}, u32[]{:S(2)}) collective-permute-start(bf16[4,64,512]{2,1,0:T(8,128)(2,1)S(1)} %get-tuple-element.25), channel_id=1, source_target_pairs={{0,2},{1,3},{2,0},{3,1},{4,6},{5,7},{6,4},{7,5},{8,10},{9,11},{10,... | collective-permute-start | bytes 786440 | tf_op jit(solution)/shard_map/ppermute | solution.py:154
  57.8 6.7 %collective-permute-start.31 = (bf16[512,128]{1,0:T(8,128)(2,1)S(1)}, bf16[512,128]{1,0:T(8,128)(2,1)S(1)}, u32[]{:S(2)}, u32[]{:S(2)}) collective-permute-start(bf16[512,128]{1,0:T(8,128)(2,1)S(1)} %get-tuple-element.32), channel_id=1, source_target_pairs={{2,0},{6,4},{10,8},{14,12},{18,16},{22,20},{26,24},{30,28}} | collective-permute-start | bytes 393224 | tf_op jit(solution)/shard_map/ppermute | solution.py:497
  59.1 6.7 %collective-permute-start.30 = (bf16[512,128]{1,0:T(8,128)(2,1)S(1)}, bf16[512,128]{1,0:T(8,128)(2,1)S(1)}, u32[]{:S(2)}, u32[]{:S(2)}) collective-permute-start(bf16[512,128]{1,0:T(8,128)(2,1)S(1)} %get-tuple-element.32), channel_id=1, source_target_pairs={{1,0},{5,4},{9,8},{13,12},{17,16},{21,20},{25,24},{29,28}} | collective-permute-start | bytes 393224 | tf_op jit(solution)/shard_map/ppermute | solution.py:497
  62.8 4.8 %collective-permute-start.3 = (f32[3,128,128]{2,1,0:T(8,128)S(1)}, f32[3,128,128]{2,1,0:T(8,128)S(1)}, u32[]{:S(2)}, u32[]{:S(2)}) collective-permute-start(f32[3,128,128]{2,1,0:T(8,128)S(1)} %products.1), channel_id=1, source_target_pairs={{0,4},{4,0},{8,12},{12,8},{16,20},{20,16},{24,28},{28,24},{1,5},{5... | collective-permute-start | bytes 589832 | tf_op jit(solution)/shard_map/ppermute | solution.py:154
  64.5 32.6 %collective-permute-start.17 = (bf16[4,64,1024]{2,1,0:T(8,128)(2,1)}, bf16[4,64,1024]{2,1,0:T(8,128)(2,1)S(1)}, u32[]{:S(2)}, u32[]{:S(2)}) collective-permute-start(bf16[4,64,1024]{2,1,0:T(8,128)(2,1)} %get-tuple-element.24), channel_id=1, source_target_pairs={{0,3},{1,2},{2,1},{3,0},{4,7},{5,6},{6,5},{7,4},{8,11},{9,10},{10,... | collective-permute-start | bytes 1572872 | tf_op jit(solution)/shard_map/ppermute | solution.py:154
  65.8 18.2 %collective-permute-start.20 = (bf16[4,64,512]{2,1,0:T(8,128)(2,1)S(1)}, bf16[4,64,512]{2,1,0:T(8,128)(2,1)S(1)}, u32[]{:S(2)}, u32[]{:S(2)}) collective-permute-start(bf16[4,64,512]{2,1,0:T(8,128)(2,1)S(1)} %get-tuple-element.26), channel_id=1, source_target_pairs={{0,1},{1,0},{2,3},{3,2},{4,5},{5,4},{6,7},{7,6},{8,9},{9,8},{10,11... | collective-permute-start | bytes 786440 | tf_op jit(solution)/shard_map/ppermute | solution.py:154
  66.4 17.6 %collective-permute-start.14 = (bf16[3,64,1024]{2,1,0:T(8,128)(2,1)S(1)}, bf16[3,64,1024]{2,1,0:T(8,128)(2,1)S(1)}, u32[]{:S(2)}, u32[]{:S(2)}) collective-permute-start(bf16[3,64,1024]{2,1,0:T(8,128)(2,1)S(1)} %collective-permute-done.10.refs_1_), channel_id=1, source_target_pairs={{0,4},{4,0},{8,12},{12,8},{16,20},{20,16},{24,28},{28,24},{1,5},{5... | collective-permute-start | bytes 1179656 | tf_op jit(solution)/shard_map/ppermute | solution.py:154
  67.6 18.4 %collective-permute-start.15 = (bf16[3,64,1024]{2,1,0:T(8,128)(2,1)}, bf16[3,64,1024]{2,1,0:T(8,128)(2,1)S(1)}, u32[]{:S(2)}, u32[]{:S(2)}) collective-permute-start(bf16[3,64,1024]{2,1,0:T(8,128)(2,1)} %collective-permute-done.11.refs_2_), channel_id=1, source_target_pairs={{0,4},{4,0},{8,12},{12,8},{16,20},{20,16},{24,28},{28,24},{1,5},{5... | collective-permute-start | bytes 1179656 | tf_op jit(solution)/shard_map/ppermute | solution.py:154
  67.7 19.9 %collective-permute-start.16 = (bf16[3,64,1024]{2,1,0:T(8,128)(2,1)}, bf16[3,64,1024]{2,1,0:T(8,128)(2,1)S(1)}, u32[]{:S(2)}, u32[]{:S(2)}) collective-permute-start(bf16[3,64,1024]{2,1,0:T(8,128)(2,1)} %collective-permute-done.12.refs_3_), channel_id=1, source_target_pairs={{0,4},{4,0},{8,12},{12,8},{16,20},{20,16},{24,28},{28,24},{1,5},{5... | collective-permute-start | bytes 1179656 | tf_op jit(solution)/shard_map/ppermute | solution.py:154
  84.0 6.0 %collective-permute-start.4 = (bf16[576,128]{1,0:T(8,128)(2,1)S(1)}, bf16[576,128]{1,0:T(8,128)(2,1)S(1)}, u32[]{:S(2)}, u32[]{:S(2)}) collective-permute-start(bf16[576,128]{1,0:T(8,128)(2,1)S(1)} %maximum_maximum_fusion.1), channel_id=1, source_target_pairs={{0,1},{1,0},{2,3},{3,2},{4,5},{5,4},{6,7},{7,6},{8,9},{9,8},{10,11... | collective-permute-start | bytes 442376 | tf_op jit(solution)/shard_map/ppermute | solution.py:154
  84.1 13.0 %collective-permute-start.6 = (bf16[704,128]{1,0:T(8,128)(2,1)S(1)}, bf16[704,128]{1,0:T(8,128)(2,1)}, u32[]{:S(2)}, u32[]{:S(2)}) collective-permute-start(bf16[704,128]{1,0:T(8,128)(2,1)S(1)} %pad_maximum_fusion.4.refs_0_), channel_id=1, source_target_pairs={{0,3},{1,2},{2,1},{3,0},{4,7},{5,6},{6,5},{7,4},{8,11},{9,10},{10,... | collective-permute-start | bytes 540680 | tf_op jit(solution)/shard_map/ppermute | solution.py:154
  86.7 8.2 %collective-permute-start.5 = (bf16[576,128]{1,0:T(8,128)(2,1)S(1)}, bf16[576,128]{1,0:T(8,128)(2,1)S(1)}, u32[]{:S(2)}, u32[]{:S(2)}) collective-permute-start(bf16[576,128]{1,0:T(8,128)(2,1)S(1)} %maximum_maximum_fusion.1), channel_id=1, source_target_pairs={{0,2},{1,3},{2,0},{3,1},{4,6},{5,7},{6,4},{7,5},{8,10},{9,11},{10,... | collective-permute-start | bytes 442376 | tf_op jit(solution)/shard_map/ppermute | solution.py:154
  88.3 19.6 %collective-permute-start.7 = (bf16[4,512,128]{2,1,0:T(8,128)(2,1)S(1)}, bf16[4,512,128]{2,1,0:T(8,128)(2,1)}, u32[]{:S(2)}, u32[]{:S(2)}) collective-permute-start(bf16[4,512,128]{2,1,0:T(8,128)(2,1)S(1)} %collective-permute-done.refs_0_), channel_id=1, source_target_pairs={{0,4},{4,0},{8,12},{12,8},{16,20},{20,16},{24,28},{28,24},{1,5},{5... | collective-permute-start | bytes 1572872 | tf_op jit(solution)/shard_map/ppermute | solution.py:154
  90.7 18.6 %collective-permute-start.8 = (bf16[4,512,128]{2,1,0:T(8,128)(2,1)S(1)}, bf16[4,512,128]{2,1,0:T(8,128)(2,1)}, u32[]{:S(2)}, u32[]{:S(2)}) collective-permute-start(bf16[4,512,128]{2,1,0:T(8,128)(2,1)S(1)} %collective-permute-done.1.refs_1_), channel_id=1, source_target_pairs={{0,4},{4,0},{8,12},{12,8},{16,20},{20,16},{24,28},{28,24},{1,5},{5... | collective-permute-start | bytes 1572872 | tf_op jit(solution)/shard_map/ppermute | solution.py:154
  95.5 3.0 %collective-permute-start.21 = (bf16[4,64,512]{2,1,0:T(8,128)(2,1)}, bf16[4,64,512]{2,1,0:T(8,128)(2,1)S(1)}, u32[]{:S(2)}, u32[]{:S(2)}) collective-permute-start(bf16[4,64,512]{2,1,0:T(8,128)(2,1)} %collective-permute-done.19.refs_10_), channel_id=1, source_target_pairs={{0,4},{4,0},{8,12},{12,8},{16,20},{20,16},{24,28},{28,24},{1,5},{5... | collective-permute-start | bytes 786440 | tf_op jit(solution)/shard_map/ppermute | solution.py:154
  97.1 14.6 %collective-permute-start.9 = (bf16[4,512,128]{2,1,0:T(8,128)(2,1)S(1)}, bf16[4,512,128]{2,1,0:T(8,128)(2,1)S(1)}, u32[]{:S(2)}, u32[]{:S(2)}) collective-permute-start(bf16[4,512,128]{2,1,0:T(8,128)(2,1)S(1)} %collective-permute-done.2.refs_2_), channel_id=1, source_target_pairs={{0,4},{4,0},{8,12},{12,8},{16,20},{20,16},{24,28},{28,24},{1,5},{5... | collective-permute-start | bytes 1572872 | tf_op jit(solution)/shard_map/ppermute | solution.py:154
  97.1 9.0 %collective-permute-start.22 = (bf16[4,64,512]{2,1,0:T(8,128)(2,1)}, bf16[4,64,512]{2,1,0:T(8,128)(2,1)S(1)}, u32[]{:S(2)}, u32[]{:S(2)}) collective-permute-start(bf16[4,64,512]{2,1,0:T(8,128)(2,1)} %copy-done.13), channel_id=1, source_target_pairs={{0,4},{4,0},{8,12},{12,8},{16,20},{20,16},{24,28},{28,24},{1,5},{5... | collective-permute-start | bytes 786440 | tf_op jit(solution)/shard_map/ppermute | solution.py:154
  98.5 32.8 %collective-permute-start.18 = (bf16[4,64,1024]{2,1,0:T(8,128)(2,1)S(1)}, bf16[4,64,1024]{2,1,0:T(8,128)(2,1)}, u32[]{:S(2)}, u32[]{:S(2)}) collective-permute-start(bf16[4,64,1024]{2,1,0:T(8,128)(2,1)S(1)} %collective-permute-done.17.refs_8_), channel_id=1, source_target_pairs={{0,4},{4,0},{8,12},{12,8},{16,20},{20,16},{24,28},{28,24},{1,5},{5... | collective-permute-start | bytes 1572872 | tf_op jit(solution)/shard_map/ppermute | solution.py:154
  106.1 6.9 %collective-permute-start.23 = (bf16[2,5,64,128]{3,2,1,0:T(8,128)(2,1)}, bf16[2,5,64,128]{3,2,1,0:T(8,128)(2,1)}, u32[]{:S(2)}, u32[]{:S(2)}) collective-permute-start(bf16[2,5,64,128]{3,2,1,0:T(8,128)(2,1)} %get-tuple-element.27.refs_14_), channel_id=1, source_target_pairs={{0,8},{4,12},{8,16},{12,20},{16,24},{20,28},{24,0},{28,4},{1,9},{5... | collective-permute-start | bytes 491528 | tf_op jit(solution)/shard_map/ppermute | solution.py:159
  107.9 14.1 %collective-permute-start.24 = (bf16[2,5,64,128]{3,2,1,0:T(8,128)(2,1)}, bf16[2,5,64,128]{3,2,1,0:T(8,128)(2,1)}, u32[]{:S(2)}, u32[]{:S(2)}) collective-permute-start(bf16[2,5,64,128]{3,2,1,0:T(8,128)(2,1)} %get-tuple-element.27.refs_14_), channel_id=1, source_target_pairs={{0,16},{4,20},{8,24},{12,28},{16,0},{20,4},{24,8},{28,12},{1,17},{... | collective-permute-start | bytes 491528 | tf_op jit(solution)/shard_map/ppermute | solution.py:159
  109.2 15.3 %collective-permute-start.25 = (bf16[2,5,64,128]{3,2,1,0:T(8,128)(2,1)}, bf16[2,5,64,128]{3,2,1,0:T(8,128)(2,1)S(1)}, u32[]{:S(2)}, u32[]{:S(2)}) collective-permute-start(bf16[2,5,64,128]{3,2,1,0:T(8,128)(2,1)} %get-tuple-element.27.refs_14_), channel_id=1, source_target_pairs={{0,24},{4,28},{8,0},{12,4},{16,8},{20,12},{24,16},{28,20},{1,25},{... | collective-permute-start | bytes 491528 | tf_op jit(solution)/shard_map/ppermute | solution.py:159
  111.7 18.9 %collective-permute-start.26 = (bf16[2,5,64,128]{3,2,1,0:T(8,128)(2,1)}, bf16[2,5,64,128]{3,2,1,0:T(8,128)(2,1)S(1)}, u32[]{:S(2)}, u32[]{:S(2)}) collective-permute-start(bf16[2,5,64,128]{3,2,1,0:T(8,128)(2,1)} %get-tuple-element.27.refs_14_), channel_id=1, source_target_pairs={{0,4},{4,0},{8,12},{12,8},{16,20},{20,16},{24,28},{28,24},{1,5},{5... | collective-permute-start | bytes 491528 | tf_op jit(solution)/shard_map/ppermute | solution.py:154
  112.9 18.4 %collective-permute-start.27 = (bf16[2,5,64,128]{3,2,1,0:T(8,128)(2,1)}, bf16[2,5,64,128]{3,2,1,0:T(8,128)(2,1)}, u32[]{:S(2)}, u32[]{:S(2)}) collective-permute-start(bf16[2,5,64,128]{3,2,1,0:T(8,128)(2,1)} %collective-permute-done.23.refs_15_), channel_id=1, source_target_pairs={{0,4},{4,0},{8,12},{12,8},{16,20},{20,16},{24,28},{28,24},{1,5},{5... | collective-permute-start | bytes 491528 | tf_op jit(solution)/shard_map/ppermute | solution.py:154
  122.0 9.3 %collective-permute-start.28 = (bf16[2,5,64,128]{3,2,1,0:T(8,128)(2,1)}, bf16[2,5,64,128]{3,2,1,0:T(8,128)(2,1)}, u32[]{:S(2)}, u32[]{:S(2)}) collective-permute-start(bf16[2,5,64,128]{3,2,1,0:T(8,128)(2,1)} %collective-permute-done.24.refs_16_), channel_id=1, source_target_pairs={{0,4},{4,0},{8,12},{12,8},{16,20},{20,16},{24,28},{28,24},{1,5},{5... | collective-permute-start | bytes 491528 | tf_op jit(solution)/shard_map/ppermute | solution.py:154
  124.6 6.7 %collective-permute-start.29 = (bf16[2,5,64,128]{3,2,1,0:T(8,128)(2,1)S(1)}, bf16[2,5,64,128]{3,2,1,0:T(8,128)(2,1)}, u32[]{:S(2)}, u32[]{:S(2)}) collective-permute-start(bf16[2,5,64,128]{3,2,1,0:T(8,128)(2,1)S(1)} %collective-permute-done.25.refs_17_), channel_id=1, source_target_pairs={{0,4},{4,0},{8,12},{12,8},{16,20},{20,16},{24,28},{28,24},{1,5},{5... | collective-permute-start | bytes 491528 | tf_op jit(solution)/shard_map/ppermute | solution.py:154
  (40 other events, 374.0 us)
where the time goes:
time: 143 us; the launch traced here: 142 us
  waiting for transfers between devices  47.5 us (33%)
  starting transfers between devices  38.8 us (27%)
  Pallas kernels  24.8 us (17%)
  local copies, waits for them, and re-layouts  19.1 us (13%)
  matrix products  6.83 us (5%)
  other arithmetic  4.21 us (3%)
    ppermute x24, starting transfers between devices, swapped(): lax.ppermute(block, axis, [(i, i ^ mask) for i in range(lax.axis_size(axi...  27 us
    ppermute x6, waiting for transfers between devices, shifted(): lax.ppermute(block, 'dp', [(i, (i + 2 * distance) % count) for i in range...  26.3 us
    ppermute x24, waiting for transfers between devices, swapped(): lax.ppermute(block, axis, [(i, i ^ mask) for i in range(lax.axis_size(axi...  18.6 us
    unnamed x80, local copies, waits for them, and re-layouts  16.7 us
    ppermute x6, starting transfers between devices, shifted(): lax.ppermute(block, 'dp', [(i, (i + 2 * distance) % count) for i in range...  9.24 us
    pallas_call x1, Pallas kernels, gathered(): pl.pallas_call(functools.partial(input_kernel, sections, tokens), grid=(s...  5.35 us
    pallas_call x1, Pallas kernels, gathered(): pl.pallas_call(functools.partial(weight_kernel, sections, steps, tokens),...  4.4 us
    pallas_call x1, Pallas kernels, gathered(): pl.pallas_call(functools.partial(pick_weights, sections), in_specs=[scala...  3.55 us
  transfers between devices with their start and end apart: 32, of which 8 were waited for; matrix products, arithmetic and copies ran while one was open for 9% of the time, Pallas kernels for 12%

commit v1 on v0

--- a/solution.py
+++ b/solution.py
@@ -165,25 +165,53 @@
     )
 
 
-def block_attention(queries, key_vectors, valid_lengths):
-    ways, seqs, length, head = queries.shape
-    tokens = seqs * length
-    scores = jnp.einsum(
-        "nth,nsh->nts",
-        queries.reshape(ways, tokens, head),
-        key_vectors.reshape(ways, tokens, head),
-        preferred_element_type=jnp.float32,
-    ) / math.sqrt(head)
-    row = lax.broadcasted_iota(jnp.int32, (tokens, tokens), 0)
-    col = lax.broadcasted_iota(jnp.int32, (tokens, tokens), 1)
-    bound = jnp.repeat(valid_lengths, length, axis=1)[:, None, :]
-    allowed = ((row // length == col // length) & (col <= row))[None] & (
-        (col % length)[None] < bound
-    )
-    scores = jnp.where(allowed, scores, -jnp.inf)
-    row_max = jnp.max(scores, axis=-1, keepdims=True)
-    raised = jnp.where(allowed, jnp.exp(scores - row_max), 0.0)
-    return (raised / jnp.sum(raised, axis=-1, keepdims=True)).astype(jnp.bfloat16)
+def heads_kernel(length, valid, inputs, cot, held, queries, key_vectors, out, sums):
+    tokens, head = queries.shape[1:]
+    for way in range(2):
+        for which, source in enumerate((inputs, cot)):
+            term = contract(source[way], held[way, which], 1, 0)
+            first = pl.program_id(0) == 0
+
+            @pl.when(first)
+            def _():
+                sums[which, way] = term
+
+            @pl.when(jnp.logical_not(first))
+            def _():
+                sums[which, way] += term
+
+    @pl.when(pl.program_id(0) == pl.num_programs(0) - 1)
+    def _():
+        row = lax.broadcasted_iota(jnp.int32, (tokens, tokens), 0)
+        col = lax.broadcasted_iota(jnp.int32, (tokens, tokens), 1)
+        out[2 * tokens : 3 * tokens, :] = jnp.zeros((tokens, head), jnp.bfloat16)
+        for way in range(2):
+            scores = contract(queries[way], key_vectors[way], 1, 1) / math.sqrt(head)
+            allowed = None
+            for seq in range(tokens // length):
+                start = seq * length
+                here = (row >= start) & (row < start + length) & (col >= start) & (col <= row)
+                here &= col - start < valid[way, seq]
+                allowed = here if allowed is None else allowed | here
+            scores = jnp.where(allowed, scores, -jnp.inf)
+            row_max = jnp.max(scores, axis=-1, keepdims=True)
+            raised = jnp.where(allowed, jnp.exp(scores - row_max), 0.0)
+            attend = (raised / jnp.sum(raised, axis=-1, keepdims=True)).astype(jnp.bfloat16)
+            mixture = contract(attend, sums[0, way].astype(jnp.bfloat16), 1, 0)
+            out[way * tokens : (way + 1) * tokens, :] = sums[1, way].astype(jnp.bfloat16)
+            out[2 * tokens : 3 * tokens, way * tokens : (way + 1) * tokens] = attend
+            rows = slice((3 + way) * tokens, (4 + way) * tokens)
+            out[rows, :] = mixture.astype(jnp.bfloat16)
+
+
+def pack_kernel(near, far, tail, short, full):
+    head = near.shape[-1]
+    rows = near.shape[0] * head
+    total = (near[...] + far[...]).astype(jnp.bfloat16).reshape(rows, head)
+    short[:rows, :] = total
+    full[:rows, :] = total
+    short[rows:, :] = tail[: short.shape[0] - rows, :]
+    full[rows:, :] = tail[...]
 
 
 def chain_kernel(sections, tokens, head, place, *refs):
@@ -246,7 +274,7 @@
         weights = jnp.concatenate([block[0] for block in fetched], axis=1)
         total = contract(steer[...], weights, 1, 1)
         for way in range(2):
-            branch = contract(own[way], held[way, 0, pl.ds(start, width), :], 1, 1)
+            branch = contract(own[way], held[way, pl.ds(start, width), :], 1, 1)
             branch += total[way * tokens : (way + 1) * tokens]
             base = cot[way, :, pl.ds(start, width)].astype(jnp.float32)
             out[way, :, pl.ds(start, width)] = (base + branch).astype(jnp.bfloat16)
@@ -274,8 +302,14 @@
         copy.wait()
 
 
-def pick_outputs(place, halved, out, sem):
-    carried_out([pltpu.make_async_copy(halved.at[:, 1, :, place[1]], out, sem)])
+def pick_outputs(place, halved, whole, out, own, part, sems):
+    carried_out(
+        [
+            pltpu.make_async_copy(halved.at[1, 0, place[2], place[1]], part, sems.at[2]),
+            pltpu.make_async_copy(halved.at[:, 1, :, place[1]], out, sems.at[0]),
+            pltpu.make_async_copy(whole.at[:, 0], own, sems.at[1]),
+        ]
+    )
 
 
 def pick_columns(steps, width, place, inputs, cot, *refs):
@@ -333,7 +367,9 @@
     columns = refs[: 2 * steps]
     mirrored, lent = refs[2 * steps : 2 * steps + 2], refs[2 * steps + 2 : 2 * steps + 6]
     sent = refs[2 * steps + 6 : 4 * steps + 6]
-    held, out, lefts, rights, steers = refs[4 * steps + 6 :]
+    refs = refs[4 * steps + 6 :]
+    own_slice, fetched, lent_slices = refs[0], refs[:sections], refs[sections - 1 :]
+    out, lefts, rights, steers = refs[2 * sections - 1 :]
     width, head = out.shape[1:]
     every = 2 * steps * tokens
     lanes = pl.ds(pl.multiple_of(place[1] * width, 128), width)
@@ -362,10 +398,28 @@
             def _():
                 rights[both, :] = lent[2 * (index // steps) + way][index % steps]
 
-    for way in range(2):
+    def corrected(here, way):
         rows = slice(way * every, (way + 1) * every)
-        total = contract(steers[way], held[way], 1, 1)
-        rights[rows, :] = (rights[rows, :].astype(jnp.float32) + total).astype(jnp.bfloat16)
+        total = rights[rows, :].astype(jnp.float32)
+        for far in range(1, sections - here):
+            holder = here + far if way == 0 else sections - 1 - here - far
+            if holder == here:
+                held = own_slice[...]
+            elif way == 1 and holder > here:
+                held = lent_slices[holder ^ here][...]
+            else:
+                held = fetched[holder ^ here][place[2]]
+            steer = steers[way, :, (far - 1) * head : far * head]
+            total += contract(steer, held, 1, 1)
+        rights[rows, :] = total.astype(jnp.bfloat16)
+
+    for here in range(sections - 1):
+
+        @pl.when(place[0] == here)
+        def _():
+            for way in range(2):
+                corrected(here, way)
+
     out[1] = contract(lefts[1], rights[...], 0, 0).T
 
 
@@ -399,7 +453,7 @@
         out_shape=[jax.ShapeDtypeStruct((steps, width, head), jnp.bfloat16)] * (sections - 1),
         scratch_shapes=[pltpu.SemaphoreType.DMA((sections - 1,))],
         name="pick_weights",
-        compiler_params=pltpu.CompilerParams(vmem_limit_bytes=61 << 20),
+        compiler_params=pltpu.CompilerParams(vmem_limit_bytes=52 << 20),
     )(place, halved)
     fetched = [None] * sections
     for mask in range(sections - 1, 0, -1):
@@ -412,32 +466,53 @@
         out_shape=[jax.ShapeDtypeStruct((3, tokens, 2 * width), jnp.bfloat16)] * steps,
         scratch_shapes=[pltpu.SemaphoreType.DMA((3 * steps,))],
         name="pick_columns",
-        compiler_params=pltpu.CompilerParams(vmem_limit_bytes=8 << 20),
+        compiler_params=pltpu.CompilerParams(vmem_limit_bytes=52 << 20),
     )(place, inputs, cot)
     near_columns = [picked[0]]
     for distance in range(1, steps):
         near_columns.append(shifted(picked[distance], distance))
 
-    attend = block_attention(saved_queries[0], saved_keys[0], valid_lengths)
-    values = jnp.einsum(
-        "ntd,ndh->nth", inputs, held[:, 0], preferred_element_type=jnp.float32
-    ).astype(jnp.bfloat16)
-    mixtures = jnp.einsum(
-        "nts,nsh->nth", attend, values, preferred_element_type=jnp.float32
-    ).astype(jnp.bfloat16)
-    first_grad = jnp.einsum(
-        "ntd,ndh->nth", cot, held[:, 1], preferred_element_type=jnp.float32
-    ).astype(jnp.bfloat16)
-
-    outputs = pl.pallas_call(
+    lengths = valid_lengths
+    blocks = 4
+    cut = model_width // blocks
+    tail = pl.pallas_call(
+        functools.partial(heads_kernel, length),
+        grid=(blocks,),
+        in_specs=[
+            scalars,
+            pl.BlockSpec((2, tokens, cut), lambda i: (0, 0, i)),
+            pl.BlockSpec((2, tokens, cut), lambda i: (0, 0, i)),
+            pl.BlockSpec((2, 2, cut, head), lambda i: (0, 0, i, 0)),
+            pl.BlockSpec((2, tokens, head), lambda i: (0, 0, 0)),
+            pl.BlockSpec((2, tokens, head), lambda i: (0, 0, 0)),
+        ],
+        out_specs=pl.BlockSpec((5 * tokens, head), lambda i: (0, 0)),
+        out_shape=jax.ShapeDtypeStruct((5 * tokens, head), jnp.bfloat16),
+        scratch_shapes=[pltpu.VMEM((2, 2, tokens, head), jnp.float32)],
+        name="heads",
+        compiler_params=pltpu.CompilerParams(vmem_limit_bytes=12 << 20),
+    )(
+        lengths,
+        inputs,
+        cot,
+        held,
+        saved_queries[0].reshape(2, tokens, head),
+        saved_keys[0].reshape(2, tokens, head),
+    )
+
+    outputs, own_values, own_slice = pl.pallas_call(
         pick_outputs,
-        in_specs=[scalars, hbm],
-        out_specs=memory,
-        out_shape=jax.ShapeDtypeStruct((2, steps, width, head), jnp.bfloat16),
-        scratch_shapes=[pltpu.SemaphoreType.DMA],
+        in_specs=[scalars, hbm, hbm],
+        out_specs=[memory] * 3,
+        out_shape=[
+            jax.ShapeDtypeStruct((2, steps, width, head), jnp.bfloat16),
+            jax.ShapeDtypeStruct((2, model_width, head), jnp.bfloat16),
+            jax.ShapeDtypeStruct((width, head), jnp.bfloat16),
+        ],
+        scratch_shapes=[pltpu.SemaphoreType.DMA((3,))],
         name="pick_outputs",
-        compiler_params=pltpu.CompilerParams(vmem_limit_bytes=58 << 20),
-    )(place, halved)
+        compiler_params=pltpu.CompilerParams(vmem_limit_bytes=8 << 20),
+    )(place, halved, held)
     products = pl.pallas_call(
         functools.partial(product_kernel, sections, steps),
         in_specs=[scalars] + [memory] * sections,
@@ -446,25 +521,26 @@
         name="products",
         compiler_params=pltpu.CompilerParams(vmem_limit_bytes=8 << 20),
     )(place, outputs, *fetched[1:])
-    products = (products + swapped(products, "dp", 1)).astype(jnp.bfloat16)
+    far_products = swapped(products, "dp", 1)
     lent_back = [None] * sections
     for mask in range(1, sections):
         lent_back[mask] = swapped(fetched[mask], "dp", 1)
 
-    part = jnp.concatenate(
-        [
-            products.reshape(-1, head),
-            first_grad.reshape(-1, head),
-            jnp.pad(
-                jnp.concatenate([attend[0], attend[1]], axis=1), ((0, 0), (0, head - 2 * tokens))
-            ),
-            mixtures.reshape(-1, head),
-        ]
-    )
-    rows = part.shape[0] - 2 * tokens
-    parts = [part]
+    rows = (sections - 1) * head + 3 * tokens
+    short, full = pl.pallas_call(
+        pack_kernel,
+        in_specs=[memory] * 3,
+        out_specs=[memory] * 2,
+        out_shape=[
+            jax.ShapeDtypeStruct((rows, head), jnp.bfloat16),
+            jax.ShapeDtypeStruct((rows + 2 * tokens, head), jnp.bfloat16),
+        ],
+        name="pack",
+        compiler_params=pltpu.CompilerParams(vmem_limit_bytes=8 << 20),
+    )(products, far_products, tail)
+    parts = [full]
     for mask in range(1, sections):
-        parts.append(swapped(part if mask == sections - 1 else part[:rows], "section", mask))
+        parts.append(swapped(full if mask == sections - 1 else short, "section", mask))
 
     upward, *sideways = pl.pallas_call(
         functools.partial(pick_moving, steps),
@@ -486,15 +562,12 @@
     far_columns = []
     for distance in range(steps):
         far_columns.append(swapped(near_columns[distance], "dp", 1))
-    own_slice = lax.dynamic_slice(
-        halved, (1, 0, depth, core, 0, 0), (1, 1, 1, 1, width, head)
-    ).reshape(width, head)
     lent = [own_slice]
     for mask in range(1, sections):
         route = [
             (i, i ^ mask) for i in range(sections) if i ^ mask < i < sections - 1 - (i ^ mask)
         ]
-        lent.append(lax.ppermute(own_slice, "section", route) if route else None)
+        lent.append(lax.ppermute(own_slice, "section", route) if route else own_slice)
 
     sent, steer, own = pl.pallas_call(
         functools.partial(chain_kernel, sections, tokens, head),
@@ -524,47 +597,19 @@
             pl.BlockSpec((2, tokens, 2 * width), lambda i: (0, 0, i)),
             pl.BlockSpec((2 * tokens, (sections - 1) * head), lambda i: (0, 0)),
             pl.BlockSpec((2, tokens, head), lambda i: (0, 0, 0)),
-            pl.BlockSpec((2, 1, 2 * width, head), lambda i: (0, 0, i, 0)),
+            pl.BlockSpec((2, 2 * width, head), lambda i: (0, i, 0)),
         ]
         + [pl.BlockSpec((1, width, head), lambda i: (i, 0, 0))] * (2 * sections - 2),
         out_specs=pl.BlockSpec((2, tokens, 2 * width), lambda i: (0, 0, i)),
         out_shape=jax.ShapeDtypeStruct((2, tokens, model_width), jnp.bfloat16),
         name="input_side",
-        compiler_params=pltpu.CompilerParams(vmem_limit_bytes=61 << 20),
-    )(place, cot, steer, own, held, *fetched[1:], *lent_back[1:])
-
-    sliced = [own_slice] + [
-        lax.dynamic_index_in_dim(block, depth, 0, keepdims=False) for block in fetched[1:]
-    ]
-    down = jnp.stack(sliced)
-    up = jnp.stack(
-        [own_slice]
-        + [
-            sliced[mask]
-            if lent[mask] is None
-            else jnp.where((here ^ mask) < here, sliced[mask], lent[mask])
-            for mask in range(1, sections)
-        ]
-    )
-    nearby = []
-    for distance in range(1, sections):
-        inside = here + distance < sections
-        below = jnp.where(inside, here ^ (here + distance), 0)
-        above = jnp.where(inside, here ^ (sections - 1 - here - distance), 0)
-        nearby.append(
-            jnp.stack(
-                [
-                    lax.dynamic_index_in_dim(down, below, 0, keepdims=False),
-                    lax.dynamic_index_in_dim(up, above, 0, keepdims=False),
-                ]
-            )
-        )
-    nearby = jnp.concatenate(nearby, axis=2)
+        compiler_params=pltpu.CompilerParams(vmem_limit_bytes=12 << 20),
+    )(place, cot, steer, own, own_values, *fetched[1:], *lent_back[1:])
 
     every = replicas * tokens
     weight_grads = pl.pallas_call(
         functools.partial(weight_kernel, sections, steps, tokens),
-        in_specs=[scalars] + [memory] * (4 * steps + 7),
+        in_specs=[scalars] + [memory] * (4 * steps + 2 * sections + 5),
         out_specs=memory,
         out_shape=jax.ShapeDtypeStruct((2, width, head), jnp.float32),
         scratch_shapes=[
@@ -584,7 +629,9 @@
         *far_aside,
         *near_sent,
         *far_sent,
-        nearby,
+        own_slice,
+        *fetched[1:],
+        *lent[1:],
     )
     shape = (1, 2, seqs, length, model_width)
     return (grads_in.reshape(shape), weight_grads[None])

time: 143 us -> 107 us (0.75)
  local copies, waits for them, and re-layouts: 19.1 us -> 0.11 us
  matrix products: 6.83 us -> 0 us
  starting transfers between devices: 38.8 us -> 33.1 us
  other arithmetic: 4.21 us -> 0 us
  waiting for transfers between devices: 47.5 us -> 51 us
  Pallas kernels: 24.8 us -> 21.4 us
    unnamed x80 -> x12, local copies, waits for them, and re-layouts: 16.7 us -> 0.03 us
    ppermute x6, waiting for transfers between devices: 26.3 us -> 35.8 us  [shifted(): lax.ppermute(block, 'dp', [(i, (i + 2 * distance) % count) for i in range...]
    dot_general x2 -> x0, matrix products: 5.22 us -> none  [the longest x1 3.14 us: gathered(): jnp.einsum('nts,nsh->nth', attend, values, preferred_element_type=jnp.flo...]
    ppermute x24, waiting for transfers between devices: 18.6 us -> 13.7 us  [swapped(): lax.ppermute(block, axis, [(i, i ^ mask) for i in range(lax.axis_size(axi...]
    ppermute x24, starting transfers between devices: 27 us -> 23.3 us  [swapped(): lax.ppermute(block, axis, [(i, i ^ mask) for i in range(lax.axis_size(axi...]
    another operation x3 -> x0, other arithmetic: 2.87 us -> none  [the longest x2 1.85 us: gathered(): jnp.stack([own_slice] + [sliced[mask] if lent[mask] is None else jnp.wher...]
    pallas_call x1 -> x3, Pallas kernels: 3 us -> 5.58 us  [the longest x1 4.58 us: gathered(): pl.pallas_call(functools.partial(heads_kernel, length), grid=(blocks,), i...]
    ppermute x6, starting transfers between devices: 9.24 us -> 7.18 us  [shifted(): lax.ppermute(block, 'dp', [(i, (i + 2 * distance) % count) for i in range...]
  transfers between devices with their start and end apart: 32 -> 32, of which waited for: 8 -> 10; matrix products, arithmetic and copies ran while one was open for 9% -> 0% of each run, Pallas kernels for 12% -> 15%
where the time goes in v1:
time: 107 us; the launch traced here: 106 us
  waiting for transfers between devices  51 us (48%)
  starting transfers between devices  33.1 us (31%)
  Pallas kernels  21.4 us (20%)
    ppermute x6, waiting for transfers between devices, shifted(): lax.ppermute(block, 'dp', [(i, (i + 2 * distance) % count) for i in range...  35.8 us
    ppermute x24, starting transfers between devices, swapped(): lax.ppermute(block, axis, [(i, i ^ mask) for i in range(lax.axis_size(axi...  23.3 us
    ppermute x24, waiting for transfers between devices, swapped(): lax.ppermute(block, axis, [(i, i ^ mask) for i in range(lax.axis_size(axi...  13.7 us
    ppermute x6, starting transfers between devices, shifted(): lax.ppermute(block, 'dp', [(i, (i + 2 * distance) % count) for i in range...  7.18 us
    pallas_call x1, Pallas kernels, gathered(): pl.pallas_call(functools.partial(heads_kernel, length), grid=(blocks,), i...  4.58 us
    pallas_call x1, Pallas kernels, gathered(): pl.pallas_call(functools.partial(weight_kernel, sections, steps, tokens),...  3.72 us
    pallas_call x1, Pallas kernels, gathered(): pl.pallas_call(functools.partial(input_kernel, sections, tokens), grid=(s...  3.68 us
    ppermute x2, starting transfers between devices, gathered(): lax.ppermute(own_slice, 'section', route)  2.58 us
  transfers between devices with their start and end apart: 32, of which 10 were waited for; matrix products, arithmetic and copies ran while one was open for 0% of the time, Pallas kernels for 15%

profile of v1, /device:TPU:9, one launch (start us, length us, event | category | flops | bytes accessed | tf_op | source)
XLA Modules:
  0.0 106.5 jit_solution(14956904978123622366)
XLA Ops:
  0.7 2.3 %pick_columns.1 = (bf16[3,64,1024]{2,1,0:T(8,128)(2,1)S(1)}, bf16[3,64,1024]{2,1,0:T(8,128)(2,1)S(1)}, bf16[3,64,1024]{2,1,0:T(8,128)(2,1)S(1)}, bf16[3,64,1024]{2,1,0:T(8,128)(2,1)S(1)}) custom-call(s32[5]{0:T(128)S(1)} %stack.23.place, bf16[2,64,4096]{2,1,0:T(8,128)(2,1)} %bitcast.20, bf16[2,64,4096]{2,1,0:T(8,128)(2,1)} %bitcast.17), custom_call_target="tpu_custom_call" | custom-call | tf_op jit(solution)/shard_map/pick_columns/pallas_call | solution.py:462
  3.0 1.3 %collective-permute-start.10 = (bf16[3,64,1024]{2,1,0:T(8,128)(2,1)S(1)}, bf16[3,64,1024]{2,1,0:T(8,128)(2,1)S(1)}, u32[]{:S(2)}, u32[]{:S(2)}) collective-permute-start(bf16[3,64,1024]{2,1,0:T(8,128)(2,1)S(1)} %get-tuple-element.30), channel_id=1, source_target_pairs={{0,8},{4,12},{8,16},{12,20},{16,24},{20,28},{24,0},{28,4},{1,9},{5... | collective-permute-start | bytes 1179656 | tf_op jit(solution)/shard_map/ppermute | solution.py:159
  5.5 2.0 %pick_weights.1 = (bf16[4,512,128]{2,1,0:T(8,128)(2,1)S(1)}, bf16[4,512,128]{2,1,0:T(8,128)(2,1)S(1)}, bf16[4,512,128]{2,1,0:T(8,128)(2,1)S(1)}) custom-call(s32[5]{0:T(128)S(1)} %stack.23.place, bf16[2,2,4,2,512,128]{5,4,3,2,1,0:T(8,128)(2,1)} %bitcast.13), custom_call_target="tpu_custom_call" | custom-call | tf_op jit(solution)/shard_map/pick_weights/pallas_call | solution.py:449
  8.7 1.5 %collective-permute-start.1 = (bf16[4,512,128]{2,1,0:T(8,128)(2,1)S(1)}, bf16[4,512,128]{2,1,0:T(8,128)(2,1)S(1)}, u32[]{:S(2)}, u32[]{:S(2)}) collective-permute-start(bf16[4,512,128]{2,1,0:T(8,128)(2,1)S(1)} %get-tuple-element.22), channel_id=1, source_target_pairs={{0,2},{1,3},{2,0},{3,1},{4,6},{5,7},{6,4},{7,5},{8,10},{9,11},{10,... | collective-permute-start | bytes 1572872 | tf_op jit(solution)/shard_map/ppermute | solution.py:154
  10.1 1.4 %collective-permute-start.12 = (bf16[3,64,1024]{2,1,0:T(8,128)(2,1)S(1)}, bf16[3,64,1024]{2,1,0:T(8,128)(2,1)S(1)}, u32[]{:S(2)}, u32[]{:S(2)}) collective-permute-start(bf16[3,64,1024]{2,1,0:T(8,128)(2,1)S(1)} %get-tuple-element.32), channel_id=1, source_target_pairs={{0,24},{4,28},{8,0},{12,4},{16,8},{20,12},{24,16},{28,20},{1,25},{... | collective-permute-start | bytes 1179656 | tf_op jit(solution)/shard_map/ppermute | solution.py:159
  11.5 1.6 %collective-permute-done.10.refs_1_ = bf16[3,64,1024]{2,1,0:T(8,128)(2,1)S(1)} collective-permute-done((bf16[3,64,1024]{2,1,0:T(8,128)(2,1)S(1)}, bf16[3,64,1024]{2,1,0:T(8,128)(2,1)S(1)}, u32[]{:S(2)}, u32[]{:S(2)}) %collective-permute-start.10) | collective-permute-done | bytes 393248 | tf_op jit(solution)/shard_map/ppermute | solution.py:159
  13.1 2.2 %collective-permute-start.2 = (bf16[4,512,128]{2,1,0:T(8,128)(2,1)S(1)}, bf16[4,512,128]{2,1,0:T(8,128)(2,1)S(1)}, u32[]{:S(2)}, u32[]{:S(2)}) collective-permute-start(bf16[4,512,128]{2,1,0:T(8,128)(2,1)S(1)} %get-tuple-element.23), channel_id=1, source_target_pairs={{0,3},{1,2},{2,1},{3,0},{4,7},{5,6},{6,5},{7,4},{8,11},{9,10},{10,... | collective-permute-start | bytes 1572872 | tf_op jit(solution)/shard_map/ppermute | solution.py:154
  15.2 22.2 %collective-permute-done.11.refs_2_ = bf16[3,64,1024]{2,1,0:T(8,128)(2,1)S(1)} collective-permute-done((bf16[3,64,1024]{2,1,0:T(8,128)(2,1)S(1)}, bf16[3,64,1024]{2,1,0:T(8,128)(2,1)S(1)}, u32[]{:S(2)}, u32[]{:S(2)}) %collective-permute-start.11) | collective-permute-done | bytes 393248 | tf_op jit(solution)/shard_map/ppermute | solution.py:159
  37.4 1.5 %collective-permute-start.13 = (bf16[3,64,1024]{2,1,0:T(8,128)(2,1)S(1)}, bf16[3,64,1024]{2,1,0:T(8,128)(2,1)S(1)}, u32[]{:S(2)}, u32[]{:S(2)}) collective-permute-start(bf16[3,64,1024]{2,1,0:T(8,128)(2,1)S(1)} %get-tuple-element.29.refs_0_), channel_id=1, source_target_pairs={{0,4},{4,0},{8,12},{12,8},{16,20},{20,16},{24,28},{28,24},{1,5},{5... | collective-permute-start | bytes 1179656 | tf_op jit(solution)/shard_map/ppermute | solution.py:154
  39.0 1.3 %collective-permute-done.12.refs_3_ = bf16[3,64,1024]{2,1,0:T(8,128)(2,1)S(1)} collective-permute-done((bf16[3,64,1024]{2,1,0:T(8,128)(2,1)S(1)}, bf16[3,64,1024]{2,1,0:T(8,128)(2,1)S(1)}, u32[]{:S(2)}, u32[]{:S(2)}) %collective-permute-start.12) | collective-permute-done | bytes 393248 | tf_op jit(solution)/shard_map/ppermute | solution.py:159
  41.1 1.3 %collective-permute-start.19 = (bf16[4,64,512]{2,1,0:T(8,128)(2,1)S(1)}, bf16[4,64,512]{2,1,0:T(8,128)(2,1)S(1)}, u32[]{:S(2)}, u32[]{:S(2)}) collective-permute-start(bf16[4,64,512]{2,1,0:T(8,128)(2,1)S(1)} %get-tuple-element.34), channel_id=1, source_target_pairs={{0,2},{1,3},{2,0},{3,1},{4,6},{5,7},{6,4},{7,5},{8,10},{9,11},{10,... | collective-permute-start | bytes 786440 | tf_op jit(solution)/shard_map/ppermute | solution.py:154
  43.5 1.3 %collective-permute-start.30 = (bf16[512,128]{1,0:T(8,128)(2,1)S(1)}, bf16[512,128]{1,0:T(8,128)(2,1)S(1)}, u32[]{:S(2)}, u32[]{:S(2)}) collective-permute-start(bf16[512,128]{1,0:T(8,128)(2,1)S(1)} %get-tuple-element.37.refs_22_.refs_28_), channel_id=1, source_target_pairs={{1,0},{5,4},{9,8},{13,12},{17,16},{21,20},{25,24},{29,28}} | collective-permute-start | bytes 393224 | tf_op jit(solution)/shard_map/ppermute | solution.py:570
  44.8 1.3 %collective-permute-start.31 = (bf16[512,128]{1,0:T(8,128)(2,1)S(1)}, bf16[512,128]{1,0:T(8,128)(2,1)S(1)}, u32[]{:S(2)}, u32[]{:S(2)}) collective-permute-start(bf16[512,128]{1,0:T(8,128)(2,1)S(1)} %get-tuple-element.37.refs_22_.refs_28_), channel_id=1, source_target_pairs={{2,0},{6,4},{10,8},{14,12},{18,16},{22,20},{26,24},{30,28}} | collective-permute-start | bytes 393224 | tf_op jit(solution)/shard_map/ppermute | solution.py:570
  48.1 1.6 %collective-permute-done.30.refs_26_ = bf16[512,128]{1,0:T(8,128)(2,1)S(1)} collective-permute-done((bf16[512,128]{1,0:T(8,128)(2,1)S(1)}, bf16[512,128]{1,0:T(8,128)(2,1)S(1)}, u32[]{:S(2)}, u32[]{:S(2)}) %collective-permute-start.30) | collective-permute-done | bytes 131104 | tf_op jit(solution)/shard_map/ppermute | solution.py:570
  49.6 1.6 %collective-permute-start.3 = (f32[3,128,128]{2,1,0:T(8,128)S(1)}, f32[3,128,128]{2,1,0:T(8,128)S(1)}, u32[]{:S(2)}, u32[]{:S(2)}) collective-permute-start(f32[3,128,128]{2,1,0:T(8,128)S(1)} %products.1.near), channel_id=1, source_target_pairs={{0,4},{4,0},{8,12},{12,8},{16,20},{20,16},{24,28},{28,24},{1,5},{5... | collective-permute-start | bytes 589832 | tf_op jit(solution)/shard_map/ppermute | solution.py:154
  51.3 1.4 %collective-permute-start.15 = (bf16[3,64,1024]{2,1,0:T(8,128)(2,1)S(1)}, bf16[3,64,1024]{2,1,0:T(8,128)(2,1)S(1)}, u32[]{:S(2)}, u32[]{:S(2)}) collective-permute-start(bf16[3,64,1024]{2,1,0:T(8,128)(2,1)S(1)} %collective-permute-done.11.refs_2_), channel_id=1, source_target_pairs={{0,4},{4,0},{8,12},{12,8},{16,20},{20,16},{24,28},{28,24},{1,5},{5... | collective-permute-start | bytes 1179656 | tf_op jit(solution)/shard_map/ppermute | solution.py:154
  53.5 4.6 %heads.1.tail = bf16[320,128]{1,0:T(8,128)(2,1)S(1)} custom-call(s32[2,2]{1,0:T(2,128)S(1)} %copy-done.5, bf16[2,64,4096]{2,1,0:T(8,128)(2,1)S(1)} %bitcast.21, bf16[2,64,4096]{2,1,0:T(8,128)(2,1)S(1)} %bitcast.18, bf16[2,2,4096,128]{3,2,1,0:T(8,128)(2,1)S(1)} %bitcast.16, bf16[2,64,128]{2,1,0:T(8,128)(2,1)S(1)} %bitcast.22, bf16[2,64,128]{2,1,0:T(8,128)(2,1)S(1)} %bitcast.23), custom_call_target="tpu_custom_call" | custom-call | tf_op jit(solution)/shard_map/heads/pallas_call | solution.py:478
  58.1 2.5 %collective-permute-done.20.refs_11_ = bf16[4,64,512]{2,1,0:T(8,128)(2,1)S(1)} collective-permute-done((bf16[4,64,512]{2,1,0:T(8,128)(2,1)S(1)}, bf16[4,64,512]{2,1,0:T(8,128)(2,1)S(1)}, u32[]{:S(2)}, u32[]{:S(2)}) %collective-permute-start.20) | collective-permute-done | bytes 262176 | tf_op jit(solution)/shard_map/ppermute | solution.py:154
  60.9 2.4 %collective-permute-start.6 = (bf16[704,128]{1,0:T(8,128)(2,1)S(1)}, bf16[704,128]{1,0:T(8,128)(2,1)S(1)}, u32[]{:S(2)}, u32[]{:S(2)}) collective-permute-start(bf16[704,128]{1,0:T(8,128)(2,1)S(1)} %get-tuple-element.24.refs_0_), channel_id=1, source_target_pairs={{0,3},{1,2},{2,1},{3,0},{4,7},{5,6},{6,5},{7,4},{8,11},{9,10},{10,... | collective-permute-start | bytes 540680 | tf_op jit(solution)/shard_map/ppermute | solution.py:154
  63.2 2.2 %collective-permute-start.7 = (bf16[4,512,128]{2,1,0:T(8,128)(2,1)S(1)}, bf16[4,512,128]{2,1,0:T(8,128)(2,1)S(1)}, u32[]{:S(2)}, u32[]{:S(2)}) collective-permute-start(bf16[4,512,128]{2,1,0:T(8,128)(2,1)S(1)} %collective-permute-done.refs_0_.refs_23_), channel_id=1, source_target_pairs={{0,4},{4,0},{8,12},{12,8},{16,20},{20,16},{24,28},{28,24},{1,5},{5... | collective-permute-start | bytes 1572872 | tf_op jit(solution)/shard_map/ppermute | solution.py:154
  65.4 9.6 %collective-permute-done.4.refs_1_ = bf16[576,128]{1,0:T(8,128)(2,1)S(1)} collective-permute-done((bf16[576,128]{1,0:T(8,128)(2,1)S(1)}, bf16[576,128]{1,0:T(8,128)(2,1)S(1)}, u32[]{:S(2)}, u32[]{:S(2)}) %collective-permute-start.4) | collective-permute-done | bytes 147488 | tf_op jit(solution)/shard_map/ppermute | solution.py:154
  75.0 1.3 %collective-permute-start.8 = (bf16[4,512,128]{2,1,0:T(8,128)(2,1)S(1)}, bf16[4,512,128]{2,1,0:T(8,128)(2,1)S(1)}, u32[]{:S(2)}, u32[]{:S(2)}) collective-permute-start(bf16[4,512,128]{2,1,0:T(8,128)(2,1)S(1)} %collective-permute-done.1.refs_1_.refs_24_), channel_id=1, source_target_pairs={{0,4},{4,0},{8,12},{12,8},{16,20},{20,16},{24,28},{28,24},{1,5},{5... | collective-permute-start | bytes 1572872 | tf_op jit(solution)/shard_map/ppermute | solution.py:154
  76.3 1.5 %collective-permute-done.6.refs_3_ = bf16[704,128]{1,0:T(8,128)(2,1)S(1)} collective-permute-done((bf16[704,128]{1,0:T(8,128)(2,1)S(1)}, bf16[704,128]{1,0:T(8,128)(2,1)S(1)}, u32[]{:S(2)}, u32[]{:S(2)}) %collective-permute-start.6) | collective-permute-done | bytes 180256 | tf_op jit(solution)/shard_map/ppermute | solution.py:154
  79.2 2.2 %chain.1 = (bf16[2,5,64,128]{3,2,1,0:T(8,128)(2,1)S(1)}, bf16[128,384]{1,0:T(8,128)(2,1)S(1)}, bf16[2,64,128]{2,1,0:T(8,128)(2,1)S(1)}) custom-call(s32[5]{0:T(128)S(1)} %stack.23.place, bf16[704,128]{1,0:T(8,128)(2,1)S(1)} %get-tuple-element.24.refs_0_, bf16[576,128]{1,0:T(8,128)(2,1)S(1)} %collective-permute-done.4.refs_1_, ...), custom_call_target="tpu_custom_call" | custom-call | tf_op jit(solution)/shard_map/chain/pallas_call | solution.py:572
  81.5 1.9 %collective-permute-start.24 = (bf16[2,5,64,128]{3,2,1,0:T(8,128)(2,1)S(1)}, bf16[2,5,64,128]{3,2,1,0:T(8,128)(2,1)S(1)}, u32[]{:S(2)}, u32[]{:S(2)}) collective-permute-start(bf16[2,5,64,128]{3,2,1,0:T(8,128)(2,1)S(1)} %get-tuple-element.36.refs_14_), channel_id=1, source_target_pairs={{0,16},{4,20},{8,24},{12,28},{16,0},{20,4},{24,8},{28,12},{1,17},{... | collective-permute-start | bytes 491528 | tf_op jit(solution)/shard_map/ppermute | solution.py:159
  83.4 1.4 %collective-permute-start.25 = (bf16[2,5,64,128]{3,2,1,0:T(8,128)(2,1)S(1)}, bf16[2,5,64,128]{3,2,1,0:T(8,128)(2,1)S(1)}, u32[]{:S(2)}, u32[]{:S(2)}) collective-permute-start(bf16[2,5,64,128]{3,2,1,0:T(8,128)(2,1)S(1)} %get-tuple-element.36.refs_14_), channel_id=1, source_target_pairs={{0,24},{4,28},{8,0},{12,4},{16,8},{20,12},{24,16},{28,20},{1,25},{... | collective-permute-start | bytes 491528 | tf_op jit(solution)/shard_map/ppermute | solution.py:159
  85.7 1.4 %collective-permute-done.23.refs_15_ = bf16[2,5,64,128]{3,2,1,0:T(8,128)(2,1)S(1)} collective-permute-done((bf16[2,5,64,128]{3,2,1,0:T(8,128)(2,1)S(1)}, bf16[2,5,64,128]{3,2,1,0:T(8,128)(2,1)S(1)}, u32[]{:S(2)}, u32[]{:S(2)}) %collective-permute-start.23) | collective-permute-done | bytes 163872 | tf_op jit(solution)/shard_map/ppermute | solution.py:159
  87.2 1.5 %collective-permute-start.27 = (bf16[2,5,64,128]{3,2,1,0:T(8,128)(2,1)S(1)}, bf16[2,5,64,128]{3,2,1,0:T(8,128)(2,1)S(1)}, u32[]{:S(2)}, u32[]{:S(2)}) collective-permute-start(bf16[2,5,64,128]{3,2,1,0:T(8,128)(2,1)S(1)} %collective-permute-done.23.refs_15_), channel_id=1, source_target_pairs={{0,4},{4,0},{8,12},{12,8},{16,20},{20,16},{24,28},{28,24},{1,5},{5... | collective-permute-start | bytes 491528 | tf_op jit(solution)/shard_map/ppermute | solution.py:154
  88.6 7.2 %collective-permute-done.24.refs_16_ = bf16[2,5,64,128]{3,2,1,0:T(8,128)(2,1)S(1)} collective-permute-done((bf16[2,5,64,128]{3,2,1,0:T(8,128)(2,1)S(1)}, bf16[2,5,64,128]{3,2,1,0:T(8,128)(2,1)S(1)}, u32[]{:S(2)}, u32[]{:S(2)}) %collective-permute-start.24) | collective-permute-done | bytes 163872 | tf_op jit(solution)/shard_map/ppermute | solution.py:159
  96.4 2.1 %collective-permute-done.25.refs_17_ = bf16[2,5,64,128]{3,2,1,0:T(8,128)(2,1)S(1)} collective-permute-done((bf16[2,5,64,128]{3,2,1,0:T(8,128)(2,1)S(1)}, bf16[2,5,64,128]{3,2,1,0:T(8,128)(2,1)S(1)}, u32[]{:S(2)}, u32[]{:S(2)}) %collective-permute-start.25) | collective-permute-done | bytes 163872 | tf_op jit(solution)/shard_map/ppermute | solution.py:159
  99.0 3.7 %input_side.1 = bf16[2,64,4096]{2,1,0:T(8,128)(2,1)} custom-call(s32[5]{0:T(128)S(1)} %stack.23.place, bf16[2,64,4096]{2,1,0:T(8,128)(2,1)S(1)} %bitcast.19, bf16[128,384]{1,0:T(8,128)(2,1)S(1)} %get-tuple-element.26.steer, bf16[2,64,128]{2,1,0:T(8,128)(2,1)S(1)} %get-tuple-element.27.own, bf16[2,4096,128]{2,1,0:T(8,128)(2,1)S(1)} %get-tuple-element.28.held, ...), custom_call_target="tpu_custom_call" | custom-call | tf_op jit(solution)/shard_map/input_side/pallas_call | solution.py:592
  102.7 3.7 %weight_side.1 = f32[2,512,128]{2,1,0:T(8,128)} custom-call(s32[5]{0:T(128)S(1)} %stack.23.place, bf16[3,64,1024]{2,1,0:T(8,128)(2,1)S(1)} %get-tuple-element.29.refs_0_, bf16[3,64,1024]{2,1,0:T(8,128)(2,1)S(1)} %collective-permute-done.10.refs_1_, bf16[3,64,1024]{2,1,0:T(8,128)(2,1)S(1)} %collective-permute-done.11.refs_2_, ...), custom_call_target="tpu_custom_call" | custom-call | tf_op jit(solution)/shard_map/weight_side/pallas_call | solution.py:610
  (55 shorter events, 10.8 us)
Async XLA Ops:
  3.0 10.1 %collective-permute-start.10 = (bf16[3,64,1024]{2,1,0:T(8,128)(2,1)S(1)}, bf16[3,64,1024]{2,1,0:T(8,128)(2,1)S(1)}, u32[]{:S(2)}, u32[]{:S(2)}) collective-permute-start(bf16[3,64,1024]{2,1,0:T(8,128)(2,1)S(1)} %get-tuple-element.30), channel_id=1, source_target_pairs={{0,8},{4,12},{8,16},{12,20},{16,24},{20,28},{24,0},{28,4},{1,9},{5... | collective-permute-start | bytes 1179656 | tf_op jit(solution)/shard_map/ppermute | solution.py:159
  4.4 33.1 %collective-permute-start.11 = (bf16[3,64,1024]{2,1,0:T(8,128)(2,1)S(1)}, bf16[3,64,1024]{2,1,0:T(8,128)(2,1)S(1)}, u32[]{:S(2)}, u32[]{:S(2)}) collective-permute-start(bf16[3,64,1024]{2,1,0:T(8,128)(2,1)S(1)} %get-tuple-element.31), channel_id=1, source_target_pairs={{0,16},{4,20},{8,24},{12,28},{16,0},{20,4},{24,8},{28,12},{1,17},{... | collective-permute-start | bytes 1179656 | tf_op jit(solution)/shard_map/ppermute | solution.py:159
  7.5 36.0 %collective-permute-start = (bf16[4,512,128]{2,1,0:T(8,128)(2,1)S(1)}, bf16[4,512,128]{2,1,0:T(8,128)(2,1)S(1)}, u32[]{:S(2)}, u32[]{:S(2)}) collective-permute-start(bf16[4,512,128]{2,1,0:T(8,128)(2,1)S(1)} %get-tuple-element.21), channel_id=1, source_target_pairs={{0,1},{1,0},{2,3},{3,2},{4,5},{5,4},{6,7},{7,6},{8,9},{9,8},{10,11... | collective-permute-start | bytes 1572872 | tf_op jit(solution)/shard_map/ppermute | solution.py:154
  8.7 36.1 %collective-permute-start.1 = (bf16[4,512,128]{2,1,0:T(8,128)(2,1)S(1)}, bf16[4,512,128]{2,1,0:T(8,128)(2,1)S(1)}, u32[]{:S(2)}, u32[]{:S(2)}) collective-permute-start(bf16[4,512,128]{2,1,0:T(8,128)(2,1)S(1)} %get-tuple-element.22), channel_id=1, source_target_pairs={{0,2},{1,3},{2,0},{3,1},{4,6},{5,7},{6,4},{7,5},{8,10},{9,11},{10,... | collective-permute-start | bytes 1572872 | tf_op jit(solution)/shard_map/ppermute | solution.py:154
  10.1 30.1 %collective-permute-start.12 = (bf16[3,64,1024]{2,1,0:T(8,128)(2,1)S(1)}, bf16[3,64,1024]{2,1,0:T(8,128)(2,1)S(1)}, u32[]{:S(2)}, u32[]{:S(2)}) collective-permute-start(bf16[3,64,1024]{2,1,0:T(8,128)(2,1)S(1)} %get-tuple-element.32), channel_id=1, source_target_pairs={{0,24},{4,28},{8,0},{12,4},{16,8},{20,12},{24,16},{28,20},{1,25},{... | collective-permute-start | bytes 1179656 | tf_op jit(solution)/shard_map/ppermute | solution.py:159
  13.1 33.0 %collective-permute-start.2 = (bf16[4,512,128]{2,1,0:T(8,128)(2,1)S(1)}, bf16[4,512,128]{2,1,0:T(8,128)(2,1)S(1)}, u32[]{:S(2)}, u32[]{:S(2)}) collective-permute-start(bf16[4,512,128]{2,1,0:T(8,128)(2,1)S(1)} %get-tuple-element.23), channel_id=1, source_target_pairs={{0,3},{1,2},{2,1},{3,0},{4,7},{5,6},{6,5},{7,4},{8,11},{9,10},{10,... | collective-permute-start | bytes 1572872 | tf_op jit(solution)/shard_map/ppermute | solution.py:154
  37.4 15.3 %collective-permute-start.13 = (bf16[3,64,1024]{2,1,0:T(8,128)(2,1)S(1)}, bf16[3,64,1024]{2,1,0:T(8,128)(2,1)S(1)}, u32[]{:S(2)}, u32[]{:S(2)}) collective-permute-start(bf16[3,64,1024]{2,1,0:T(8,128)(2,1)S(1)} %get-tuple-element.29.refs_0_), channel_id=1, source_target_pairs={{0,4},{4,0},{8,12},{12,8},{16,20},{20,16},{24,28},{28,24},{1,5},{5... | collective-permute-start | bytes 1179656 | tf_op jit(solution)/shard_map/ppermute | solution.py:154
  41.1 11.6 %collective-permute-start.19 = (bf16[4,64,512]{2,1,0:T(8,128)(2,1)S(1)}, bf16[4,64,512]{2,1,0:T(8,128)(2,1)S(1)}, u32[]{:S(2)}, u32[]{:S(2)}) collective-permute-start(bf16[4,64,512]{2,1,0:T(8,128)(2,1)S(1)} %get-tuple-element.34), channel_id=1, source_target_pairs={{0,2},{1,3},{2,0},{3,1},{4,6},{5,7},{6,4},{7,5},{8,10},{9,11},{10,... | collective-permute-start | bytes 786440 | tf_op jit(solution)/shard_map/ppermute | solution.py:154
  43.5 6.2 %collective-permute-start.30 = (bf16[512,128]{1,0:T(8,128)(2,1)S(1)}, bf16[512,128]{1,0:T(8,128)(2,1)S(1)}, u32[]{:S(2)}, u32[]{:S(2)}) collective-permute-start(bf16[512,128]{1,0:T(8,128)(2,1)S(1)} %get-tuple-element.37.refs_22_.refs_28_), channel_id=1, source_target_pairs={{1,0},{5,4},{9,8},{13,12},{17,16},{21,20},{25,24},{29,28}} | collective-permute-start | bytes 393224 | tf_op jit(solution)/shard_map/ppermute | solution.py:570
  44.8 6.5 %collective-permute-start.31 = (bf16[512,128]{1,0:T(8,128)(2,1)S(1)}, bf16[512,128]{1,0:T(8,128)(2,1)S(1)}, u32[]{:S(2)}, u32[]{:S(2)}) collective-permute-start(bf16[512,128]{1,0:T(8,128)(2,1)S(1)} %get-tuple-element.37.refs_22_.refs_28_), channel_id=1, source_target_pairs={{2,0},{6,4},{10,8},{14,12},{18,16},{22,20},{26,24},{30,28}} | collective-permute-start | bytes 393224 | tf_op jit(solution)/shard_map/ppermute | solution.py:570
  46.1 14.8 %collective-permute-start.14 = (bf16[3,64,1024]{2,1,0:T(8,128)(2,1)S(1)}, bf16[3,64,1024]{2,1,0:T(8,128)(2,1)S(1)}, u32[]{:S(2)}, u32[]{:S(2)}) collective-permute-start(bf16[3,64,1024]{2,1,0:T(8,128)(2,1)S(1)} %collective-permute-done.10.refs_1_), channel_id=1, source_target_pairs={{0,4},{4,0},{8,12},{12,8},{16,20},{20,16},{24,28},{28,24},{1,5},{5... | collective-permute-start | bytes 1179656 | tf_op jit(solution)/shard_map/ppermute | solution.py:154
  49.6 3.2 %collective-permute-start.3 = (f32[3,128,128]{2,1,0:T(8,128)S(1)}, f32[3,128,128]{2,1,0:T(8,128)S(1)}, u32[]{:S(2)}, u32[]{:S(2)}) collective-permute-start(f32[3,128,128]{2,1,0:T(8,128)S(1)} %products.1.near), channel_id=1, source_target_pairs={{0,4},{4,0},{8,12},{12,8},{16,20},{20,16},{24,28},{28,24},{1,5},{5... | collective-permute-start | bytes 589832 | tf_op jit(solution)/shard_map/ppermute | solution.py:154
  51.3 9.6 %collective-permute-start.15 = (bf16[3,64,1024]{2,1,0:T(8,128)(2,1)S(1)}, bf16[3,64,1024]{2,1,0:T(8,128)(2,1)S(1)}, u32[]{:S(2)}, u32[]{:S(2)}) collective-permute-start(bf16[3,64,1024]{2,1,0:T(8,128)(2,1)S(1)} %collective-permute-done.11.refs_2_), channel_id=1, source_target_pairs={{0,4},{4,0},{8,12},{12,8},{16,20},{20,16},{24,28},{28,24},{1,5},{5... | collective-permute-start | bytes 1179656 | tf_op jit(solution)/shard_map/ppermute | solution.py:154
  52.7 7.9 %collective-permute-start.20 = (bf16[4,64,512]{2,1,0:T(8,128)(2,1)S(1)}, bf16[4,64,512]{2,1,0:T(8,128)(2,1)S(1)}, u32[]{:S(2)}, u32[]{:S(2)}) collective-permute-start(bf16[4,64,512]{2,1,0:T(8,128)(2,1)S(1)} %get-tuple-element.35), channel_id=1, source_target_pairs={{0,1},{1,0},{2,3},{3,2},{4,5},{5,4},{6,7},{7,6},{8,9},{9,8},{10,11... | collective-permute-start | bytes 786440 | tf_op jit(solution)/shard_map/ppermute | solution.py:154
  52.7 10.5 %collective-permute-start.16 = (bf16[3,64,1024]{2,1,0:T(8,128)(2,1)S(1)}, bf16[3,64,1024]{2,1,0:T(8,128)(2,1)S(1)}, u32[]{:S(2)}, u32[]{:S(2)}) collective-permute-start(bf16[3,64,1024]{2,1,0:T(8,128)(2,1)S(1)} %collective-permute-done.12.refs_3_), channel_id=1, source_target_pairs={{0,4},{4,0},{8,12},{12,8},{16,20},{20,16},{24,28},{28,24},{1,5},{5... | collective-permute-start | bytes 1179656 | tf_op jit(solution)/shard_map/ppermute | solution.py:154
  52.8 25.9 %collective-permute-start.17 = (bf16[4,64,1024]{2,1,0:T(8,128)(2,1)S(1)}, bf16[4,64,1024]{2,1,0:T(8,128)(2,1)S(1)}, u32[]{:S(2)}, u32[]{:S(2)}) collective-permute-start(bf16[4,64,1024]{2,1,0:T(8,128)(2,1)S(1)} %get-tuple-element.33), channel_id=1, source_target_pairs={{0,3},{1,2},{2,1},{3,0},{4,7},{5,6},{6,5},{7,4},{8,11},{9,10},{10,... | collective-permute-start | bytes 1572872 | tf_op jit(solution)/shard_map/ppermute | solution.py:154
  60.6 14.4 %collective-permute-start.4 = (bf16[576,128]{1,0:T(8,128)(2,1)S(1)}, bf16[576,128]{1,0:T(8,128)(2,1)S(1)}, u32[]{:S(2)}, u32[]{:S(2)}) collective-permute-start(bf16[576,128]{1,0:T(8,128)(2,1)S(1)} %get-tuple-element.25), channel_id=1, source_target_pairs={{0,1},{1,0},{2,3},{3,2},{4,5},{5,4},{6,7},{7,6},{8,9},{9,8},{10,11... | collective-permute-start | bytes 442376 | tf_op jit(solution)/shard_map/ppermute | solution.py:154
  60.9 15.5 %collective-permute-start.5 = (bf16[576,128]{1,0:T(8,128)(2,1)S(1)}, bf16[576,128]{1,0:T(8,128)(2,1)S(1)}, u32[]{:S(2)}, u32[]{:S(2)}) collective-permute-start(bf16[576,128]{1,0:T(8,128)(2,1)S(1)} %get-tuple-element.25), channel_id=1, source_target_pairs={{0,2},{1,3},{2,0},{3,1},{4,6},{5,7},{6,4},{7,5},{8,10},{9,11},{10,... | collective-permute-start | bytes 442376 | tf_op jit(solution)/shard_map/ppermute | solution.py:154
  60.9 17.0 %collective-permute-start.6 = (bf16[704,128]{1,0:T(8,128)(2,1)S(1)}, bf16[704,128]{1,0:T(8,128)(2,1)S(1)}, u32[]{:S(2)}, u32[]{:S(2)}) collective-permute-start(bf16[704,128]{1,0:T(8,128)(2,1)S(1)} %get-tuple-element.24.refs_0_), channel_id=1, source_target_pairs={{0,3},{1,2},{2,1},{3,0},{4,7},{5,6},{6,5},{7,4},{8,11},{9,10},{10,... | collective-permute-start | bytes 540680 | tf_op jit(solution)/shard_map/ppermute | solution.py:154
  63.2 18.3 %collective-permute-start.7 = (bf16[4,512,128]{2,1,0:T(8,128)(2,1)S(1)}, bf16[4,512,128]{2,1,0:T(8,128)(2,1)S(1)}, u32[]{:S(2)}, u32[]{:S(2)}) collective-permute-start(bf16[4,512,128]{2,1,0:T(8,128)(2,1)S(1)} %collective-permute-done.refs_0_.refs_23_), channel_id=1, source_target_pairs={{0,4},{4,0},{8,12},{12,8},{16,20},{20,16},{24,28},{28,24},{1,5},{5... | collective-permute-start | bytes 1572872 | tf_op jit(solution)/shard_map/ppermute | solution.py:154
  75.0 8.4 %collective-permute-start.8 = (bf16[4,512,128]{2,1,0:T(8,128)(2,1)S(1)}, bf16[4,512,128]{2,1,0:T(8,128)(2,1)S(1)}, u32[]{:S(2)}, u32[]{:S(2)}) collective-permute-start(bf16[4,512,128]{2,1,0:T(8,128)(2,1)S(1)} %collective-permute-done.1.refs_1_.refs_24_), channel_id=1, source_target_pairs={{0,4},{4,0},{8,12},{12,8},{16,20},{20,16},{24,28},{28,24},{1,5},{5... | collective-permute-start | bytes 1572872 | tf_op jit(solution)/shard_map/ppermute | solution.py:154
  76.3 2.4 %collective-permute-start.21 = (bf16[4,64,512]{2,1,0:T(8,128)(2,1)S(1)}, bf16[4,64,512]{2,1,0:T(8,128)(2,1)S(1)}, u32[]{:S(2)}, u32[]{:S(2)}) collective-permute-start(bf16[4,64,512]{2,1,0:T(8,128)(2,1)S(1)} %collective-permute-done.19.refs_10_), channel_id=1, source_target_pairs={{0,4},{4,0},{8,12},{12,8},{16,20},{20,16},{24,28},{28,24},{1,5},{5... | collective-permute-start | bytes 786440 | tf_op jit(solution)/shard_map/ppermute | solution.py:154
  77.8 6.9 %collective-permute-start.9 = (bf16[4,512,128]{2,1,0:T(8,128)(2,1)S(1)}, bf16[4,512,128]{2,1,0:T(8,128)(2,1)S(1)}, u32[]{:S(2)}, u32[]{:S(2)}) collective-permute-start(bf16[4,512,128]{2,1,0:T(8,128)(2,1)S(1)} %collective-permute-done.2.refs_2_.refs_25_), channel_id=1, source_target_pairs={{0,4},{4,0},{8,12},{12,8},{16,20},{20,16},{24,28},{28,24},{1,5},{5... | collective-permute-start | bytes 1572872 | tf_op jit(solution)/shard_map/ppermute | solution.py:154
  78.7 2.7 %collective-permute-start.22 = (bf16[4,64,512]{2,1,0:T(8,128)(2,1)S(1)}, bf16[4,64,512]{2,1,0:T(8,128)(2,1)S(1)}, u32[]{:S(2)}, u32[]{:S(2)}) collective-permute-start(bf16[4,64,512]{2,1,0:T(8,128)(2,1)S(1)} %collective-permute-done.20.refs_11_), channel_id=1, source_target_pairs={{0,4},{4,0},{8,12},{12,8},{16,20},{20,16},{24,28},{28,24},{1,5},{5... | collective-permute-start | bytes 786440 | tf_op jit(solution)/shard_map/ppermute | solution.py:154
  78.7 24.0 %collective-permute-start.18 = (bf16[4,64,1024]{2,1,0:T(8,128)(2,1)S(1)}, bf16[4,64,1024]{2,1,0:T(8,128)(2,1)S(1)}, u32[]{:S(2)}, u32[]{:S(2)}) collective-permute-start(bf16[4,64,1024]{2,1,0:T(8,128)(2,1)S(1)} %collective-permute-done.17.refs_8_), channel_id=1, source_target_pairs={{0,4},{4,0},{8,12},{12,8},{16,20},{20,16},{24,28},{28,24},{1,5},{5... | collective-permute-start | bytes 1572872 | tf_op jit(solution)/shard_map/ppermute | solution.py:154
  81.4 5.7 %collective-permute-start.23 = (bf16[2,5,64,128]{3,2,1,0:T(8,128)(2,1)S(1)}, bf16[2,5,64,128]{3,2,1,0:T(8,128)(2,1)S(1)}, u32[]{:S(2)}, u32[]{:S(2)}) collective-permute-start(bf16[2,5,64,128]{3,2,1,0:T(8,128)(2,1)S(1)} %get-tuple-element.36.refs_14_), channel_id=1, source_target_pairs={{0,8},{4,12},{8,16},{12,20},{16,24},{20,28},{24,0},{28,4},{1,9},{5... | collective-permute-start | bytes 491528 | tf_op jit(solution)/shard_map/ppermute | solution.py:159
  81.5 14.3 %collective-permute-start.24 = (bf16[2,5,64,128]{3,2,1,0:T(8,128)(2,1)S(1)}, bf16[2,5,64,128]{3,2,1,0:T(8,128)(2,1)S(1)}, u32[]{:S(2)}, u32[]{:S(2)}) collective-permute-start(bf16[2,5,64,128]{3,2,1,0:T(8,128)(2,1)S(1)} %get-tuple-element.36.refs_14_), channel_id=1, source_target_pairs={{0,16},{4,20},{8,24},{12,28},{16,0},{20,4},{24,8},{28,12},{1,17},{... | collective-permute-start | bytes 491528 | tf_op jit(solution)/shard_map/ppermute | solution.py:159
  83.4 15.1 %collective-permute-start.25 = (bf16[2,5,64,128]{3,2,1,0:T(8,128)(2,1)S(1)}, bf16[2,5,64,128]{3,2,1,0:T(8,128)(2,1)S(1)}, u32[]{:S(2)}, u32[]{:S(2)}) collective-permute-start(bf16[2,5,64,128]{3,2,1,0:T(8,128)(2,1)S(1)} %get-tuple-element.36.refs_14_), channel_id=1, source_target_pairs={{0,24},{4,28},{8,0},{12,4},{16,8},{20,12},{24,16},{28,20},{1,25},{... | collective-permute-start | bytes 491528 | tf_op jit(solution)/shard_map/ppermute | solution.py:159
  84.8 17.9 %collective-permute-start.26 = (bf16[2,5,64,128]{3,2,1,0:T(8,128)(2,1)S(1)}, bf16[2,5,64,128]{3,2,1,0:T(8,128)(2,1)S(1)}, u32[]{:S(2)}, u32[]{:S(2)}) collective-permute-start(bf16[2,5,64,128]{3,2,1,0:T(8,128)(2,1)S(1)} %get-tuple-element.36.refs_14_), channel_id=1, source_target_pairs={{0,4},{4,0},{8,12},{12,8},{16,20},{20,16},{24,28},{28,24},{1,5},{5... | collective-permute-start | bytes 491528 | tf_op jit(solution)/shard_map/ppermute | solution.py:154
  87.2 15.6 %collective-permute-start.27 = (bf16[2,5,64,128]{3,2,1,0:T(8,128)(2,1)S(1)}, bf16[2,5,64,128]{3,2,1,0:T(8,128)(2,1)S(1)}, u32[]{:S(2)}, u32[]{:S(2)}) collective-permute-start(bf16[2,5,64,128]{3,2,1,0:T(8,128)(2,1)S(1)} %collective-permute-done.23.refs_15_), channel_id=1, source_target_pairs={{0,4},{4,0},{8,12},{12,8},{16,20},{20,16},{24,28},{28,24},{1,5},{5... | collective-permute-start | bytes 491528 | tf_op jit(solution)/shard_map/ppermute | solution.py:154
  95.8 6.9 %collective-permute-start.28 = (bf16[2,5,64,128]{3,2,1,0:T(8,128)(2,1)S(1)}, bf16[2,5,64,128]{3,2,1,0:T(8,128)(2,1)S(1)}, u32[]{:S(2)}, u32[]{:S(2)}) collective-permute-start(bf16[2,5,64,128]{3,2,1,0:T(8,128)(2,1)S(1)} %collective-permute-done.24.refs_16_), channel_id=1, source_target_pairs={{0,4},{4,0},{8,12},{12,8},{16,20},{20,16},{24,28},{28,24},{1,5},{5... | collective-permute-start | bytes 491528 | tf_op jit(solution)/shard_map/ppermute | solution.py:154
  98.5 4.2 %collective-permute-start.29 = (bf16[2,5,64,128]{3,2,1,0:T(8,128)(2,1)S(1)}, bf16[2,5,64,128]{3,2,1,0:T(8,128)(2,1)S(1)}, u32[]{:S(2)}, u32[]{:S(2)}) collective-permute-start(bf16[2,5,64,128]{3,2,1,0:T(8,128)(2,1)S(1)} %collective-permute-done.25.refs_17_), channel_id=1, source_target_pairs={{0,4},{4,0},{8,12},{12,8},{16,20},{20,16},{24,28},{28,24},{1,5},{5... | collective-permute-start | bytes 491528 | tf_op jit(solution)/shard_map/ppermute | solution.py:154
  (6 other events, 96.7 us)

commit v2 on v1

--- a/solution.py
+++ b/solution.py
@@ -313,15 +313,13 @@
 
 
 def pick_columns(steps, width, place, inputs, cot, *refs):
-    outs, sems = refs[:steps], refs[steps]
+    outs, halves, sems = refs[:steps], refs[steps : 2 * steps], refs[2 * steps]
     copies = []
     for distance in range(steps):
         start = pl.multiple_of((place[2] + distance) % steps * 2 * width, 128)
         copies.append(
             pltpu.make_async_copy(
-                inputs.at[:, :, pl.ds(start, 2 * width)],
-                outs[distance].at[0:2],
-                sems.at[3 * distance],
+                inputs.at[:, :, pl.ds(start, 2 * width)], outs[distance], sems.at[3 * distance]
             )
         )
         for way in range(2):
@@ -329,25 +327,20 @@
             copies.append(
                 pltpu.make_async_copy(
                     cot.at[way, :, pl.ds(half, width)],
-                    outs[distance].at[2, :, way * width : (way + 1) * width],
+                    halves[distance].at[way],
                     sems.at[3 * distance + 1 + way],
                 )
             )
     carried_out(copies)
 
 
-def pick_moving(steps, *refs):
-    sources, upward, sems = refs[:steps], refs[steps], refs[steps + 3]
-    width = upward.shape[-1] // 2
+def pick_moving(steps, which, *refs):
+    sources, outs, sems = refs[:steps], refs[steps:-1], refs[-1]
     copies = []
     for step, source in enumerate(sources):
-        copies.append(pltpu.make_async_copy(source.at[1], upward.at[step], sems.at[3 * step]))
-        for way in range(2):
-            half = source.at[2, :, way * width : (way + 1) * width]
+        for index, out in zip(which, outs):
             copies.append(
-                pltpu.make_async_copy(
-                    half, refs[steps + 1 + way].at[step], sems.at[3 * step + 1 + way]
-                )
+                pltpu.make_async_copy(source.at[index], out.at[step], sems.at[len(copies)])
             )
     carried_out(copies)
 
@@ -365,6 +358,7 @@
 
 def weight_kernel(sections, steps, tokens, place, *refs):
     columns = refs[: 2 * steps]
+    halves, refs = refs[2 * steps : 4 * steps], refs[2 * steps :]
     mirrored, lent = refs[2 * steps : 2 * steps + 2], refs[2 * steps + 2 : 2 * steps + 6]
     sent = refs[2 * steps + 6 : 4 * steps + 6]
     refs = refs[4 * steps + 6 :]
@@ -388,11 +382,10 @@
     for index in range(2 * steps):
         for way in range(2):
             both = slice(way * every + index * tokens, way * every + (index + 1) * tokens)
-            half = slice(way * width, (way + 1) * width)
 
             @pl.when(place[3 + way] == place[1])
             def _():
-                rights[both, :] = columns[index][2, :, half]
+                rights[both, :] = halves[index][way]
 
             @pl.when(place[3 + way] != place[1])
             def _():
@@ -400,18 +393,18 @@
 
     def corrected(here, way):
         rows = slice(way * every, (way + 1) * every)
-        total = rights[rows, :].astype(jnp.float32)
+        blocks = []
         for far in range(1, sections - here):
             holder = here + far if way == 0 else sections - 1 - here - far
             if holder == here:
-                held = own_slice[...]
+                blocks.append(own_slice[...])
             elif way == 1 and holder > here:
-                held = lent_slices[holder ^ here][...]
+                blocks.append(lent_slices[holder ^ here][...])
             else:
-                held = fetched[holder ^ here][place[2]]
-            steer = steers[way, :, (far - 1) * head : far * head]
-            total += contract(steer, held, 1, 1)
-        rights[rows, :] = total.astype(jnp.bfloat16)
+                blocks.append(fetched[holder ^ here][place[2]])
+        steer = steers[way, :, : len(blocks) * head]
+        total = contract(steer, jnp.concatenate(blocks, axis=1), 1, 1)
+        rights[rows, :] = (rights[rows, :].astype(jnp.float32) + total).astype(jnp.bfloat16)
 
     for here in range(sections - 1):
 
@@ -459,18 +452,42 @@
     for mask in range(sections - 1, 0, -1):
         fetched[mask] = swapped(picked[mask - 1], "section", mask)
 
+    wide = jax.ShapeDtypeStruct((2, tokens, 2 * width), jnp.bfloat16)
+    slim = jax.ShapeDtypeStruct((2, tokens, width), jnp.bfloat16)
     picked = pl.pallas_call(
         functools.partial(pick_columns, steps, width),
         in_specs=[scalars] + [hbm] * 2,
-        out_specs=[memory] * steps,
-        out_shape=[jax.ShapeDtypeStruct((3, tokens, 2 * width), jnp.bfloat16)] * steps,
+        out_specs=[memory] * (2 * steps),
+        out_shape=[wide] * steps + [slim] * steps,
         scratch_shapes=[pltpu.SemaphoreType.DMA((3 * steps,))],
         name="pick_columns",
         compiler_params=pltpu.CompilerParams(vmem_limit_bytes=52 << 20),
     )(place, inputs, cot)
-    near_columns = [picked[0]]
+    near_columns, near_halves = [picked[0]], [picked[steps]]
+    for distance in range(1, steps):
+        near_halves.append(shifted(picked[steps + distance], distance))
     for distance in range(1, steps):
         near_columns.append(shifted(picked[distance], distance))
+
+    def moving(sources, which, shape):
+        return pl.pallas_call(
+            functools.partial(pick_moving, steps, which),
+            in_specs=[anywhere] * steps,
+            out_specs=[memory] * len(which),
+            out_shape=[jax.ShapeDtypeStruct((steps,) + shape, jnp.bfloat16)] * len(which),
+            scratch_shapes=[pltpu.SemaphoreType.DMA((steps * len(which),))],
+            name="pick_moving",
+            compiler_params=pltpu.CompilerParams(vmem_limit_bytes=8 << 20),
+        )(*sources)
+
+    sideways = moving(near_halves, (0, 1), (tokens, width))
+    near_aside, far_aside, far_columns, far_halves = [], [], [], []
+    for way in range(2):
+        near_aside.append(swapped(sideways[way], "section", asides[way]))
+    for way in range(2):
+        far_aside.append(swapped(near_aside[way], "dp", 1))
+    for distance in range(steps):
+        far_halves.append(swapped(near_halves[distance], "dp", 1))
 
     lengths = valid_lengths
     blocks = 4
@@ -542,24 +559,9 @@
     for mask in range(1, sections):
         parts.append(swapped(full if mask == sections - 1 else short, "section", mask))
 
-    upward, *sideways = pl.pallas_call(
-        functools.partial(pick_moving, steps),
-        in_specs=[anywhere] * steps,
-        out_specs=[memory] * 3,
-        out_shape=[jax.ShapeDtypeStruct((steps, tokens, 2 * width), jnp.bfloat16)]
-        + [jax.ShapeDtypeStruct((steps, tokens, width), jnp.bfloat16)] * 2,
-        scratch_shapes=[pltpu.SemaphoreType.DMA((3 * steps,))],
-        name="pick_moving",
-        compiler_params=pltpu.CompilerParams(vmem_limit_bytes=8 << 20),
-    )(*near_columns)
+    (upward,) = moving(near_columns, (1,), (tokens, 2 * width))
     near_mirror = swapped(upward, "section", sections - 1)
-    near_aside, far_aside = [], []
-    for way in range(2):
-        near_aside.append(swapped(sideways[way], "section", asides[way]))
     far_mirror = swapped(near_mirror, "dp", 1)
-    for way in range(2):
-        far_aside.append(swapped(near_aside[way], "dp", 1))
-    far_columns = []
     for distance in range(steps):
         far_columns.append(swapped(near_columns[distance], "dp", 1))
     lent = [own_slice]
@@ -609,7 +611,7 @@
     every = replicas * tokens
     weight_grads = pl.pallas_call(
         functools.partial(weight_kernel, sections, steps, tokens),
-        in_specs=[scalars] + [memory] * (4 * steps + 2 * sections + 5),
+        in_specs=[scalars] + [memory] * (6 * steps + 2 * sections + 5),
         out_specs=memory,
         out_shape=jax.ShapeDtypeStruct((2, width, head), jnp.float32),
         scratch_shapes=[
@@ -623,6 +625,8 @@
         place,
         *near_columns,
         *far_columns,
+        *near_halves,
+        *far_halves,
         near_mirror,
         far_mirror,
         *near_aside,

time: 107 us -> 121 us (1.13)
  starting transfers between devices: 33.1 us -> 43.7 us
  local copies, waits for them, and re-layouts: 0.11 us -> 5.15 us
  waiting for transfers between devices: 51 us -> 47.1 us
  Pallas kernels: 21.4 us -> 23.8 us
    ppermute x6 -> x9, waiting for transfers between devices: 35.8 us -> 18.9 us  [shifted(): lax.ppermute(block, 'dp', [(i, (i + 2 * distance) % count) for i in range...]
    ppermute x24 -> x28, waiting for transfers between devices: 13.7 us -> 27.2 us  [swapped(): lax.ppermute(block, axis, [(i, i ^ mask) for i in range(lax.axis_size(axi...]
    ppermute x24 -> x28, starting transfers between devices: 23.3 us -> 30.4 us  [swapped(): lax.ppermute(block, axis, [(i, i ^ mask) for i in range(lax.axis_size(axi...]
    unnamed x12 -> x28, local copies, waits for them, and re-layouts: 0.03 us -> 5.07 us
    ppermute x6 -> x9, starting transfers between devices: 7.18 us -> 10.7 us  [shifted(): lax.ppermute(block, 'dp', [(i, (i + 2 * distance) % count) for i in range...]
  transfers between devices with their start and end apart: 32 -> 39, of which waited for: 10 -> 14; matrix products, arithmetic and copies ran while one was open for 0% -> 0% of each run, Pallas kernels for 15% -> 14%
where the time goes in v2:
time: 121 us
  waiting for transfers between devices  47.1 us (39%)
  starting transfers between devices  43.7 us (36%)
  Pallas kernels  23.8 us (20%)
  local copies, waits for them, and re-layouts  5.15 us (4%)
    ppermute x28, starting transfers between devices, swapped(): lax.ppermute(block, axis, [(i, i ^ mask) for i in range(lax.axis_size(axi...  30.4 us
    ppermute x28, waiting for transfers between devices, swapped(): lax.ppermute(block, axis, [(i, i ^ mask) for i in range(lax.axis_size(axi...  27.2 us
    ppermute x9, waiting for transfers between devices, shifted(): lax.ppermute(block, 'dp', [(i, (i + 2 * distance) % count) for i in range...  18.9 us
    ppermute x9, starting transfers between devices, shifted(): lax.ppermute(block, 'dp', [(i, (i + 2 * distance) % count) for i in range...  10.7 us
    unnamed x28, local copies, waits for them, and re-layouts  5.07 us
    pallas_call x1, Pallas kernels, gathered(): pl.pallas_call(functools.partial(heads_kernel, length), grid=(blocks,), i...  4.58 us
    pallas_call x1, Pallas kernels, gathered(): pl.pallas_call(functools.partial(weight_kernel, sections, steps, tokens),...  4.01 us
    pallas_call x1, Pallas kernels, gathered(): pl.pallas_call(functools.partial(input_kernel, sections, tokens), grid=(s...  3.67 us
  transfers between devices with their start and end apart: 39, of which 14 were waited for; matrix products, arithmetic and copies ran while one was open for 0% of the time, Pallas kernels for 14%

profile of v2, /device:TPU:9, one launch (start us, length us, event | category | flops | bytes accessed | tf_op | source)
XLA Modules:
  0.0 120.6 jit_solution(17746302050955945736)
XLA Ops:
  0.7 2.9 %pick_columns.1 = (bf16[2,64,1024]{2,1,0:T(8,128)(2,1)S(1)}, bf16[2,64,1024]{2,1,0:T(8,128)(2,1)}, bf16[2,64,1024]{2,1,0:T(8,128)(2,1)}, bf16[2,64,1024]{2,1,0:T...) custom-call(s32[5]{0:T(128)S(1)} %stack.23.place, ...), custom_call_target="tpu_custom_call" | custom-call | tf_op jit(solution)/shard_map/pick_columns/pallas_call | solution.py:457
  3.6 1.3 %collective-permute-start.17 = (bf16[2,64,512]{2,1,0:T(8,128)(2,1)S(1)}, bf16[2,64,512]{2,1,0:T(8,128)(2,1)S(1)}, u32[]{:S(2)}, u32[]{:S(2)}) collective-permute-start(bf16[2,64,512]{2,1,0:T(8,128)(2,1)S(1)} %get-tuple-element.37), channel_id=1, source_target_pairs={{0,8},{4,12},{8,16},{12,20},{16,24},{20,28},{24,0},{28,4},{1,9},{5... | collective-permute-start | bytes 393224 | tf_op jit(solution)/shard_map/ppermute | solution.py:159
  6.1 1.4 %collective-permute-start.19 = (bf16[2,64,512]{2,1,0:T(8,128)(2,1)S(1)}, bf16[2,64,512]{2,1,0:T(8,128)(2,1)S(1)}, u32[]{:S(2)}, u32[]{:S(2)}) collective-permute-start(bf16[2,64,512]{2,1,0:T(8,128)(2,1)S(1)} %get-tuple-element.39), channel_id=1, source_target_pairs={{0,24},{4,28},{8,0},{12,4},{16,8},{20,12},{24,16},{28,20},{1,25},{... | collective-permute-start | bytes 393224 | tf_op jit(solution)/shard_map/ppermute | solution.py:159
  7.4 1.5 %collective-permute-start.20 = (bf16[2,64,512]{2,1,0:T(8,128)(2,1)S(1)}, bf16[2,64,512]{2,1,0:T(8,128)(2,1)S(1)}, u32[]{:S(2)}, u32[]{:S(2)}) collective-permute-start(bf16[2,64,512]{2,1,0:T(8,128)(2,1)S(1)} %get-tuple-element.36.refs_0_.refs_8_), channel_id=1, source_target_pairs={{0,4},{4,0},{8,12},{12,8},{16,20},{20,16},{24,28},{28,24},{1,5},{5... | collective-permute-start | bytes 393224 | tf_op jit(solution)/shard_map/ppermute | solution.py:154
  9.0 2.2 %copy-done = bf16[1,2,2,4096,128]{4,3,2,1,0:T(8,128)(2,1)S(1)} copy-done((bf16[1,2,2,4096,128]{4,3,2,1,0:T(8,128)(2,1)S(1)}, bf16[1,2,2,4096,128]{4,3,2,1,0:T(8,128)(2,1)}, u32[]{:S(2)}) %copy-start) | copy-done | bytes 4194328
  12.1 1.3 %collective-permute-start.37 = (bf16[512,128]{1,0:T(8,128)(2,1)S(1)}, bf16[512,128]{1,0:T(8,128)(2,1)S(1)}, u32[]{:S(2)}, u32[]{:S(2)}) collective-permute-start(bf16[512,128]{1,0:T(8,128)(2,1)S(1)} %get-tuple-element.43.refs_30_.refs_36_), channel_id=1, source_target_pairs={{1,0},{5,4},{9,8},{13,12},{17,16},{21,20},{25,24},{29,28}} | collective-permute-start | bytes 393224 | tf_op jit(solution)/shard_map/ppermute | solution.py:572
  13.5 2.1 %collective-permute-done.18.refs_2_.refs_10_ = bf16[2,64,512]{2,1,0:T(8,128)(2,1)} collective-permute-done((bf16[2,64,512]{2,1,0:T(8,128)(2,1)S(1)}, bf16[2,64,512]{2,1,0:T(8,128)(2,1)}, u32[]{:S(2)}, u32[]{:S(2)}) %collective-permute-start.18) | collective-permute-done | bytes 131104 | tf_op jit(solution)/shard_map/ppermute | solution.py:159
  15.6 3.2 %collective-permute-start.11 = (bf16[2,64,1024]{2,1,0:T(8,128)(2,1)}, bf16[2,64,1024]{2,1,0:T(8,128)(2,1)S(1)}, u32[]{:S(2)}, u32[]{:S(2)}) collective-permute-start(bf16[2,64,1024]{2,1,0:T(8,128)(2,1)} %get-tuple-element.34), channel_id=1, source_target_pairs={{0,16},{4,20},{8,24},{12,28},{16,0},{20,4},{24,8},{28,12},{1,17},{... | collective-permute-start | bytes 786440 | tf_op jit(solution)/shard_map/ppermute | solution.py:159
  18.8 10.6 %collective-permute-done.19.refs_3_.refs_11_ = bf16[2,64,512]{2,1,0:T(8,128)(2,1)S(1)} collective-permute-done((bf16[2,64,512]{2,1,0:T(8,128)(2,1)S(1)}, bf16[2,64,512]{2,1,0:T(8,128)(2,1)S(1)}, u32[]{:S(2)}, u32[]{:S(2)}) %collective-permute-start.19) | collective-permute-done | bytes 131104 | tf_op jit(solution)/shard_map/ppermute | solution.py:159
  30.7 1.3 %collective-permute-start.38 = (bf16[512,128]{1,0:T(8,128)(2,1)S(1)}, bf16[512,128]{1,0:T(8,128)(2,1)}, u32[]{:S(2)}, u32[]{:S(2)}) collective-permute-start(bf16[512,128]{1,0:T(8,128)(2,1)S(1)} %get-tuple-element.43.refs_30_.refs_36_), channel_id=1, source_target_pairs={{2,0},{6,4},{10,8},{14,12},{18,16},{22,20},{26,24},{30,28}} | collective-permute-start | bytes 393224 | tf_op jit(solution)/shard_map/ppermute | solution.py:572
  33.5 2.4 %pick_weights.1 = (bf16[4,512,128]{2,1,0:T(8,128)(2,1)S(1)}, bf16[4,512,128]{2,1,0:T(8,128)(2,1)S(1)}, bf16[4,512,128]{2,1,0:T(8,128)(2,1)S(1)}) custom-call(s32[5]{0:T(128)S(1)} %stack.23.place, bf16[2,2,4,2,512,128]{5,4,3,2,1,0:T(8,128)(2,1)} %bitcast.13), custom_call_target="tpu_custom_call" | custom-call | tf_op jit(solution)/shard_map/pick_weights/pallas_call | solution.py:442
  37.0 1.6 %collective-permute-start.21 = (bf16[2,64,512]{2,1,0:T(8,128)(2,1)S(1)}, bf16[2,64,512]{2,1,0:T(8,128)(2,1)S(1)}, u32[]{:S(2)}, u32[]{:S(2)}) collective-permute-start(bf16[2,64,512]{2,1,0:T(8,128)(2,1)S(1)} %collective-permute-done.17.refs_1_.refs_9_), channel_id=1, source_target_pairs={{0,4},{4,0},{8,12},{12,8},{16,20},{20,16},{24,28},{28,24},{1,5},{5... | collective-permute-start | bytes 393224 | tf_op jit(solution)/shard_map/ppermute | solution.py:154
  39.2 1.7 %collective-permute-done.12.refs_3_ = bf16[2,64,1024]{2,1,0:T(8,128)(2,1)S(1)} collective-permute-done((bf16[2,64,1024]{2,1,0:T(8,128)(2,1)}, bf16[2,64,1024]{2,1,0:T(8,128)(2,1)S(1)}, u32[]{:S(2)}, u32[]{:S(2)}) %collective-permute-start.12) | collective-permute-done | bytes 262176 | tf_op jit(solution)/shard_map/ppermute | solution.py:159
  40.9 2.2 %collective-permute-start.2 = (bf16[4,512,128]{2,1,0:T(8,128)(2,1)S(1)}, bf16[4,512,128]{2,1,0:T(8,128)(2,1)S(1)}, u32[]{:S(2)}, u32[]{:S(2)}) collective-permute-start(bf16[4,512,128]{2,1,0:T(8,128)(2,1)S(1)} %get-tuple-element.26), channel_id=1, source_target_pairs={{0,3},{1,2},{2,1},{3,0},{4,7},{5,6},{6,5},{7,4},{8,11},{9,10},{10,... | collective-permute-start | bytes 1572872 | tf_op jit(solution)/shard_map/ppermute | solution.py:154
  44.7 1.3 %pick_moving.3 = (bf16[4,64,512]{2,1,0:T(8,128)(2,1)S(1)}, bf16[4,64,512]{2,1,0:T(8,128)(2,1)S(1)}) custom-call(bf16[2,64,512]{2,1,0:T(8,128)(2,1)S(1)} %get-tuple-element.36.refs_0_.refs_8_, bf16[2,64,512]{2,1,0:T(8,128)(2,1)S(1)} %collective-permute-done.17.refs_1_.refs_9_, bf16[2,64,512]{2,1,0:T(8,128)(2,1)} %collective-permute-done.18.refs_2_.refs_10_, ...), custom_call_target="tpu_custom_call" | custom-call | tf_op jit(solution)/shard_map/pick_moving/pallas_call | solution.py:473
  48.2 19.7 %collective-permute-done.26.refs_18_ = bf16[4,64,512]{2,1,0:T(8,128)(2,1)S(1)} collective-permute-done((bf16[4,64,512]{2,1,0:T(8,128)(2,1)S(1)}, bf16[4,64,512]{2,1,0:T(8,128)(2,1)S(1)}, u32[]{:S(2)}, u32[]{:S(2)}) %collective-permute-start.26) | collective-permute-done | bytes 262176 | tf_op jit(solution)/shard_map/ppermute | solution.py:154
  67.8 1.9 %collective-permute-start.14 = (bf16[2,64,1024]{2,1,0:T(8,128)(2,1)S(1)}, bf16[2,64,1024]{2,1,0:T(8,128)(2,1)S(1)}, u32[]{:S(2)}, u32[]{:S(2)}) collective-permute-start(bf16[2,64,1024]{2,1,0:T(8,128)(2,1)S(1)} %collective-permute-done.10.refs_1_), channel_id=1, source_target_pairs={{0,4},{4,0},{8,12},{12,8},{16,20},{20,16},{24,28},{28,24},{1,5},{5... | collective-permute-start | bytes 786440 | tf_op jit(solution)/shard_map/ppermute | solution.py:154
  70.5 1.8 %collective-permute-start.24 = (bf16[4,64,1024]{2,1,0:T(8,128)(2,1)S(1)}, bf16[4,64,1024]{2,1,0:T(8,128)(2,1)S(1)}, u32[]{:S(2)}, u32[]{:S(2)}) collective-permute-start(bf16[4,64,1024]{2,1,0:T(8,128)(2,1)S(1)} %pick_moving.2), channel_id=1, source_target_pairs={{0,3},{1,2},{2,1},{3,0},{4,7},{5,6},{6,5},{7,4},{8,11},{9,10},{10,... | collective-permute-start | bytes 1572872 | tf_op jit(solution)/shard_map/ppermute | solution.py:154
  75.8 4.6 %heads.1.tail = bf16[320,128]{1,0:T(8,128)(2,1)S(1)} custom-call(s32[2,2]{1,0:T(2,128)S(1)} %copy-done.13, bf16[2,64,4096]{2,1,0:T(8,128)(2,1)S(1)} %bitcast.21, bf16[2,64,4096]{2,1,0:T(8,128)(2,1)S(1)} %bitcast.18, bf16[2,2,4096,128]{3,2,1,0:T(8,128)(2,1)S(1)} %bitcast.16, bf16[2,64,128]{2,1,0:T(8,128)(2,1)S(1)} %bitcast.22, bf16[2,64,128]{2,1,0:T(8,128)(2,1)S(1)} %bitcast.23), custom_call_target="tpu_custom_call" | custom-call | tf_op jit(solution)/shard_map/heads/pallas_call | solution.py:495
  80.6 1.3 %collective-permute-start.5 = (bf16[576,128]{1,0:T(8,128)(2,1)S(1)}, bf16[576,128]{1,0:T(8,128)(2,1)S(1)}, u32[]{:S(2)}, u32[]{:S(2)}) collective-permute-start(bf16[576,128]{1,0:T(8,128)(2,1)S(1)} %get-tuple-element.28), channel_id=1, source_target_pairs={{0,2},{1,3},{2,0},{3,1},{4,6},{5,7},{6,4},{7,5},{8,10},{9,11},{10,... | collective-permute-start | bytes 442376 | tf_op jit(solution)/shard_map/ppermute | solution.py:154
  81.8 3.1 %collective-permute-done.24.refs_16_ = bf16[4,64,1024]{2,1,0:T(8,128)(2,1)S(1)} collective-permute-done((bf16[4,64,1024]{2,1,0:T(8,128)(2,1)S(1)}, bf16[4,64,1024]{2,1,0:T(8,128)(2,1)S(1)}, u32[]{:S(2)}, u32[]{:S(2)}) %collective-permute-start.24) | collective-permute-done | bytes 524320 | tf_op jit(solution)/shard_map/ppermute | solution.py:154
  84.9 1.7 %collective-permute-start.6 = (bf16[704,128]{1,0:T(8,128)(2,1)S(1)}, bf16[704,128]{1,0:T(8,128)(2,1)S(1)}, u32[]{:S(2)}, u32[]{:S(2)}) collective-permute-start(bf16[704,128]{1,0:T(8,128)(2,1)S(1)} %get-tuple-element.27.refs_0_), channel_id=1, source_target_pairs={{0,3},{1,2},{2,1},{3,0},{4,7},{5,6},{6,5},{7,4},{8,11},{9,10},{10,... | collective-permute-start | bytes 540680 | tf_op jit(solution)/shard_map/ppermute | solution.py:154
  89.0 1.7 %collective-permute-done.6.refs_3_ = bf16[704,128]{1,0:T(8,128)(2,1)S(1)} collective-permute-done((bf16[704,128]{1,0:T(8,128)(2,1)S(1)}, bf16[704,128]{1,0:T(8,128)(2,1)S(1)}, u32[]{:S(2)}, u32[]{:S(2)}) %collective-permute-start.6) | collective-permute-done | bytes 180256 | tf_op jit(solution)/shard_map/ppermute | solution.py:154
  90.6 2.2 %collective-permute-start.25 = (bf16[4,64,1024]{2,1,0:T(8,128)(2,1)S(1)}, bf16[4,64,1024]{2,1,0:T(8,128)(2,1)S(1)}, u32[]{:S(2)}, u32[]{:S(2)}) collective-permute-start(bf16[4,64,1024]{2,1,0:T(8,128)(2,1)S(1)} %collective-permute-done.24.refs_16_), channel_id=1, source_target_pairs={{0,4},{4,0},{8,12},{12,8},{16,20},{20,16},{24,28},{28,24},{1,5},{5... | collective-permute-start | bytes 1572872 | tf_op jit(solution)/shard_map/ppermute | solution.py:154
  92.8 2.2 %chain.1 = (bf16[2,5,64,128]{3,2,1,0:T(8,128)(2,1)S(1)}, bf16[128,384]{1,0:T(8,128)(2,1)S(1)}, bf16[2,64,128]{2,1,0:T(8,128)(2,1)S(1)}) custom-call(s32[5]{0:T(128)S(1)} %stack.23.place, bf16[704,128]{1,0:T(8,128)(2,1)S(1)} %get-tuple-element.27.refs_0_, bf16[576,128]{1,0:T(8,128)(2,1)S(1)} %collective-permute-done.4.refs_1_, ...), custom_call_target="tpu_custom_call" | custom-call | tf_op jit(solution)/shard_map/chain/pallas_call | solution.py:574
  95.0 1.6 %collective-permute-start.30 = (bf16[2,5,64,128]{3,2,1,0:T(8,128)(2,1)S(1)}, bf16[2,5,64,128]{3,2,1,0:T(8,128)(2,1)S(1)}, u32[]{:S(2)}, u32[]{:S(2)}) collective-permute-start(bf16[2,5,64,128]{3,2,1,0:T(8,128)(2,1)S(1)} %get-tuple-element.42.refs_22_), channel_id=1, source_target_pairs={{0,8},{4,12},{8,16},{12,20},{16,24},{20,28},{24,0},{28,4},{1,9},{5... | collective-permute-start | bytes 491528 | tf_op jit(solution)/shard_map/ppermute | solution.py:159
  97.3 1.4 %collective-permute-start.32 = (bf16[2,5,64,128]{3,2,1,0:T(8,128)(2,1)S(1)}, bf16[2,5,64,128]{3,2,1,0:T(8,128)(2,1)S(1)}, u32[]{:S(2)}, u32[]{:S(2)}) collective-permute-start(bf16[2,5,64,128]{3,2,1,0:T(8,128)(2,1)S(1)} %get-tuple-element.42.refs_22_), channel_id=1, source_target_pairs={{0,24},{4,28},{8,0},{12,4},{16,8},{20,12},{24,16},{28,20},{1,25},{... | collective-permute-start | bytes 491528 | tf_op jit(solution)/shard_map/ppermute | solution.py:159
  99.5 1.3 %collective-permute-done.30.refs_23_ = bf16[2,5,64,128]{3,2,1,0:T(8,128)(2,1)S(1)} collective-permute-done((bf16[2,5,64,128]{3,2,1,0:T(8,128)(2,1)S(1)}, bf16[2,5,64,128]{3,2,1,0:T(8,128)(2,1)S(1)}, u32[]{:S(2)}, u32[]{:S(2)}) %collective-permute-start.30) | collective-permute-done | bytes 163872 | tf_op jit(solution)/shard_map/ppermute | solution.py:159
  100.8 7.6 %collective-permute-start.34 = (bf16[2,5,64,128]{3,2,1,0:T(8,128)(2,1)S(1)}, bf16[2,5,64,128]{3,2,1,0:T(8,128)(2,1)S(1)}, u32[]{:S(2)}, u32[]{:S(2)}) collective-permute-start(bf16[2,5,64,128]{3,2,1,0:T(8,128)(2,1)S(1)} %collective-permute-done.30.refs_23_), channel_id=1, source_target_pairs={{0,4},{4,0},{8,12},{12,8},{16,20},{20,16},{24,28},{28,24},{1,5},{5... | collective-permute-start | bytes 491528 | tf_op jit(solution)/shard_map/ppermute | solution.py:154
  108.4 2.3 %collective-permute-done.31.refs_24_ = bf16[2,5,64,128]{3,2,1,0:T(8,128)(2,1)S(1)} collective-permute-done((bf16[2,5,64,128]{3,2,1,0:T(8,128)(2,1)S(1)}, bf16[2,5,64,128]{3,2,1,0:T(8,128)(2,1)S(1)}, u32[]{:S(2)}, u32[]{:S(2)}) %collective-permute-start.31) | collective-permute-done | bytes 163872 | tf_op jit(solution)/shard_map/ppermute | solution.py:159
  112.9 3.7 %input_side.1 = bf16[2,64,4096]{2,1,0:T(8,128)(2,1)} custom-call(s32[5]{0:T(128)S(1)} %stack.23.place, bf16[2,64,4096]{2,1,0:T(8,128)(2,1)S(1)} %bitcast.19, bf16[128,384]{1,0:T(8,128)(2,1)S(1)} %get-tuple-element.29.steer, bf16[2,64,128]{2,1,0:T(8,128)(2,1)S(1)} %get-tuple-element.30.own, bf16[2,4096,128]{2,1,0:T(8,128)(2,1)S(1)} %get-tuple-element.31.held, ...), custom_call_target="tpu_custom_call" | custom-call | tf_op jit(solution)/shard_map/input_side/pallas_call | solution.py:594
  116.6 4.0 %weight_side.1 = f32[2,512,128]{2,1,0:T(8,128)} custom-call(s32[5]{0:T(128)S(1)} %stack.23.place, bf16[2,64,1024]{2,1,0:T(8,128)(2,1)S(1)} %get-tuple-element.32.refs_0_, bf16[2,64,1024]{2,1,0:T(8,128)(2,1)S(1)} %collective-permute-done.10.refs_1_, bf16[2,64,1024]{2,1,0:T(8,128)(2,1)S(1)} %collective-permute-done.11.refs_2_, ...), custom_call_target="tpu_custom_call" | custom-call | tf_op jit(solution)/shard_map/weight_side/pallas_call | solution.py:612
  (86 shorter events, 20.8 us)
Async XLA Ops:
  3.6 9.8 %collective-permute-start.17 = (bf16[2,64,512]{2,1,0:T(8,128)(2,1)S(1)}, bf16[2,64,512]{2,1,0:T(8,128)(2,1)S(1)}, u32[]{:S(2)}, u32[]{:S(2)}) collective-permute-start(bf16[2,64,512]{2,1,0:T(8,128)(2,1)S(1)} %get-tuple-element.37), channel_id=1, source_target_pairs={{0,8},{4,12},{8,16},{12,20},{16,24},{20,28},{24,0},{28,4},{1,9},{5... | collective-permute-start | bytes 393224 | tf_op jit(solution)/shard_map/ppermute | solution.py:159
  5.0 10.6 %collective-permute-start.18 = (bf16[2,64,512]{2,1,0:T(8,128)(2,1)S(1)}, bf16[2,64,512]{2,1,0:T(8,128)(2,1)}, u32[]{:S(2)}, u32[]{:S(2)}) collective-permute-start(bf16[2,64,512]{2,1,0:T(8,128)(2,1)S(1)} %get-tuple-element.38), channel_id=1, source_target_pairs={{0,16},{4,20},{8,24},{12,28},{16,0},{20,4},{24,8},{28,12},{1,17},{... | collective-permute-start | bytes 393224 | tf_op jit(solution)/shard_map/ppermute | solution.py:159
  6.1 23.3 %collective-permute-start.19 = (bf16[2,64,512]{2,1,0:T(8,128)(2,1)S(1)}, bf16[2,64,512]{2,1,0:T(8,128)(2,1)S(1)}, u32[]{:S(2)}, u32[]{:S(2)}) collective-permute-start(bf16[2,64,512]{2,1,0:T(8,128)(2,1)S(1)} %get-tuple-element.39), channel_id=1, source_target_pairs={{0,24},{4,28},{8,0},{12,4},{16,8},{20,12},{24,16},{28,20},{1,25},{... | collective-permute-start | bytes 393224 | tf_op jit(solution)/shard_map/ppermute | solution.py:159
  7.4 22.6 %collective-permute-start.20 = (bf16[2,64,512]{2,1,0:T(8,128)(2,1)S(1)}, bf16[2,64,512]{2,1,0:T(8,128)(2,1)S(1)}, u32[]{:S(2)}, u32[]{:S(2)}) collective-permute-start(bf16[2,64,512]{2,1,0:T(8,128)(2,1)S(1)} %get-tuple-element.36.refs_0_.refs_8_), channel_id=1, source_target_pairs={{0,4},{4,0},{8,12},{12,8},{16,20},{20,16},{24,28},{28,24},{1,5},{5... | collective-permute-start | bytes 393224 | tf_op jit(solution)/shard_map/ppermute | solution.py:154
  12.1 19.9 %collective-permute-start.37 = (bf16[512,128]{1,0:T(8,128)(2,1)S(1)}, bf16[512,128]{1,0:T(8,128)(2,1)S(1)}, u32[]{:S(2)}, u32[]{:S(2)}) collective-permute-start(bf16[512,128]{1,0:T(8,128)(2,1)S(1)} %get-tuple-element.43.refs_30_.refs_36_), channel_id=1, source_target_pairs={{1,0},{5,4},{9,8},{13,12},{17,16},{21,20},{25,24},{29,28}} | collective-permute-start | bytes 393224 | tf_op jit(solution)/shard_map/ppermute | solution.py:572
  13.4 23.5 %collective-permute-start.10 = (bf16[2,64,1024]{2,1,0:T(8,128)(2,1)}, bf16[2,64,1024]{2,1,0:T(8,128)(2,1)S(1)}, u32[]{:S(2)}, u32[]{:S(2)}) collective-permute-start(bf16[2,64,1024]{2,1,0:T(8,128)(2,1)} %get-tuple-element.33), channel_id=1, source_target_pairs={{0,8},{4,12},{8,16},{12,20},{16,24},{20,28},{24,0},{28,4},{1,9},{5... | collective-permute-start | bytes 786440 | tf_op jit(solution)/shard_map/ppermute | solution.py:159
  15.6 23.0 %collective-permute-start.11 = (bf16[2,64,1024]{2,1,0:T(8,128)(2,1)}, bf16[2,64,1024]{2,1,0:T(8,128)(2,1)S(1)}, u32[]{:S(2)}, u32[]{:S(2)}) collective-permute-start(bf16[2,64,1024]{2,1,0:T(8,128)(2,1)} %get-tuple-element.34), channel_id=1, source_target_pairs={{0,16},{4,20},{8,24},{12,28},{16,0},{20,4},{24,8},{28,12},{1,17},{... | collective-permute-start | bytes 786440 | tf_op jit(solution)/shard_map/ppermute | solution.py:159
  30.0 10.9 %collective-permute-start.12 = (bf16[2,64,1024]{2,1,0:T(8,128)(2,1)}, bf16[2,64,1024]{2,1,0:T(8,128)(2,1)S(1)}, u32[]{:S(2)}, u32[]{:S(2)}) collective-permute-start(bf16[2,64,1024]{2,1,0:T(8,128)(2,1)} %get-tuple-element.35), channel_id=1, source_target_pairs={{0,24},{4,28},{8,0},{12,4},{16,8},{20,12},{24,16},{28,20},{1,25},{... | collective-permute-start | bytes 786440 | tf_op jit(solution)/shard_map/ppermute | solution.py:159
  30.7 6.3 %collective-permute-start.38 = (bf16[512,128]{1,0:T(8,128)(2,1)S(1)}, bf16[512,128]{1,0:T(8,128)(2,1)}, u32[]{:S(2)}, u32[]{:S(2)}) collective-permute-start(bf16[512,128]{1,0:T(8,128)(2,1)S(1)} %get-tuple-element.43.refs_30_.refs_36_), channel_id=1, source_target_pairs={{2,0},{6,4},{10,8},{14,12},{18,16},{22,20},{26,24},{30,28}} | collective-permute-start | bytes 393224 | tf_op jit(solution)/shard_map/ppermute | solution.py:572
  32.6 10.4 %collective-permute-start.13 = (bf16[2,64,1024]{2,1,0:T(8,128)(2,1)S(1)}, bf16[2,64,1024]{2,1,0:T(8,128)(2,1)}, u32[]{:S(2)}, u32[]{:S(2)}) collective-permute-start(bf16[2,64,1024]{2,1,0:T(8,128)(2,1)S(1)} %get-tuple-element.32.refs_0_), channel_id=1, source_target_pairs={{0,4},{4,0},{8,12},{12,8},{16,20},{20,16},{24,28},{28,24},{1,5},{5... | collective-permute-start | bytes 786440 | tf_op jit(solution)/shard_map/ppermute | solution.py:154
  36.9 33.5 %collective-permute-start = (bf16[4,512,128]{2,1,0:T(8,128)(2,1)S(1)}, bf16[4,512,128]{2,1,0:T(8,128)(2,1)S(1)}, u32[]{:S(2)}, u32[]{:S(2)}) collective-permute-start(bf16[4,512,128]{2,1,0:T(8,128)(2,1)S(1)} %get-tuple-element.24), channel_id=1, source_target_pairs={{0,1},{1,0},{2,3},{3,2},{4,5},{5,4},{6,7},{7,6},{8,9},{9,8},{10,11... | collective-permute-start | bytes 1572872 | tf_op jit(solution)/shard_map/ppermute | solution.py:154
  37.0 9.1 %collective-permute-start.21 = (bf16[2,64,512]{2,1,0:T(8,128)(2,1)S(1)}, bf16[2,64,512]{2,1,0:T(8,128)(2,1)S(1)}, u32[]{:S(2)}, u32[]{:S(2)}) collective-permute-start(bf16[2,64,512]{2,1,0:T(8,128)(2,1)S(1)} %collective-permute-done.17.refs_1_.refs_9_), channel_id=1, source_target_pairs={{0,4},{4,0},{8,12},{12,8},{16,20},{20,16},{24,28},{28,24},{1,5},{5... | collective-permute-start | bytes 393224 | tf_op jit(solution)/shard_map/ppermute | solution.py:154
  38.6 33.7 %collective-permute-start.1 = (bf16[4,512,128]{2,1,0:T(8,128)(2,1)S(1)}, bf16[4,512,128]{2,1,0:T(8,128)(2,1)S(1)}, u32[]{:S(2)}, u32[]{:S(2)}) collective-permute-start(bf16[4,512,128]{2,1,0:T(8,128)(2,1)S(1)} %get-tuple-element.25), channel_id=1, source_target_pairs={{0,2},{1,3},{2,0},{3,1},{4,6},{5,7},{6,4},{7,5},{8,10},{9,11},{10,... | collective-permute-start | bytes 1572872 | tf_op jit(solution)/shard_map/ppermute | solution.py:154
  40.9 31.7 %collective-permute-start.2 = (bf16[4,512,128]{2,1,0:T(8,128)(2,1)S(1)}, bf16[4,512,128]{2,1,0:T(8,128)(2,1)S(1)}, u32[]{:S(2)}, u32[]{:S(2)}) collective-permute-start(bf16[4,512,128]{2,1,0:T(8,128)(2,1)S(1)} %get-tuple-element.26), channel_id=1, source_target_pairs={{0,3},{1,2},{2,1},{3,0},{4,7},{5,6},{6,5},{7,4},{8,11},{9,10},{10,... | collective-permute-start | bytes 1572872 | tf_op jit(solution)/shard_map/ppermute | solution.py:154
  46.0 21.8 %collective-permute-start.26 = (bf16[4,64,512]{2,1,0:T(8,128)(2,1)S(1)}, bf16[4,64,512]{2,1,0:T(8,128)(2,1)S(1)}, u32[]{:S(2)}, u32[]{:S(2)}) collective-permute-start(bf16[4,64,512]{2,1,0:T(8,128)(2,1)S(1)} %get-tuple-element.40), channel_id=1, source_target_pairs={{0,2},{1,3},{2,0},{3,1},{4,6},{5,7},{6,4},{7,5},{8,10},{9,11},{10,... | collective-permute-start | bytes 786440 | tf_op jit(solution)/shard_map/ppermute | solution.py:154
  48.1 25.8 %collective-permute-start.27 = (bf16[4,64,512]{2,1,0:T(8,128)(2,1)S(1)}, bf16[4,64,512]{2,1,0:T(8,128)(2,1)S(1)}, u32[]{:S(2)}, u32[]{:S(2)}) collective-permute-start(bf16[4,64,512]{2,1,0:T(8,128)(2,1)S(1)} %get-tuple-element.41), channel_id=1, source_target_pairs={{0,1},{1,0},{2,3},{3,2},{4,5},{5,4},{6,7},{7,6},{8,9},{9,8},{10,11... | collective-permute-start | bytes 786440 | tf_op jit(solution)/shard_map/ppermute | solution.py:154
  67.8 6.5 %collective-permute-start.14 = (bf16[2,64,1024]{2,1,0:T(8,128)(2,1)S(1)}, bf16[2,64,1024]{2,1,0:T(8,128)(2,1)S(1)}, u32[]{:S(2)}, u32[]{:S(2)}) collective-permute-start(bf16[2,64,1024]{2,1,0:T(8,128)(2,1)S(1)} %collective-permute-done.10.refs_1_), channel_id=1, source_target_pairs={{0,4},{4,0},{8,12},{12,8},{16,20},{20,16},{24,28},{28,24},{1,5},{5... | collective-permute-start | bytes 786440 | tf_op jit(solution)/shard_map/ppermute | solution.py:154
  70.5 14.4 %collective-permute-start.24 = (bf16[4,64,1024]{2,1,0:T(8,128)(2,1)S(1)}, bf16[4,64,1024]{2,1,0:T(8,128)(2,1)S(1)}, u32[]{:S(2)}, u32[]{:S(2)}) collective-permute-start(bf16[4,64,1024]{2,1,0:T(8,128)(2,1)S(1)} %pick_moving.2), channel_id=1, source_target_pairs={{0,3},{1,2},{2,1},{3,0},{4,7},{5,6},{6,5},{7,4},{8,11},{9,10},{10,... | collective-permute-start | bytes 1572872 | tf_op jit(solution)/shard_map/ppermute | solution.py:154
  72.6 7.9 %collective-permute-start.16 = (bf16[2,64,1024]{2,1,0:T(8,128)(2,1)S(1)}, bf16[2,64,1024]{2,1,0:T(8,128)(2,1)S(1)}, u32[]{:S(2)}, u32[]{:S(2)}) collective-permute-start(bf16[2,64,1024]{2,1,0:T(8,128)(2,1)S(1)} %collective-permute-done.12.refs_3_), channel_id=1, source_target_pairs={{0,4},{4,0},{8,12},{12,8},{16,20},{20,16},{24,28},{28,24},{1,5},{5... | collective-permute-start | bytes 786440 | tf_op jit(solution)/shard_map/ppermute | solution.py:154
  74.3 6.2 %collective-permute-start.28 = (bf16[4,64,512]{2,1,0:T(8,128)(2,1)S(1)}, bf16[4,64,512]{2,1,0:T(8,128)(2,1)S(1)}, u32[]{:S(2)}, u32[]{:S(2)}) collective-permute-start(bf16[4,64,512]{2,1,0:T(8,128)(2,1)S(1)} %collective-permute-done.26.refs_18_), channel_id=1, source_target_pairs={{0,4},{4,0},{8,12},{12,8},{16,20},{20,16},{24,28},{28,24},{1,5},{5... | collective-permute-start | bytes 786440 | tf_op jit(solution)/shard_map/ppermute | solution.py:154
  74.5 22.1 %collective-permute-start.7 = (bf16[4,512,128]{2,1,0:T(8,128)(2,1)S(1)}, bf16[4,512,128]{2,1,0:T(8,128)(2,1)S(1)}, u32[]{:S(2)}, u32[]{:S(2)}) collective-permute-start(bf16[4,512,128]{2,1,0:T(8,128)(2,1)S(1)} %collective-permute-done.refs_0_.refs_31_), channel_id=1, source_target_pairs={{0,4},{4,0},{8,12},{12,8},{16,20},{20,16},{24,28},{28,24},{1,5},{5... | collective-permute-start | bytes 1572872 | tf_op jit(solution)/shard_map/ppermute | solution.py:154
  75.5 21.8 %collective-permute-start.8 = (bf16[4,512,128]{2,1,0:T(8,128)(2,1)S(1)}, bf16[4,512,128]{2,1,0:T(8,128)(2,1)S(1)}, u32[]{:S(2)}, u32[]{:S(2)}) collective-permute-start(bf16[4,512,128]{2,1,0:T(8,128)(2,1)S(1)} %collective-permute-done.1.refs_1_.refs_32_), channel_id=1, source_target_pairs={{0,4},{4,0},{8,12},{12,8},{16,20},{20,16},{24,28},{28,24},{1,5},{5... | collective-permute-start | bytes 1572872 | tf_op jit(solution)/shard_map/ppermute | solution.py:154
  80.5 7.0 %collective-permute-start.4 = (bf16[576,128]{1,0:T(8,128)(2,1)S(1)}, bf16[576,128]{1,0:T(8,128)(2,1)S(1)}, u32[]{:S(2)}, u32[]{:S(2)}) collective-permute-start(bf16[576,128]{1,0:T(8,128)(2,1)S(1)} %get-tuple-element.28), channel_id=1, source_target_pairs={{0,1},{1,0},{2,3},{3,2},{4,5},{5,4},{6,7},{7,6},{8,9},{9,8},{10,11... | collective-permute-start | bytes 442376 | tf_op jit(solution)/shard_map/ppermute | solution.py:154
  80.6 7.9 %collective-permute-start.5 = (bf16[576,128]{1,0:T(8,128)(2,1)S(1)}, bf16[576,128]{1,0:T(8,128)(2,1)S(1)}, u32[]{:S(2)}, u32[]{:S(2)}) collective-permute-start(bf16[576,128]{1,0:T(8,128)(2,1)S(1)} %get-tuple-element.28), channel_id=1, source_target_pairs={{0,2},{1,3},{2,0},{3,1},{4,6},{5,7},{6,4},{7,5},{8,10},{9,11},{10,... | collective-permute-start | bytes 442376 | tf_op jit(solution)/shard_map/ppermute | solution.py:154
  87.5 11.2 %collective-permute-start.9 = (bf16[4,512,128]{2,1,0:T(8,128)(2,1)S(1)}, bf16[4,512,128]{2,1,0:T(8,128)(2,1)S(1)}, u32[]{:S(2)}, u32[]{:S(2)}) collective-permute-start(bf16[4,512,128]{2,1,0:T(8,128)(2,1)S(1)} %collective-permute-done.2.refs_2_.refs_33_), channel_id=1, source_target_pairs={{0,4},{4,0},{8,12},{12,8},{16,20},{20,16},{24,28},{28,24},{1,5},{5... | collective-permute-start | bytes 1572872 | tf_op jit(solution)/shard_map/ppermute | solution.py:154
  88.5 6.5 %collective-permute-start.29 = (bf16[4,64,512]{2,1,0:T(8,128)(2,1)S(1)}, bf16[4,64,512]{2,1,0:T(8,128)(2,1)S(1)}, u32[]{:S(2)}, u32[]{:S(2)}) collective-permute-start(bf16[4,64,512]{2,1,0:T(8,128)(2,1)S(1)} %collective-permute-done.27.refs_19_), channel_id=1, source_target_pairs={{0,4},{4,0},{8,12},{12,8},{16,20},{20,16},{24,28},{28,24},{1,5},{5... | collective-permute-start | bytes 786440 | tf_op jit(solution)/shard_map/ppermute | solution.py:154
  90.6 25.9 %collective-permute-start.25 = (bf16[4,64,1024]{2,1,0:T(8,128)(2,1)S(1)}, bf16[4,64,1024]{2,1,0:T(8,128)(2,1)S(1)}, u32[]{:S(2)}, u32[]{:S(2)}) collective-permute-start(bf16[4,64,1024]{2,1,0:T(8,128)(2,1)S(1)} %collective-permute-done.24.refs_16_), channel_id=1, source_target_pairs={{0,4},{4,0},{8,12},{12,8},{16,20},{20,16},{24,28},{28,24},{1,5},{5... | collective-permute-start | bytes 1572872 | tf_op jit(solution)/shard_map/ppermute | solution.py:154
  96.6 14.1 %collective-permute-start.31 = (bf16[2,5,64,128]{3,2,1,0:T(8,128)(2,1)S(1)}, bf16[2,5,64,128]{3,2,1,0:T(8,128)(2,1)S(1)}, u32[]{:S(2)}, u32[]{:S(2)}) collective-permute-start(bf16[2,5,64,128]{3,2,1,0:T(8,128)(2,1)S(1)} %get-tuple-element.42.refs_22_), channel_id=1, source_target_pairs={{0,16},{4,20},{8,24},{12,28},{16,0},{20,4},{24,8},{28,12},{1,17},{... | collective-permute-start | bytes 491528 | tf_op jit(solution)/shard_map/ppermute | solution.py:159
  97.3 15.1 %collective-permute-start.32 = (bf16[2,5,64,128]{3,2,1,0:T(8,128)(2,1)S(1)}, bf16[2,5,64,128]{3,2,1,0:T(8,128)(2,1)S(1)}, u32[]{:S(2)}, u32[]{:S(2)}) collective-permute-start(bf16[2,5,64,128]{3,2,1,0:T(8,128)(2,1)S(1)} %get-tuple-element.42.refs_22_), channel_id=1, source_target_pairs={{0,24},{4,28},{8,0},{12,4},{16,8},{20,12},{24,16},{28,20},{1,25},{... | collective-permute-start | bytes 491528 | tf_op jit(solution)/shard_map/ppermute | solution.py:159
  98.7 17.9 %collective-permute-start.33 = (bf16[2,5,64,128]{3,2,1,0:T(8,128)(2,1)S(1)}, bf16[2,5,64,128]{3,2,1,0:T(8,128)(2,1)S(1)}, u32[]{:S(2)}, u32[]{:S(2)}) collective-permute-start(bf16[2,5,64,128]{3,2,1,0:T(8,128)(2,1)S(1)} %get-tuple-element.42.refs_22_), channel_id=1, source_target_pairs={{0,4},{4,0},{8,12},{12,8},{16,20},{20,16},{24,28},{28,24},{1,5},{5... | collective-permute-start | bytes 491528 | tf_op jit(solution)/shard_map/ppermute | solution.py:154
  100.8 15.8 %collective-permute-start.34 = (bf16[2,5,64,128]{3,2,1,0:T(8,128)(2,1)S(1)}, bf16[2,5,64,128]{3,2,1,0:T(8,128)(2,1)S(1)}, u32[]{:S(2)}, u32[]{:S(2)}) collective-permute-start(bf16[2,5,64,128]{3,2,1,0:T(8,128)(2,1)S(1)} %collective-permute-done.30.refs_23_), channel_id=1, source_target_pairs={{0,4},{4,0},{8,12},{12,8},{16,20},{20,16},{24,28},{28,24},{1,5},{5... | collective-permute-start | bytes 491528 | tf_op jit(solution)/shard_map/ppermute | solution.py:154
  110.7 5.9 %collective-permute-start.35 = (bf16[2,5,64,128]{3,2,1,0:T(8,128)(2,1)S(1)}, bf16[2,5,64,128]{3,2,1,0:T(8,128)(2,1)S(1)}, u32[]{:S(2)}, u32[]{:S(2)}) collective-permute-start(bf16[2,5,64,128]{3,2,1,0:T(8,128)(2,1)S(1)} %collective-permute-done.31.refs_24_), channel_id=1, source_target_pairs={{0,4},{4,0},{8,12},{12,8},{16,20},{20,16},{24,28},{28,24},{1,5},{5... | collective-permute-start | bytes 491528 | tf_op jit(solution)/shard_map/ppermute | solution.py:154
  (21 other events, 373.0 us)

commit v3 on v2

--- a/solution.py
+++ b/solution.py
@@ -165,7 +165,7 @@
     )
 
 
-def heads_kernel(length, valid, inputs, cot, held, queries, key_vectors, out, sums):
+def heads_kernel(length, valid, inputs, cot, held, queries, key_vectors, short, out, sums):
     tokens, head = queries.shape[1:]
     for way in range(2):
         for which, source in enumerate((inputs, cot)):
@@ -202,22 +202,17 @@
             out[2 * tokens : 3 * tokens, way * tokens : (way + 1) * tokens] = attend
             rows = slice((3 + way) * tokens, (4 + way) * tokens)
             out[rows, :] = mixture.astype(jnp.bfloat16)
-
-
-def pack_kernel(near, far, tail, short, full):
-    head = near.shape[-1]
-    rows = near.shape[0] * head
-    total = (near[...] + far[...]).astype(jnp.bfloat16).reshape(rows, head)
-    short[:rows, :] = total
-    full[:rows, :] = total
-    short[rows:, :] = tail[: short.shape[0] - rows, :]
-    full[rows:, :] = tail[...]
-
-
-def chain_kernel(sections, tokens, head, place, *refs):
-    parts = refs[:sections]
-    gathered, steer, own = refs[sections:]
-    products = (sections - 1) * head
+        short[...] = out[: 3 * tokens, :]
+
+
+def pack_kernel(near, far, out):
+    out[...] = (near[...] + far[...]).astype(jnp.bfloat16)
+
+
+def chain_kernel(sections, tokens, head, *refs):
+    place = position()
+    parts, tails = refs[:sections], refs[sections : 2 * sections]
+    gathered, steer, own = refs[2 * sections :]
 
     def at(here):
         mine = [[None] * sections, [None] * sections]
@@ -225,16 +220,11 @@
             order = range(sections - 1, -1, -1) if way == 0 else range(sections)
             done = []
             for holder in order:
-                part = parts[here ^ holder]
-                first = products + way * tokens
-                total = part[first : first + tokens, :].astype(jnp.float32)
+                part, tail = parts[here ^ holder], tails[here ^ holder]
+                total = tail[way * tokens : (way + 1) * tokens, :].astype(jnp.float32)
                 for other in done:
-                    block = (other ^ holder) - 1
-                    total += contract(
-                        mine[way][other], part[block * head : (block + 1) * head, :], 1, 0
-                    )
-                base = products + 2 * tokens
-                weights = part[base : base + tokens, way * tokens : (way + 1) * tokens]
+                    total += contract(mine[way][other], part[(other ^ holder) - 1], 1, 0)
+                weights = tail[2 * tokens : 3 * tokens, way * tokens : (way + 1) * tokens]
                 mine[way][holder] = contract(weights, total.astype(jnp.bfloat16), 0, 0).astype(
                     jnp.bfloat16
                 )
@@ -245,9 +235,8 @@
             gathered[0, far] = mine[0][here + far] if inside else zero
             gathered[1, far] = mine[1][sections - 1 - here - far] if inside else zero
         mirror = here ^ (sections - 1)
-        base = products + 2 * tokens + tokens
-        gathered[0, sections] = parts[0][base : base + tokens, :]
-        gathered[1, sections] = parts[here ^ mirror][base + tokens : base + 2 * tokens, :]
+        gathered[0, sections] = tails[0][3 * tokens : 4 * tokens, :]
+        gathered[1, sections] = tails[here ^ mirror][4 * tokens : 5 * tokens, :]
         for way in range(2):
             own[way] = mine[way][here]
         for mask in range(1, sections):
@@ -264,7 +253,8 @@
             at(here)
 
 
-def input_kernel(sections, tokens, place, cot, steer, own, held, *refs):
+def input_kernel(sections, tokens, cot, steer, own, held, *refs):
+    place = position()
     near, far = refs[: sections - 1], refs[sections - 1 : 2 * sections - 2]
     out = refs[2 * sections - 2]
     width = near[0].shape[1]
@@ -280,7 +270,8 @@
             out[way, :, pl.ds(start, width)] = (base + branch).astype(jnp.bfloat16)
 
 
-def pick_weights(sections, place, halved, *refs):
+def pick_weights(sections, halved, *refs):
+    place = position()
     outs, sems = refs[: sections - 1], refs[sections - 1]
     here, core = place[0], place[1]
     copies = []
@@ -295,6 +286,13 @@
         copy.wait()
 
 
+def position():
+    here, replica = lax.axis_index("section"), lax.axis_index("dp")
+    asides = (lax.axis_size("section") // 2, 1)
+    bits = [jnp.where((here & aside) != 0, 1, 0) for aside in asides]
+    return (here, lax.rem(replica, 2), lax.div(replica, 2), *bits)
+
+
 def carried_out(copies):
     for copy in copies:
         copy.start()
@@ -302,7 +300,8 @@
         copy.wait()
 
 
-def pick_outputs(place, halved, whole, out, own, part, sems):
+def pick_outputs(halved, whole, out, own, part, sems):
+    place = position()
     carried_out(
         [
             pltpu.make_async_copy(halved.at[1, 0, place[2], place[1]], part, sems.at[2]),
@@ -312,7 +311,8 @@
     )
 
 
-def pick_columns(steps, width, place, inputs, cot, *refs):
+def pick_columns(steps, width, inputs, cot, *refs):
+    place = position()
     outs, halves, sems = refs[:steps], refs[steps : 2 * steps], refs[2 * steps]
     copies = []
     for distance in range(steps):
@@ -345,7 +345,8 @@
     carried_out(copies)
 
 
-def product_kernel(sections, steps, place, outputs, *refs):
+def product_kernel(sections, steps, outputs, *refs):
+    place = position()
     fetched, out = refs[: sections - 1], refs[sections - 1]
     for mask in range(1, sections):
         way = jnp.where((place[0] ^ mask) > place[0], 0, 1)
@@ -356,7 +357,8 @@
         out[mask - 1] = total
 
 
-def weight_kernel(sections, steps, tokens, place, *refs):
+def weight_kernel(sections, steps, tokens, *refs):
+    place = position()
     columns = refs[: 2 * steps]
     halves, refs = refs[2 * steps : 4 * steps], refs[2 * steps :]
     mirrored, lent = refs[2 * steps : 2 * steps + 2], refs[2 * steps + 2 : 2 * steps + 6]
@@ -420,9 +422,6 @@
     sections = lax.axis_size("section")
     replicas = lax.axis_size("dp")
     steps = replicas // 2
-    here = lax.axis_index("section")
-    core = lax.axis_index("dp") % 2
-    depth = lax.axis_index("dp") // 2
     inputs = layer_inputs[0]
     held = held_weights[0]
     seqs, length, model_width = inputs.shape[1:]
@@ -433,7 +432,6 @@
     cot = cotangent.reshape(2, tokens, model_width)
     halved = held.reshape(2, 2, steps, 2, width, head)
     asides = (sections // 2, 1)
-    place = jnp.stack([here, core, depth] + [jnp.where(here & aside, 1, 0) for aside in asides])
     memory = pl.BlockSpec(memory_space=pltpu.VMEM)
     scalars = pl.BlockSpec(memory_space=pltpu.SMEM)
     anywhere = pl.BlockSpec(memory_space=pl.ANY)
@@ -441,13 +439,13 @@
 
     picked = pl.pallas_call(
         functools.partial(pick_weights, sections),
-        in_specs=[scalars, hbm],
+        in_specs=[hbm],
         out_specs=[memory] * (sections - 1),
         out_shape=[jax.ShapeDtypeStruct((steps, width, head), jnp.bfloat16)] * (sections - 1),
         scratch_shapes=[pltpu.SemaphoreType.DMA((sections - 1,))],
         name="pick_weights",
         compiler_params=pltpu.CompilerParams(vmem_limit_bytes=52 << 20),
-    )(place, halved)
+    )(halved)
     fetched = [None] * sections
     for mask in range(sections - 1, 0, -1):
         fetched[mask] = swapped(picked[mask - 1], "section", mask)
@@ -456,13 +454,13 @@
     slim = jax.ShapeDtypeStruct((2, tokens, width), jnp.bfloat16)
     picked = pl.pallas_call(
         functools.partial(pick_columns, steps, width),
-        in_specs=[scalars] + [hbm] * 2,
+        in_specs=[hbm] * 2,
         out_specs=[memory] * (2 * steps),
         out_shape=[wide] * steps + [slim] * steps,
         scratch_shapes=[pltpu.SemaphoreType.DMA((3 * steps,))],
         name="pick_columns",
         compiler_params=pltpu.CompilerParams(vmem_limit_bytes=52 << 20),
-    )(place, inputs, cot)
+    )(inputs, cot)
     near_columns, near_halves = [picked[0]], [picked[steps]]
     for distance in range(1, steps):
         near_halves.append(shifted(picked[steps + distance], distance))
@@ -492,7 +490,7 @@
     lengths = valid_lengths
     blocks = 4
     cut = model_width // blocks
-    tail = pl.pallas_call(
+    short, full = pl.pallas_call(
         functools.partial(heads_kernel, length),
         grid=(blocks,),
         in_specs=[
@@ -503,8 +501,8 @@
             pl.BlockSpec((2, tokens, head), lambda i: (0, 0, 0)),
             pl.BlockSpec((2, tokens, head), lambda i: (0, 0, 0)),
         ],
-        out_specs=pl.BlockSpec((5 * tokens, head), lambda i: (0, 0)),
-        out_shape=jax.ShapeDtypeStruct((5 * tokens, head), jnp.bfloat16),
+        out_specs=[pl.BlockSpec((rows * tokens, head), lambda i: (0, 0)) for rows in (3, 5)],
+        out_shape=[jax.ShapeDtypeStruct((rows * tokens, head), jnp.bfloat16) for rows in (3, 5)],
         scratch_shapes=[pltpu.VMEM((2, 2, tokens, head), jnp.float32)],
         name="heads",
         compiler_params=pltpu.CompilerParams(vmem_limit_bytes=12 << 20),
@@ -517,9 +515,13 @@
         saved_keys[0].reshape(2, tokens, head),
     )
 
+    tails = [full]
+    for mask in range(1, sections):
+        tails.append(swapped(full if mask == sections - 1 else short, "section", mask))
+
     outputs, own_values, own_slice = pl.pallas_call(
         pick_outputs,
-        in_specs=[scalars, hbm, hbm],
+        in_specs=[hbm, hbm],
         out_specs=[memory] * 3,
         out_shape=[
             jax.ShapeDtypeStruct((2, steps, width, head), jnp.bfloat16),
@@ -529,35 +531,31 @@
         scratch_shapes=[pltpu.SemaphoreType.DMA((3,))],
         name="pick_outputs",
         compiler_params=pltpu.CompilerParams(vmem_limit_bytes=8 << 20),
-    )(place, halved, held)
+    )(halved, held)
     products = pl.pallas_call(
         functools.partial(product_kernel, sections, steps),
-        in_specs=[scalars] + [memory] * sections,
+        in_specs=[memory] * sections,
         out_specs=memory,
         out_shape=jax.ShapeDtypeStruct((sections - 1, head, head), jnp.float32),
         name="products",
         compiler_params=pltpu.CompilerParams(vmem_limit_bytes=8 << 20),
-    )(place, outputs, *fetched[1:])
+    )(outputs, *fetched[1:])
     far_products = swapped(products, "dp", 1)
     lent_back = [None] * sections
     for mask in range(1, sections):
         lent_back[mask] = swapped(fetched[mask], "dp", 1)
 
-    rows = (sections - 1) * head + 3 * tokens
-    short, full = pl.pallas_call(
+    packed = pl.pallas_call(
         pack_kernel,
-        in_specs=[memory] * 3,
-        out_specs=[memory] * 2,
-        out_shape=[
-            jax.ShapeDtypeStruct((rows, head), jnp.bfloat16),
-            jax.ShapeDtypeStruct((rows + 2 * tokens, head), jnp.bfloat16),
-        ],
+        in_specs=[memory] * 2,
+        out_specs=memory,
+        out_shape=jax.ShapeDtypeStruct((sections - 1, head, head), jnp.bfloat16),
         name="pack",
         compiler_params=pltpu.CompilerParams(vmem_limit_bytes=8 << 20),
-    )(products, far_products, tail)
-    parts = [full]
+    )(products, far_products)
+    parts = [packed]
     for mask in range(1, sections):
-        parts.append(swapped(full if mask == sections - 1 else short, "section", mask))
+        parts.append(swapped(packed, "section", mask))
 
     (upward,) = moving(near_columns, (1,), (tokens, 2 * width))
     near_mirror = swapped(upward, "section", sections - 1)
@@ -573,7 +571,7 @@
 
     sent, steer, own = pl.pallas_call(
         functools.partial(chain_kernel, sections, tokens, head),
-        in_specs=[scalars] + [memory] * sections,
+        in_specs=[memory] * (2 * sections),
         out_specs=(memory, memory, memory),
         out_shape=(
             jax.ShapeDtypeStruct((2, sections + 1, tokens, head), jnp.bfloat16),
@@ -582,7 +580,7 @@
         ),
         name="chain",
         compiler_params=pltpu.CompilerParams(vmem_limit_bytes=8 << 20),
-    )(place, *parts)
+    )(*parts, *tails)
 
     near_sent = [sent]
     for distance in range(1, steps):
@@ -595,7 +593,6 @@
         functools.partial(input_kernel, sections, tokens),
         grid=(steps,),
         in_specs=[
-            scalars,
             pl.BlockSpec((2, tokens, 2 * width), lambda i: (0, 0, i)),
             pl.BlockSpec((2 * tokens, (sections - 1) * head), lambda i: (0, 0)),
             pl.BlockSpec((2, tokens, head), lambda i: (0, 0, 0)),
@@ -606,12 +603,12 @@
         out_shape=jax.ShapeDtypeStruct((2, tokens, model_width), jnp.bfloat16),
         name="input_side",
         compiler_params=pltpu.CompilerParams(vmem_limit_bytes=12 << 20),
-    )(place, cot, steer, own, own_values, *fetched[1:], *lent_back[1:])
+    )(cot, steer, own, own_values, *fetched[1:], *lent_back[1:])
 
     every = replicas * tokens
     weight_grads = pl.pallas_call(
         functools.partial(weight_kernel, sections, steps, tokens),
-        in_specs=[scalars] + [memory] * (6 * steps + 2 * sections + 5),
+        in_specs=[memory] * (6 * steps + 2 * sections + 5),
         out_specs=memory,
         out_shape=jax.ShapeDtypeStruct((2, width, head), jnp.float32),
         scratch_shapes=[
@@ -622,7 +619,6 @@
         name="weight_side",
         compiler_params=pltpu.CompilerParams(vmem_limit_bytes=20 << 20),
     )(
-        place,
         *near_columns,
         *far_columns,
         *near_halves,

time: 121 us -> 123 us (1.017)
  the two profiles are of different devices: /device:TPU:9 before, /device:TPU:0 now
where the time goes in v3:
time: 123 us
  waiting for transfers between devices  65.1 us (53%)
  starting transfers between devices  32.5 us (26%)
  Pallas kernels  17.5 us (14%)
  local copies, waits for them, and re-layouts  6.83 us (6%)
    ppermute x9, waiting for transfers between devices, shifted(): lax.ppermute(block, 'dp', [(i, (i + 2 * distance) % count) for i in range...  34.2 us
    ppermute x31, waiting for transfers between devices, swapped(): lax.ppermute(block, axis, [(i, i ^ mask) for i in range(lax.axis_size(axi...  29.2 us
    ppermute x31, starting transfers between devices, swapped(): lax.ppermute(block, axis, [(i, i ^ mask) for i in range(lax.axis_size(axi...  15.9 us
    ppermute x9, starting transfers between devices, shifted(): lax.ppermute(block, 'dp', [(i, (i + 2 * distance) % count) for i in range...  14.1 us
    unnamed x16, local copies, waits for them, and re-layouts  6.83 us
    pallas_call x1, Pallas kernels, gathered(): pl.pallas_call(functools.partial(heads_kernel, length), grid=(blocks,), i...  4.57 us
    pallas_call x1, Pallas kernels, gathered(): pl.pallas_call(functools.partial(input_kernel, sections, tokens), grid=(s...  3.17 us
    pallas_call x1, Pallas kernels, gathered(): pl.pallas_call(functools.partial(weight_kernel, sections, steps, tokens),...  2.81 us
  transfers between devices with their start and end apart: 42, of which 15 were waited for; matrix products, arithmetic and copies ran while one was open for 0% of the time, Pallas kernels for 8%

profile of v3, /device:TPU:0, one launch (start us, length us, event | category | flops | bytes accessed | tf_op | source)
XLA Modules:
  0.0 122.8 jit_solution(15004345890803039846)
XLA Ops:
  0.6 2.2 %copy-done = bf16[1,2,2,4096,128]{4,3,2,1,0:T(8,128)(2,1)S(1)} copy-done((bf16[1,2,2,4096,128]{4,3,2,1,0:T(8,128)(2,1)S(1)}, bf16[1,2,2,4096,128]{4,3,2,1,0:T(8,128)(2,1)}, u32[]{:S(2)}) %copy-start) | copy-done | bytes 4194328
  2.8 1.2 copy-done.2
  4.0 1.2 copy-done.4
  7.5 4.6 %heads.1 = (bf16[192,128]{1,0:T(8,128)(2,1)S(1)}, bf16[320,128]{1,0:T(8,128)(2,1)S(1)}) custom-call(s32[2,2]{1,0:T(2,128)S(1)} %copy-done.7, bf16[2,64,4096]{2,1,0:T(8,128)(2,1)S(1)} %bitcast.16, bf16[2,64,4096]{2,1,0:T(8,128)(2,1)S(1)} %bitcast.13, bf16[2,2,4096,128]{3,2,1,0:T(8,128)(2,1)S(1)} %bitcast.9, bf16[2,64,128]{2,1,0:T(8,128)(2,1)S(1)} %bitcast.17, ...), custom_call_target="tpu_custom_call" | custom-call | tf_op jit(solution)/shard_map/heads/pallas_call | solution.py:493
  12.0 4.0 %collective-permute-start.9 = (bf16[320,128]{1,0:T(8,128)(2,1)S(1)}, bf16[320,128]{1,0:T(8,128)(2,1)S(1)}, u32[]{:S(2)}, u32[]{:S(2)}) collective-permute-start(bf16[320,128]{1,0:T(8,128)(2,1)S(1)} %get-tuple-element.27.refs_4_), channel_id=1, source_target_pairs={{0,3},{1,2},{2,1},{3,0},{4,7},{5,6},{6,5},{7,4},{8,11},{9,10},{10,... | collective-permute-start | bytes 245768 | tf_op jit(solution)/shard_map/ppermute | solution.py:154
  16.0 1.4 %pick_columns.1 = (bf16[2,64,1024]{2,1,0:T(8,128)(2,1)S(1)}, bf16[2,64,1024]{2,1,0:T(8,128)(2,1)S(1)}, bf16[2,64,1024]{2,1,0:T(8,128)(2,1)S(1)}, bf16[2,64,1024]...) custom-call(bf16[2,64,4096]{2,1,0:T(8,128)(2,1)} %bitcast.15, ...), custom_call_target="tpu_custom_call" | custom-call | tf_op jit(solution)/shard_map/pick_columns/pallas_call | solution.py:455
  17.5 1.6 %collective-permute-start.20 = (bf16[2,64,512]{2,1,0:T(8,128)(2,1)S(1)}, bf16[2,64,512]{2,1,0:T(8,128)(2,1)S(1)}, u32[]{:S(2)}, u32[]{:S(2)}) collective-permute-start(bf16[2,64,512]{2,1,0:T(8,128)(2,1)S(1)} %get-tuple-element.37), channel_id=1, source_target_pairs={{0,8},{4,12},{8,16},{12,20},{16,24},{20,28},{24,0},{28,4},{1,9},{5... | collective-permute-start | bytes 393224 | tf_op jit(solution)/shard_map/ppermute | solution.py:159
  20.1 2.6 %collective-permute-start.21 = (bf16[2,64,512]{2,1,0:T(8,128)(2,1)S(1)}, bf16[2,64,512]{2,1,0:T(8,128)(2,1)S(1)}, u32[]{:S(2)}, u32[]{:S(2)}) collective-permute-start(bf16[2,64,512]{2,1,0:T(8,128)(2,1)S(1)} %get-tuple-element.38), channel_id=1, source_target_pairs={{0,16},{4,20},{8,24},{12,28},{16,0},{20,4},{24,8},{28,12},{1,17},{... | collective-permute-start | bytes 393224 | tf_op jit(solution)/shard_map/ppermute | solution.py:159
  23.2 2.2 %collective-permute-start.22 = (bf16[2,64,512]{2,1,0:T(8,128)(2,1)S(1)}, bf16[2,64,512]{2,1,0:T(8,128)(2,1)S(1)}, u32[]{:S(2)}, u32[]{:S(2)}) collective-permute-start(bf16[2,64,512]{2,1,0:T(8,128)(2,1)S(1)} %get-tuple-element.39), channel_id=1, source_target_pairs={{0,24},{4,28},{8,0},{12,4},{16,8},{20,12},{24,16},{28,20},{1,25},{... | collective-permute-start | bytes 393224 | tf_op jit(solution)/shard_map/ppermute | solution.py:159
  26.0 1.3 %collective-permute-start.40 = (bf16[512,128]{1,0:T(8,128)(2,1)S(1)}, bf16[512,128]{1,0:T(8,128)(2,1)S(1)}, u32[]{:S(2)}, u32[]{:S(2)}) collective-permute-start(bf16[512,128]{1,0:T(8,128)(2,1)S(1)} %get-tuple-element.43.refs_30_.refs_36_), channel_id=1, source_target_pairs={{1,0},{5,4},{9,8},{13,12},{17,16},{21,20},{25,24},{29,28}} | collective-permute-start | bytes 393224 | tf_op jit(solution)/shard_map/ppermute | solution.py:570
  27.3 8.4 %collective-permute-done.21.refs_2_.refs_10_ = bf16[2,64,512]{2,1,0:T(8,128)(2,1)S(1)} collective-permute-done((bf16[2,64,512]{2,1,0:T(8,128)(2,1)S(1)}, bf16[2,64,512]{2,1,0:T(8,128)(2,1)S(1)}, u32[]{:S(2)}, u32[]{:S(2)}) %collective-permute-start.21) | collective-permute-done | bytes 131104 | tf_op jit(solution)/shard_map/ppermute | solution.py:159
  35.7 1.3 %collective-permute-start.41 = (bf16[512,128]{1,0:T(8,128)(2,1)S(1)}, bf16[512,128]{1,0:T(8,128)(2,1)S(1)}, u32[]{:S(2)}, u32[]{:S(2)}) collective-permute-start(bf16[512,128]{1,0:T(8,128)(2,1)S(1)} %get-tuple-element.43.refs_30_.refs_36_), channel_id=1, source_target_pairs={{2,0},{6,4},{10,8},{14,12},{18,16},{22,20},{26,24},{30,28}} | collective-permute-start | bytes 393224 | tf_op jit(solution)/shard_map/ppermute | solution.py:570
  38.0 1.4 %pick_weights.1 = (bf16[4,512,128]{2,1,0:T(8,128)(2,1)S(1)}, bf16[4,512,128]{2,1,0:T(8,128)(2,1)S(1)}, bf16[4,512,128]{2,1,0:T(8,128)(2,1)S(1)}) custom-call(bf16[2,2,4,2,512,128]{5,4,3,2,1,0:T(8,128)(2,1)} %bitcast.8), custom_call_target="tpu_custom_call" | custom-call | tf_op jit(solution)/shard_map/pick_weights/pallas_call | solution.py:440
  39.9 1.5 %collective-permute-start.1 = (bf16[4,512,128]{2,1,0:T(8,128)(2,1)S(1)}, bf16[4,512,128]{2,1,0:T(8,128)(2,1)S(1)}, u32[]{:S(2)}, u32[]{:S(2)}) collective-permute-start(bf16[4,512,128]{2,1,0:T(8,128)(2,1)S(1)} %get-tuple-element.25), channel_id=1, source_target_pairs={{0,2},{1,3},{2,0},{3,1},{4,6},{5,7},{6,4},{7,5},{8,10},{9,11},{10,... | collective-permute-start | bytes 1572872 | tf_op jit(solution)/shard_map/ppermute | solution.py:154
  41.4 1.7 %collective-permute-done.41.refs_35_ = bf16[512,128]{1,0:T(8,128)(2,1)S(1)} collective-permute-done((bf16[512,128]{1,0:T(8,128)(2,1)S(1)}, bf16[512,128]{1,0:T(8,128)(2,1)S(1)}, u32[]{:S(2)}, u32[]{:S(2)}) %collective-permute-start.41) | collective-permute-done | bytes 131104 | tf_op jit(solution)/shard_map/ppermute | solution.py:570
  43.1 3.2 %collective-permute-start.15 = (bf16[2,64,1024]{2,1,0:T(8,128)(2,1)S(1)}, bf16[2,64,1024]{2,1,0:T(8,128)(2,1)S(1)}, u32[]{:S(2)}, u32[]{:S(2)}) collective-permute-start(bf16[2,64,1024]{2,1,0:T(8,128)(2,1)S(1)} %get-tuple-element.35), channel_id=1, source_target_pairs={{0,24},{4,28},{8,0},{12,4},{16,8},{20,12},{24,16},{28,20},{1,25},{... | collective-permute-start | bytes 786440 | tf_op jit(solution)/shard_map/ppermute | solution.py:159
  46.4 6.1 %collective-permute-done.14.refs_2_ = bf16[2,64,1024]{2,1,0:T(8,128)(2,1)S(1)} collective-permute-done((bf16[2,64,1024]{2,1,0:T(8,128)(2,1)S(1)}, bf16[2,64,1024]{2,1,0:T(8,128)(2,1)S(1)}, u32[]{:S(2)}, u32[]{:S(2)}) %collective-permute-start.14) | collective-permute-done | bytes 262176 | tf_op jit(solution)/shard_map/ppermute | solution.py:159
  54.0 1.0 collective-permute-start.29
  55.4 9.4 %collective-permute-done.1.refs_1_.refs_32_ = bf16[4,512,128]{2,1,0:T(8,128)(2,1)S(1)} collective-permute-done((bf16[4,512,128]{2,1,0:T(8,128)(2,1)S(1)}, bf16[4,512,128]{2,1,0:T(8,128)(2,1)S(1)}, u32[]{:S(2)}, u32[]{:S(2)}) %collective-permute-start.1) | collective-permute-done | bytes 524320 | tf_op jit(solution)/shard_map/ppermute | solution.py:154
  64.8 2.0 %collective-permute-done.2.refs_2_.refs_33_ = bf16[4,512,128]{2,1,0:T(8,128)(2,1)S(1)} collective-permute-done((bf16[4,512,128]{2,1,0:T(8,128)(2,1)S(1)}, bf16[4,512,128]{2,1,0:T(8,128)(2,1)S(1)}, u32[]{:S(2)}, u32[]{:S(2)}) %collective-permute-start.2) | collective-permute-done | bytes 524320 | tf_op jit(solution)/shard_map/ppermute | solution.py:154
  68.3 2.3 %collective-permute-done.29.refs_18_ = bf16[4,64,512]{2,1,0:T(8,128)(2,1)S(1)} collective-permute-done((bf16[4,64,512]{2,1,0:T(8,128)(2,1)S(1)}, bf16[4,64,512]{2,1,0:T(8,128)(2,1)S(1)}, u32[]{:S(2)}, u32[]{:S(2)}) %collective-permute-start.29) | collective-permute-done | bytes 262176 | tf_op jit(solution)/shard_map/ppermute | solution.py:154
  72.8 1.4 %collective-permute-start.4 = (bf16[3,128,128]{2,1,0:T(8,128)(2,1)S(1)}, bf16[3,128,128]{2,1,0:T(8,128)(2,1)S(1)}, u32[]{:S(2)}, u32[]{:S(2)}) collective-permute-start(bf16[3,128,128]{2,1,0:T(8,128)(2,1)S(1)} %pack.1.refs_0_), channel_id=1, source_target_pairs={{0,1},{1,0},{2,3},{3,2},{4,5},{5,4},{6,7},{7,6},{8,9},{9,8},{10,11... | collective-permute-start | bytes 294920 | tf_op jit(solution)/shard_map/ppermute | solution.py:154
  74.3 1.3 %collective-permute-start.5 = (bf16[3,128,128]{2,1,0:T(8,128)(2,1)S(1)}, bf16[3,128,128]{2,1,0:T(8,128)(2,1)S(1)}, u32[]{:S(2)}, u32[]{:S(2)}) collective-permute-start(bf16[3,128,128]{2,1,0:T(8,128)(2,1)S(1)} %pack.1.refs_0_), channel_id=1, source_target_pairs={{0,2},{1,3},{2,0},{3,1},{4,6},{5,7},{6,4},{7,5},{8,10},{9,11},{10,... | collective-permute-start | bytes 294920 | tf_op jit(solution)/shard_map/ppermute | solution.py:154
  76.4 12.7 %collective-permute-done.4.refs_1_ = bf16[3,128,128]{2,1,0:T(8,128)(2,1)S(1)} collective-permute-done((bf16[3,128,128]{2,1,0:T(8,128)(2,1)S(1)}, bf16[3,128,128]{2,1,0:T(8,128)(2,1)S(1)}, u32[]{:S(2)}, u32[]{:S(2)}) %collective-permute-start.4) | collective-permute-done | bytes 98336 | tf_op jit(solution)/shard_map/ppermute | solution.py:154
  89.7 1.3 %collective-permute-done.6.refs_3_ = bf16[3,128,128]{2,1,0:T(8,128)(2,1)S(1)} collective-permute-done((bf16[3,128,128]{2,1,0:T(8,128)(2,1)S(1)}, bf16[3,128,128]{2,1,0:T(8,128)(2,1)S(1)}, u32[]{:S(2)}, u32[]{:S(2)}) %collective-permute-start.6) | collective-permute-done | bytes 98336 | tf_op jit(solution)/shard_map/ppermute | solution.py:154
  91.0 1.6 %chain.1 = (bf16[2,5,64,128]{3,2,1,0:T(8,128)(2,1)S(1)}, bf16[128,384]{1,0:T(8,128)(2,1)S(1)}, bf16[2,64,128]{2,1,0:T(8,128)(2,1)S(1)}) custom-call(bf16[3,128,128]{2,1,0:T(8,128)(2,1)S(1)} %pack.1.refs_0_, bf16[3,128,128]{2,1,0:T(8,128)(2,1)S(1)} %collective-permute-done.4.refs_1_, bf16[3,128,128]{2,1,0:T(8,128)(2,1)S(1)} %collective-permute-done.5.refs_2_, ...), custom_call_target="tpu_custom_call" | custom-call | tf_op jit(solution)/shard_map/chain/pallas_call | solution.py:572
  93.7 7.4 %collective-permute-done.33.refs_23_ = bf16[2,5,64,128]{3,2,1,0:T(8,128)(2,1)S(1)} collective-permute-done((bf16[2,5,64,128]{3,2,1,0:T(8,128)(2,1)S(1)}, bf16[2,5,64,128]{3,2,1,0:T(8,128)(2,1)S(1)}, u32[]{:S(2)}, u32[]{:S(2)}) %collective-permute-start.33) | collective-permute-done | bytes 163872 | tf_op jit(solution)/shard_map/ppermute | solution.py:159
  101.1 8.6 %collective-permute-done.34.refs_24_ = bf16[2,5,64,128]{3,2,1,0:T(8,128)(2,1)S(1)} collective-permute-done((bf16[2,5,64,128]{3,2,1,0:T(8,128)(2,1)S(1)}, bf16[2,5,64,128]{3,2,1,0:T(8,128)(2,1)S(1)}, u32[]{:S(2)}, u32[]{:S(2)}) %collective-permute-start.34) | collective-permute-done | bytes 163872 | tf_op jit(solution)/shard_map/ppermute | solution.py:159
  109.7 2.6 %collective-permute-start.35 = (bf16[2,5,64,128]{3,2,1,0:T(8,128)(2,1)S(1)}, bf16[2,5,64,128]{3,2,1,0:T(8,128)(2,1)S(1)}, u32[]{:S(2)}, u32[]{:S(2)}) collective-permute-start(bf16[2,5,64,128]{3,2,1,0:T(8,128)(2,1)S(1)} %get-tuple-element.42.refs_22_), channel_id=1, source_target_pairs={{0,24},{4,28},{8,0},{12,4},{16,8},{20,12},{24,16},{28,20},{1,25},{... | collective-permute-start | bytes 491528 | tf_op jit(solution)/shard_map/ppermute | solution.py:159
  112.2 3.6 %collective-permute-done.35.refs_25_ = bf16[2,5,64,128]{3,2,1,0:T(8,128)(2,1)S(1)} collective-permute-done((bf16[2,5,64,128]{3,2,1,0:T(8,128)(2,1)S(1)}, bf16[2,5,64,128]{3,2,1,0:T(8,128)(2,1)S(1)}, u32[]{:S(2)}, u32[]{:S(2)}) %collective-permute-start.35) | collective-permute-done | bytes 163872 | tf_op jit(solution)/shard_map/ppermute | solution.py:159
  116.8 3.2 %input_side.1 = bf16[2,64,4096]{2,1,0:T(8,128)(2,1)} custom-call(bf16[2,64,4096]{2,1,0:T(8,128)(2,1)S(1)} %bitcast.14, bf16[128,384]{1,0:T(8,128)(2,1)S(1)} %get-tuple-element.29.steer, bf16[2,64,128]{2,1,0:T(8,128)(2,1)S(1)} %get-tuple-element.30.own, bf16[2,4096,128]{2,1,0:T(8,128)(2,1)S(1)} %get-tuple-element.31.held, ...), custom_call_target="tpu_custom_call" | custom-call | tf_op jit(solution)/shard_map/input_side/pallas_call | solution.py:592
  120.0 2.8 %weight_side.1 = f32[2,512,128]{2,1,0:T(8,128)} custom-call(bf16[2,64,1024]{2,1,0:T(8,128)(2,1)S(1)} %get-tuple-element.32.refs_0_, bf16[2,64,1024]{2,1,0:T(8,128)(2,1)S(1)} %collective-permute-done.13.refs_1_, bf16[2,64,1024]{2,1,0:T(8,128)(2,1)S(1)} %collective-permute-done.14.refs_2_, bf16[2,64,1024]{2,1,0:T(8,128)(2,1)S(1)} %collective-permute-done.15.refs_3_, ...), custom_call_target="tpu_custom_call" | custom-call | tf_op jit(solution)/shard_map/weight_side/pallas_call | solution.py:609
  (79 shorter events, 14.8 us)
Async XLA Ops:
  12.0 13.4 %collective-permute-start.9 = (bf16[320,128]{1,0:T(8,128)(2,1)S(1)}, bf16[320,128]{1,0:T(8,128)(2,1)S(1)}, u32[]{:S(2)}, u32[]{:S(2)}) collective-permute-start(bf16[320,128]{1,0:T(8,128)(2,1)S(1)} %get-tuple-element.27.refs_4_), channel_id=1, source_target_pairs={{0,3},{1,2},{2,1},{3,0},{4,7},{5,6},{6,5},{7,4},{8,11},{9,10},{10,... | collective-permute-start | bytes 245768 | tf_op jit(solution)/shard_map/ppermute | solution.py:154
  17.5 8.5 %collective-permute-start.20 = (bf16[2,64,512]{2,1,0:T(8,128)(2,1)S(1)}, bf16[2,64,512]{2,1,0:T(8,128)(2,1)S(1)}, u32[]{:S(2)}, u32[]{:S(2)}) collective-permute-start(bf16[2,64,512]{2,1,0:T(8,128)(2,1)S(1)} %get-tuple-element.37), channel_id=1, source_target_pairs={{0,8},{4,12},{8,16},{12,20},{16,24},{20,28},{24,0},{28,4},{1,9},{5... | collective-permute-start | bytes 393224 | tf_op jit(solution)/shard_map/ppermute | solution.py:159
  19.6 5.8 %collective-permute-start.8 = (bf16[192,128]{1,0:T(8,128)(2,1)S(1)}, bf16[192,128]{1,0:T(8,128)(2,1)S(1)}, u32[]{:S(2)}, u32[]{:S(2)}) collective-permute-start(bf16[192,128]{1,0:T(8,128)(2,1)S(1)} %get-tuple-element.28), channel_id=1, source_target_pairs={{0,2},{1,3},{2,0},{3,1},{4,6},{5,7},{6,4},{7,5},{8,10},{9,11},{10,... | collective-permute-start | bytes 147464 | tf_op jit(solution)/shard_map/ppermute | solution.py:154
  20.1 15.6 %collective-permute-start.21 = (bf16[2,64,512]{2,1,0:T(8,128)(2,1)S(1)}, bf16[2,64,512]{2,1,0:T(8,128)(2,1)S(1)}, u32[]{:S(2)}, u32[]{:S(2)}) collective-permute-start(bf16[2,64,512]{2,1,0:T(8,128)(2,1)S(1)} %get-tuple-element.38), channel_id=1, source_target_pairs={{0,16},{4,20},{8,24},{12,28},{16,0},{20,4},{24,8},{28,12},{1,17},{... | collective-permute-start | bytes 393224 | tf_op jit(solution)/shard_map/ppermute | solution.py:159
  23.2 13.8 %collective-permute-start.22 = (bf16[2,64,512]{2,1,0:T(8,128)(2,1)S(1)}, bf16[2,64,512]{2,1,0:T(8,128)(2,1)S(1)}, u32[]{:S(2)}, u32[]{:S(2)}) collective-permute-start(bf16[2,64,512]{2,1,0:T(8,128)(2,1)S(1)} %get-tuple-element.39), channel_id=1, source_target_pairs={{0,24},{4,28},{8,0},{12,4},{16,8},{20,12},{24,16},{28,20},{1,25},{... | collective-permute-start | bytes 393224 | tf_op jit(solution)/shard_map/ppermute | solution.py:159
  25.4 17.7 %collective-permute-start.13 = (bf16[2,64,1024]{2,1,0:T(8,128)(2,1)S(1)}, bf16[2,64,1024]{2,1,0:T(8,128)(2,1)S(1)}, u32[]{:S(2)}, u32[]{:S(2)}) collective-permute-start(bf16[2,64,1024]{2,1,0:T(8,128)(2,1)S(1)} %get-tuple-element.33), channel_id=1, source_target_pairs={{0,8},{4,12},{8,16},{12,20},{16,24},{20,28},{24,0},{28,4},{1,9},{5... | collective-permute-start | bytes 786440 | tf_op jit(solution)/shard_map/ppermute | solution.py:159
  25.5 14.0 %collective-permute-start.23 = (bf16[2,64,512]{2,1,0:T(8,128)(2,1)S(1)}, bf16[2,64,512]{2,1,0:T(8,128)(2,1)S(1)}, u32[]{:S(2)}, u32[]{:S(2)}) collective-permute-start(bf16[2,64,512]{2,1,0:T(8,128)(2,1)S(1)} %get-tuple-element.36.refs_0_.refs_8_), channel_id=1, source_target_pairs={{0,4},{4,0},{8,12},{12,8},{16,20},{20,16},{24,28},{28,24},{1,5},{5... | collective-permute-start | bytes 393224 | tf_op jit(solution)/shard_map/ppermute | solution.py:154
  26.0 14.0 %collective-permute-start.40 = (bf16[512,128]{1,0:T(8,128)(2,1)S(1)}, bf16[512,128]{1,0:T(8,128)(2,1)S(1)}, u32[]{:S(2)}, u32[]{:S(2)}) collective-permute-start(bf16[512,128]{1,0:T(8,128)(2,1)S(1)} %get-tuple-element.43.refs_30_.refs_36_), channel_id=1, source_target_pairs={{1,0},{5,4},{9,8},{13,12},{17,16},{21,20},{25,24},{29,28}} | collective-permute-start | bytes 393224 | tf_op jit(solution)/shard_map/ppermute | solution.py:570
  35.7 7.4 %collective-permute-start.41 = (bf16[512,128]{1,0:T(8,128)(2,1)S(1)}, bf16[512,128]{1,0:T(8,128)(2,1)S(1)}, u32[]{:S(2)}, u32[]{:S(2)}) collective-permute-start(bf16[512,128]{1,0:T(8,128)(2,1)S(1)} %get-tuple-element.43.refs_30_.refs_36_), channel_id=1, source_target_pairs={{2,0},{6,4},{10,8},{14,12},{18,16},{22,20},{26,24},{30,28}} | collective-permute-start | bytes 393224 | tf_op jit(solution)/shard_map/ppermute | solution.py:570
  37.0 15.5 %collective-permute-start.14 = (bf16[2,64,1024]{2,1,0:T(8,128)(2,1)S(1)}, bf16[2,64,1024]{2,1,0:T(8,128)(2,1)S(1)}, u32[]{:S(2)}, u32[]{:S(2)}) collective-permute-start(bf16[2,64,1024]{2,1,0:T(8,128)(2,1)S(1)} %get-tuple-element.34), channel_id=1, source_target_pairs={{0,16},{4,20},{8,24},{12,28},{16,0},{20,4},{24,8},{28,12},{1,17},{... | collective-permute-start | bytes 786440 | tf_op jit(solution)/shard_map/ppermute | solution.py:159
  39.4 16.0 %collective-permute-start = (bf16[4,512,128]{2,1,0:T(8,128)(2,1)S(1)}, bf16[4,512,128]{2,1,0:T(8,128)(2,1)S(1)}, u32[]{:S(2)}, u32[]{:S(2)}) collective-permute-start(bf16[4,512,128]{2,1,0:T(8,128)(2,1)S(1)} %get-tuple-element.24), channel_id=1, source_target_pairs={{0,1},{1,0},{2,3},{3,2},{4,5},{5,4},{6,7},{7,6},{8,9},{9,8},{10,11... | collective-permute-start | bytes 1572872 | tf_op jit(solution)/shard_map/ppermute | solution.py:154
  39.9 24.9 %collective-permute-start.1 = (bf16[4,512,128]{2,1,0:T(8,128)(2,1)S(1)}, bf16[4,512,128]{2,1,0:T(8,128)(2,1)S(1)}, u32[]{:S(2)}, u32[]{:S(2)}) collective-permute-start(bf16[4,512,128]{2,1,0:T(8,128)(2,1)S(1)} %get-tuple-element.25), channel_id=1, source_target_pairs={{0,2},{1,3},{2,0},{3,1},{4,6},{5,7},{6,4},{7,5},{8,10},{9,11},{10,... | collective-permute-start | bytes 1572872 | tf_op jit(solution)/shard_map/ppermute | solution.py:154
  43.1 23.7 %collective-permute-start.2 = (bf16[4,512,128]{2,1,0:T(8,128)(2,1)S(1)}, bf16[4,512,128]{2,1,0:T(8,128)(2,1)S(1)}, u32[]{:S(2)}, u32[]{:S(2)}) collective-permute-start(bf16[4,512,128]{2,1,0:T(8,128)(2,1)S(1)} %get-tuple-element.26), channel_id=1, source_target_pairs={{0,3},{1,2},{2,1},{3,0},{4,7},{5,6},{6,5},{7,4},{8,11},{9,10},{10,... | collective-permute-start | bytes 1572872 | tf_op jit(solution)/shard_map/ppermute | solution.py:154
  43.1 9.4 %collective-permute-start.15 = (bf16[2,64,1024]{2,1,0:T(8,128)(2,1)S(1)}, bf16[2,64,1024]{2,1,0:T(8,128)(2,1)S(1)}, u32[]{:S(2)}, u32[]{:S(2)}) collective-permute-start(bf16[2,64,1024]{2,1,0:T(8,128)(2,1)S(1)} %get-tuple-element.35), channel_id=1, source_target_pairs={{0,24},{4,28},{8,0},{12,4},{16,8},{20,12},{24,16},{28,20},{1,25},{... | collective-permute-start | bytes 786440 | tf_op jit(solution)/shard_map/ppermute | solution.py:159
  54.0 16.6 %collective-permute-start.29 = (bf16[4,64,512]{2,1,0:T(8,128)(2,1)S(1)}, bf16[4,64,512]{2,1,0:T(8,128)(2,1)S(1)}, u32[]{:S(2)}, u32[]{:S(2)}) collective-permute-start(bf16[4,64,512]{2,1,0:T(8,128)(2,1)S(1)} %get-tuple-element.40), channel_id=1, source_target_pairs={{0,2},{1,3},{2,0},{3,1},{4,6},{5,7},{6,4},{7,5},{8,10},{9,11},{10,... | collective-permute-start | bytes 786440 | tf_op jit(solution)/shard_map/ppermute | solution.py:154
  55.1 15.6 %collective-permute-start.30 = (bf16[4,64,512]{2,1,0:T(8,128)(2,1)S(1)}, bf16[4,64,512]{2,1,0:T(8,128)(2,1)S(1)}, u32[]{:S(2)}, u32[]{:S(2)}) collective-permute-start(bf16[4,64,512]{2,1,0:T(8,128)(2,1)S(1)} %get-tuple-element.41), channel_id=1, source_target_pairs={{0,1},{1,0},{2,3},{3,2},{4,5},{5,4},{6,7},{7,6},{8,9},{9,8},{10,11... | collective-permute-start | bytes 786440 | tf_op jit(solution)/shard_map/ppermute | solution.py:154
  55.4 16.5 %collective-permute-start.17 = (bf16[2,64,1024]{2,1,0:T(8,128)(2,1)S(1)}, bf16[2,64,1024]{2,1,0:T(8,128)(2,1)S(1)}, u32[]{:S(2)}, u32[]{:S(2)}) collective-permute-start(bf16[2,64,1024]{2,1,0:T(8,128)(2,1)S(1)} %collective-permute-done.13.refs_1_), channel_id=1, source_target_pairs={{0,4},{4,0},{8,12},{12,8},{16,20},{20,16},{24,28},{28,24},{1,5},{5... | collective-permute-start | bytes 786440 | tf_op jit(solution)/shard_map/ppermute | solution.py:154
  67.5 5.3 %collective-permute-start.3 = (f32[3,128,128]{2,1,0:T(8,128)S(1)}, f32[3,128,128]{2,1,0:T(8,128)S(1)}, u32[]{:S(2)}, u32[]{:S(2)}) collective-permute-start(f32[3,128,128]{2,1,0:T(8,128)S(1)} %products.1.near), channel_id=1, source_target_pairs={{0,4},{4,0},{8,12},{12,8},{16,20},{20,16},{24,28},{28,24},{1,5},{5... | collective-permute-start | bytes 589832 | tf_op jit(solution)/shard_map/ppermute | solution.py:154
  68.2 4.7 %collective-permute-start.18 = (bf16[2,64,1024]{2,1,0:T(8,128)(2,1)S(1)}, bf16[2,64,1024]{2,1,0:T(8,128)(2,1)S(1)}, u32[]{:S(2)}, u32[]{:S(2)}) collective-permute-start(bf16[2,64,1024]{2,1,0:T(8,128)(2,1)S(1)} %collective-permute-done.14.refs_2_), channel_id=1, source_target_pairs={{0,4},{4,0},{8,12},{12,8},{16,20},{20,16},{24,28},{28,24},{1,5},{5... | collective-permute-start | bytes 786440 | tf_op jit(solution)/shard_map/ppermute | solution.py:154
  70.7 4.9 %collective-permute-start.31 = (bf16[4,64,512]{2,1,0:T(8,128)(2,1)S(1)}, bf16[4,64,512]{2,1,0:T(8,128)(2,1)S(1)}, u32[]{:S(2)}, u32[]{:S(2)}) collective-permute-start(bf16[4,64,512]{2,1,0:T(8,128)(2,1)S(1)} %collective-permute-done.29.refs_18_), channel_id=1, source_target_pairs={{0,4},{4,0},{8,12},{12,8},{16,20},{20,16},{24,28},{28,24},{1,5},{5... | collective-permute-start | bytes 786440 | tf_op jit(solution)/shard_map/ppermute | solution.py:154
  71.9 21.6 %collective-permute-start.27 = (bf16[4,64,1024]{2,1,0:T(8,128)(2,1)S(1)}, bf16[4,64,1024]{2,1,0:T(8,128)(2,1)S(1)}, u32[]{:S(2)}, u32[]{:S(2)}) collective-permute-start(bf16[4,64,1024]{2,1,0:T(8,128)(2,1)S(1)} %pick_moving.2), channel_id=1, source_target_pairs={{0,3},{1,2},{2,1},{3,0},{4,7},{5,6},{6,5},{7,4},{8,11},{9,10},{10,... | collective-permute-start | bytes 1572872 | tf_op jit(solution)/shard_map/ppermute | solution.py:154
  72.8 19.8 %collective-permute-start.32 = (bf16[4,64,512]{2,1,0:T(8,128)(2,1)S(1)}, bf16[4,64,512]{2,1,0:T(8,128)(2,1)S(1)}, u32[]{:S(2)}, u32[]{:S(2)}) collective-permute-start(bf16[4,64,512]{2,1,0:T(8,128)(2,1)S(1)} %collective-permute-done.30.refs_19_), channel_id=1, source_target_pairs={{0,4},{4,0},{8,12},{12,8},{16,20},{20,16},{24,28},{28,24},{1,5},{5... | collective-permute-start | bytes 786440 | tf_op jit(solution)/shard_map/ppermute | solution.py:154
  72.8 16.2 %collective-permute-start.4 = (bf16[3,128,128]{2,1,0:T(8,128)(2,1)S(1)}, bf16[3,128,128]{2,1,0:T(8,128)(2,1)S(1)}, u32[]{:S(2)}, u32[]{:S(2)}) collective-permute-start(bf16[3,128,128]{2,1,0:T(8,128)(2,1)S(1)} %pack.1.refs_0_), channel_id=1, source_target_pairs={{0,1},{1,0},{2,3},{3,2},{4,5},{5,4},{6,7},{7,6},{8,9},{9,8},{10,11... | collective-permute-start | bytes 294920 | tf_op jit(solution)/shard_map/ppermute | solution.py:154
  74.3 15.4 %collective-permute-start.5 = (bf16[3,128,128]{2,1,0:T(8,128)(2,1)S(1)}, bf16[3,128,128]{2,1,0:T(8,128)(2,1)S(1)}, u32[]{:S(2)}, u32[]{:S(2)}) collective-permute-start(bf16[3,128,128]{2,1,0:T(8,128)(2,1)S(1)} %pack.1.refs_0_), channel_id=1, source_target_pairs={{0,2},{1,3},{2,0},{3,1},{4,6},{5,7},{6,4},{7,5},{8,10},{9,11},{10,... | collective-permute-start | bytes 294920 | tf_op jit(solution)/shard_map/ppermute | solution.py:154
  75.5 15.4 %collective-permute-start.6 = (bf16[3,128,128]{2,1,0:T(8,128)(2,1)S(1)}, bf16[3,128,128]{2,1,0:T(8,128)(2,1)S(1)}, u32[]{:S(2)}, u32[]{:S(2)}) collective-permute-start(bf16[3,128,128]{2,1,0:T(8,128)(2,1)S(1)} %pack.1.refs_0_), channel_id=1, source_target_pairs={{0,3},{1,2},{2,1},{3,0},{4,7},{5,6},{6,5},{7,4},{8,11},{9,10},{10,... | collective-permute-start | bytes 294920 | tf_op jit(solution)/shard_map/ppermute | solution.py:154
  89.1 26.7 %collective-permute-start.10 = (bf16[4,512,128]{2,1,0:T(8,128)(2,1)S(1)}, bf16[4,512,128]{2,1,0:T(8,128)(2,1)S(1)}, u32[]{:S(2)}, u32[]{:S(2)}) collective-permute-start(bf16[4,512,128]{2,1,0:T(8,128)(2,1)S(1)} %collective-permute-done.refs_0_.refs_31_), channel_id=1, source_target_pairs={{0,4},{4,0},{8,12},{12,8},{16,20},{20,16},{24,28},{28,24},{1,5},{5... | collective-permute-start | bytes 1572872 | tf_op jit(solution)/shard_map/ppermute | solution.py:154
  89.7 26.6 %collective-permute-start.11 = (bf16[4,512,128]{2,1,0:T(8,128)(2,1)S(1)}, bf16[4,512,128]{2,1,0:T(8,128)(2,1)S(1)}, u32[]{:S(2)}, u32[]{:S(2)}) collective-permute-start(bf16[4,512,128]{2,1,0:T(8,128)(2,1)S(1)} %collective-permute-done.1.refs_1_.refs_32_), channel_id=1, source_target_pairs={{0,4},{4,0},{8,12},{12,8},{16,20},{20,16},{24,28},{28,24},{1,5},{5... | collective-permute-start | bytes 1572872 | tf_op jit(solution)/shard_map/ppermute | solution.py:154
  91.0 25.4 %collective-permute-start.12 = (bf16[4,512,128]{2,1,0:T(8,128)(2,1)S(1)}, bf16[4,512,128]{2,1,0:T(8,128)(2,1)S(1)}, u32[]{:S(2)}, u32[]{:S(2)}) collective-permute-start(bf16[4,512,128]{2,1,0:T(8,128)(2,1)S(1)} %collective-permute-done.2.refs_2_.refs_33_), channel_id=1, source_target_pairs={{0,4},{4,0},{8,12},{12,8},{16,20},{20,16},{24,28},{28,24},{1,5},{5... | collective-permute-start | bytes 1572872 | tf_op jit(solution)/shard_map/ppermute | solution.py:154
  92.6 8.5 %collective-permute-start.33 = (bf16[2,5,64,128]{3,2,1,0:T(8,128)(2,1)S(1)}, bf16[2,5,64,128]{3,2,1,0:T(8,128)(2,1)S(1)}, u32[]{:S(2)}, u32[]{:S(2)}) collective-permute-start(bf16[2,5,64,128]{3,2,1,0:T(8,128)(2,1)S(1)} %get-tuple-element.42.refs_22_), channel_id=1, source_target_pairs={{0,8},{4,12},{8,16},{12,20},{16,24},{20,28},{24,0},{28,4},{1,9},{5... | collective-permute-start | bytes 491528 | tf_op jit(solution)/shard_map/ppermute | solution.py:159
  93.5 26.6 %collective-permute-start.28 = (bf16[4,64,1024]{2,1,0:T(8,128)(2,1)S(1)}, bf16[4,64,1024]{2,1,0:T(8,128)(2,1)S(1)}, u32[]{:S(2)}, u32[]{:S(2)}) collective-permute-start(bf16[4,64,1024]{2,1,0:T(8,128)(2,1)S(1)} %collective-permute-done.27.refs_16_), channel_id=1, source_target_pairs={{0,4},{4,0},{8,12},{12,8},{16,20},{20,16},{24,28},{28,24},{1,5},{5... | collective-permute-start | bytes 1572872 | tf_op jit(solution)/shard_map/ppermute | solution.py:154
  101.1 8.6 %collective-permute-start.34 = (bf16[2,5,64,128]{3,2,1,0:T(8,128)(2,1)S(1)}, bf16[2,5,64,128]{3,2,1,0:T(8,128)(2,1)S(1)}, u32[]{:S(2)}, u32[]{:S(2)}) collective-permute-start(bf16[2,5,64,128]{3,2,1,0:T(8,128)(2,1)S(1)} %get-tuple-element.42.refs_22_), channel_id=1, source_target_pairs={{0,16},{4,20},{8,24},{12,28},{16,0},{20,4},{24,8},{28,12},{1,17},{... | collective-permute-start | bytes 491528 | tf_op jit(solution)/shard_map/ppermute | solution.py:159
  109.7 6.1 %collective-permute-start.35 = (bf16[2,5,64,128]{3,2,1,0:T(8,128)(2,1)S(1)}, bf16[2,5,64,128]{3,2,1,0:T(8,128)(2,1)S(1)}, u32[]{:S(2)}, u32[]{:S(2)}) collective-permute-start(bf16[2,5,64,128]{3,2,1,0:T(8,128)(2,1)S(1)} %get-tuple-element.42.refs_22_), channel_id=1, source_target_pairs={{0,24},{4,28},{8,0},{12,4},{16,8},{20,12},{24,16},{28,20},{1,25},{... | collective-permute-start | bytes 491528 | tf_op jit(solution)/shard_map/ppermute | solution.py:159
  (18 other events, 136.2 us)

commit v4 on v3

--- a/solution.py
+++ b/solution.py
@@ -7,6 +7,9 @@
 from jax.experimental import pallas as pl
 from jax.experimental.pallas import tpu as pltpu
 from jax.sharding import PartitionSpec as P
+
+
+SECTION = "section"
 
 
 def passed_along(block, axis, distance):
@@ -42,8 +45,8 @@
 
 
 def reduced(layer_inputs, saved_queries, saved_keys, held_weights, cotangent, valid_lengths):
-    sections = lax.axis_size("section")
-    position = lax.axis_index("section")
+    sections = lax.axis_size(SECTION)
+    position = lax.axis_index(SECTION)
     inputs = layer_inputs[0]
     value_w = held_weights[0, :, 0]
     output_w = held_weights[0, :, 1]
@@ -116,8 +119,8 @@
 
     def loop_body(moment, carried):
         outgoing, held = carried
-        from_next = passed_along(outgoing[0], "section", -1)
-        from_prev = passed_along(outgoing[1], "section", 1)
+        from_next = passed_along(outgoing[0], SECTION, -1)
+        from_prev = passed_along(outgoing[1], SECTION, 1)
         return advance(moment, jnp.stack([from_next, from_prev]), held)
 
     sent, buffers = lax.fori_loop(1, sections + micro_count - 1, loop_body, (sent, buffers))
@@ -142,7 +145,7 @@
     own_part = summed[:, 0]
     mirror_part = summed[:, 1]
     for bit_no in range(sections.bit_length() - 1):
-        mirror_part = from_partner(mirror_part.astype(jnp.bfloat16), "section", bit_no).astype(
+        mirror_part = from_partner(mirror_part.astype(jnp.bfloat16), SECTION, bit_no).astype(
             mirror_part.dtype
         )
     combined = own_part + mirror_part
@@ -287,8 +290,8 @@
 
 
 def position():
-    here, replica = lax.axis_index("section"), lax.axis_index("dp")
-    asides = (lax.axis_size("section") // 2, 1)
+    here, replica = lax.axis_index(SECTION), lax.axis_index("dp")
+    asides = (lax.axis_size(SECTION) // 2, 1)
     bits = [jnp.where((here & aside) != 0, 1, 0) for aside in asides]
     return (here, lax.rem(replica, 2), lax.div(replica, 2), *bits)
 
@@ -359,11 +362,9 @@
 
 def weight_kernel(sections, steps, tokens, *refs):
     place = position()
-    columns = refs[: 2 * steps]
-    halves, refs = refs[2 * steps : 4 * steps], refs[2 * steps :]
-    mirrored, lent = refs[2 * steps : 2 * steps + 2], refs[2 * steps + 2 : 2 * steps + 6]
-    sent = refs[2 * steps + 6 : 4 * steps + 6]
-    refs = refs[4 * steps + 6 :]
+    columns, halves, refs = refs[:2], refs[2:6], refs[6:]
+    mirrored, lent, refs = refs[:2], refs[2:6], refs[6:]
+    sent, refs = refs[: 2 * steps], refs[2 * steps :]
     own_slice, fetched, lent_slices = refs[0], refs[:sections], refs[sections - 1 :]
     out, lefts, rights, steers = refs[2 * sections - 1 :]
     width, head = out.shape[1:]
@@ -377,7 +378,7 @@
             both = slice(way * every + index * tokens, way * every + (index + 1) * tokens)
             lefts[0, both, :] = sent[index][way, 0]
             lefts[1, both, :] = sent[index][way, sections]
-        rights[rows, :] = columns[index][0, :, lanes]
+        rights[rows, :] = columns[index // steps][index % steps, :, lanes]
         rows = slice(every + index * tokens, every + (index + 1) * tokens)
         rights[rows, :] = mirrored[index // steps][index % steps, :, lanes]
     out[0] = contract(lefts[0], rights[...], 0, 0).T
@@ -387,7 +388,7 @@
 
             @pl.when(place[3 + way] == place[1])
             def _():
-                rights[both, :] = halves[index][way]
+                rights[both, :] = halves[2 * (index // steps) + way][index % steps]
 
             @pl.when(place[3 + way] != place[1])
             def _():
@@ -419,7 +420,7 @@
 
 
 def gathered(layer_inputs, saved_queries, saved_keys, held_weights, cotangent, valid_lengths):
-    sections = lax.axis_size("section")
+    sections = lax.axis_size(SECTION)
     replicas = lax.axis_size("dp")
     steps = replicas // 2
     inputs = layer_inputs[0]
@@ -443,12 +444,11 @@
         out_specs=[memory] * (sections - 1),
         out_shape=[jax.ShapeDtypeStruct((steps, width, head), jnp.bfloat16)] * (sections - 1),
         scratch_shapes=[pltpu.SemaphoreType.DMA((sections - 1,))],
-        name="pick_weights",
         compiler_params=pltpu.CompilerParams(vmem_limit_bytes=52 << 20),
     )(halved)
     fetched = [None] * sections
     for mask in range(sections - 1, 0, -1):
-        fetched[mask] = swapped(picked[mask - 1], "section", mask)
+        fetched[mask] = swapped(picked[mask - 1], SECTION, mask)
 
     wide = jax.ShapeDtypeStruct((2, tokens, 2 * width), jnp.bfloat16)
     slim = jax.ShapeDtypeStruct((2, tokens, width), jnp.bfloat16)
@@ -458,7 +458,6 @@
         out_specs=[memory] * (2 * steps),
         out_shape=[wide] * steps + [slim] * steps,
         scratch_shapes=[pltpu.SemaphoreType.DMA((3 * steps,))],
-        name="pick_columns",
         compiler_params=pltpu.CompilerParams(vmem_limit_bytes=52 << 20),
     )(inputs, cot)
     near_columns, near_halves = [picked[0]], [picked[steps]]
@@ -474,18 +473,17 @@
             out_specs=[memory] * len(which),
             out_shape=[jax.ShapeDtypeStruct((steps,) + shape, jnp.bfloat16)] * len(which),
             scratch_shapes=[pltpu.SemaphoreType.DMA((steps * len(which),))],
-            name="pick_moving",
             compiler_params=pltpu.CompilerParams(vmem_limit_bytes=8 << 20),
         )(*sources)
 
     sideways = moving(near_halves, (0, 1), (tokens, width))
     near_aside, far_aside, far_columns, far_halves = [], [], [], []
     for way in range(2):
-        near_aside.append(swapped(sideways[way], "section", asides[way]))
+        near_aside.append(swapped(sideways[way], SECTION, asides[way]))
     for way in range(2):
         far_aside.append(swapped(near_aside[way], "dp", 1))
-    for distance in range(steps):
-        far_halves.append(swapped(near_halves[distance], "dp", 1))
+    for way in range(2):
+        far_halves.append(swapped(sideways[way], "dp", 1))
 
     lengths = valid_lengths
     blocks = 4
@@ -504,7 +502,6 @@
         out_specs=[pl.BlockSpec((rows * tokens, head), lambda i: (0, 0)) for rows in (3, 5)],
         out_shape=[jax.ShapeDtypeStruct((rows * tokens, head), jnp.bfloat16) for rows in (3, 5)],
         scratch_shapes=[pltpu.VMEM((2, 2, tokens, head), jnp.float32)],
-        name="heads",
         compiler_params=pltpu.CompilerParams(vmem_limit_bytes=12 << 20),
     )(
         lengths,
@@ -517,7 +514,7 @@
 
     tails = [full]
     for mask in range(1, sections):
-        tails.append(swapped(full if mask == sections - 1 else short, "section", mask))
+        tails.append(swapped(full if mask == sections - 1 else short, SECTION, mask))
 
     outputs, own_values, own_slice = pl.pallas_call(
         pick_outputs,
@@ -529,7 +526,6 @@
             jax.ShapeDtypeStruct((width, head), jnp.bfloat16),
         ],
         scratch_shapes=[pltpu.SemaphoreType.DMA((3,))],
-        name="pick_outputs",
         compiler_params=pltpu.CompilerParams(vmem_limit_bytes=8 << 20),
     )(halved, held)
     products = pl.pallas_call(
@@ -537,7 +533,6 @@
         in_specs=[memory] * sections,
         out_specs=memory,
         out_shape=jax.ShapeDtypeStruct((sections - 1, head, head), jnp.float32),
-        name="products",
         compiler_params=pltpu.CompilerParams(vmem_limit_bytes=8 << 20),
     )(outputs, *fetched[1:])
     far_products = swapped(products, "dp", 1)
@@ -550,24 +545,23 @@
         in_specs=[memory] * 2,
         out_specs=memory,
         out_shape=jax.ShapeDtypeStruct((sections - 1, head, head), jnp.bfloat16),
-        name="pack",
         compiler_params=pltpu.CompilerParams(vmem_limit_bytes=8 << 20),
     )(products, far_products)
     parts = [packed]
     for mask in range(1, sections):
-        parts.append(swapped(packed, "section", mask))
+        parts.append(swapped(packed, SECTION, mask))
 
     (upward,) = moving(near_columns, (1,), (tokens, 2 * width))
-    near_mirror = swapped(upward, "section", sections - 1)
+    near_mirror = swapped(upward, SECTION, sections - 1)
     far_mirror = swapped(near_mirror, "dp", 1)
-    for distance in range(steps):
-        far_columns.append(swapped(near_columns[distance], "dp", 1))
+    (downward,) = moving(near_columns, (0,), (tokens, 2 * width))
+    far_columns = swapped(downward, "dp", 1)
     lent = [own_slice]
     for mask in range(1, sections):
         route = [
             (i, i ^ mask) for i in range(sections) if i ^ mask < i < sections - 1 - (i ^ mask)
         ]
-        lent.append(lax.ppermute(own_slice, "section", route) if route else own_slice)
+        lent.append(lax.ppermute(own_slice, SECTION, route) if route else own_slice)
 
     sent, steer, own = pl.pallas_call(
         functools.partial(chain_kernel, sections, tokens, head),
@@ -578,7 +572,6 @@
             jax.ShapeDtypeStruct((2 * tokens, (sections - 1) * head), jnp.bfloat16),
             jax.ShapeDtypeStruct((2, tokens, head), jnp.bfloat16),
         ),
-        name="chain",
         compiler_params=pltpu.CompilerParams(vmem_limit_bytes=8 << 20),
     )(*parts, *tails)
 
@@ -601,14 +594,13 @@
         + [pl.BlockSpec((1, width, head), lambda i: (i, 0, 0))] * (2 * sections - 2),
         out_specs=pl.BlockSpec((2, tokens, 2 * width), lambda i: (0, 0, i)),
         out_shape=jax.ShapeDtypeStruct((2, tokens, model_width), jnp.bfloat16),
-        name="input_side",
         compiler_params=pltpu.CompilerParams(vmem_limit_bytes=12 << 20),
     )(cot, steer, own, own_values, *fetched[1:], *lent_back[1:])
 
     every = replicas * tokens
     weight_grads = pl.pallas_call(
         functools.partial(weight_kernel, sections, steps, tokens),
-        in_specs=[memory] * (6 * steps + 2 * sections + 5),
+        in_specs=[memory] * (2 * steps + 2 * sections + 11),
         out_specs=memory,
         out_shape=jax.ShapeDtypeStruct((2, width, head), jnp.float32),
         scratch_shapes=[
@@ -616,12 +608,11 @@
             pltpu.VMEM((2 * every, width), jnp.bfloat16),
             pltpu.VMEM((2, every, (sections - 1) * head), jnp.bfloat16),
         ],
-        name="weight_side",
         compiler_params=pltpu.CompilerParams(vmem_limit_bytes=20 << 20),
     )(
-        *near_columns,
-        *far_columns,
-        *near_halves,
+        downward,
+        far_columns,
+        *sideways,
         *far_halves,
         near_mirror,
         far_mirror,
@@ -639,7 +630,7 @@
 
 def shards(*operands):
     layer_inputs, held_weights = operands[0], operands[3]
-    sections = lax.axis_size("section")
+    sections = lax.axis_size(SECTION)
     replicas = lax.axis_size("dp")
     seqs, length, model_width = layer_inputs.shape[2:]
     head = held_weights.shape[-1]
@@ -657,13 +648,13 @@
         shards,
         mesh=mesh,
         in_specs=(
-            P("section", None, "dp", None, None),
-            P("section", None, "dp", None, None),
-            P("section", None, "dp", None, None),
-            P("section", None, None, None, None),
+            P(SECTION, None, "dp", None, None),
+            P(SECTION, None, "dp", None, None),
+            P(SECTION, None, "dp", None, None),
+            P(SECTION, None, None, None, None),
             P(None, "dp", None, None),
             P(None, "dp"),
         ),
-        out_specs=(P("section", None, "dp", None, None), P("section", None, "dp", None)),
+        out_specs=(P(SECTION, None, "dp", None, None), P(SECTION, None, "dp", None)),
         check_vma=False,
     )

time: 123 us -> 135 us (1.098)
  waiting for transfers between devices: 65.1 us -> 73.9 us
  starting transfers between devices: 32.5 us -> 35.1 us
    ppermute x2, waiting for transfers between devices: 1.75 us -> 22.1 us  [gathered(): lent.append(lax.ppermute(own_slice, SECTION, route) if route else own_slice)]
    ppermute x31 -> x26, waiting for transfers between devices: 29.2 us -> 22.2 us  [swapped(): lax.ppermute(block, axis, [(i, i ^ mask) for i in range(lax.axis_size(axi...]
    ppermute x9, waiting for transfers between devices: 34.2 us -> 29.6 us  [shifted(): lax.ppermute(block, 'dp', [(i, (i + 2 * distance) % count) for i in range...]
    ppermute x9, starting transfers between devices: 14.1 us -> 16.5 us  [shifted(): lax.ppermute(block, 'dp', [(i, (i + 2 * distance) % count) for i in range...]
    ppermute x31 -> x26, starting transfers between devices: 15.9 us -> 16 us  [swapped(): lax.ppermute(block, axis, [(i, i ^ mask) for i in range(lax.axis_size(axi...]
  transfers between devices with their start and end apart: 42 -> 37, of which waited for: 15 -> 12; matrix products, arithmetic and copies ran while one was open for 0% -> 0% of each run, Pallas kernels for 8% -> 10%
where the time goes in v4:
time: 135 us
  waiting for transfers between devices  73.9 us (55%)
  starting transfers between devices  35.1 us (26%)
  Pallas kernels  18.2 us (13%)
  local copies, waits for them, and re-layouts  6.84 us (5%)
    ppermute x9, waiting for transfers between devices, shifted(): lax.ppermute(block, 'dp', [(i, (i + 2 * distance) % count) for i in range...  29.6 us
    ppermute x26, waiting for transfers between devices, swapped(): lax.ppermute(block, axis, [(i, i ^ mask) for i in range(lax.axis_size(axi...  22.2 us
    ppermute x2, waiting for transfers between devices, gathered(): lent.append(lax.ppermute(own_slice, SECTION, route) if route else own_slice)  22.1 us
    ppermute x9, starting transfers between devices, shifted(): lax.ppermute(block, 'dp', [(i, (i + 2 * distance) % count) for i in range...  16.5 us
    ppermute x26, starting transfers between devices, swapped(): lax.ppermute(block, axis, [(i, i ^ mask) for i in range(lax.axis_size(axi...  16 us
    unnamed x16, local copies, waits for them, and re-layouts  6.84 us
    pallas_call x1, Pallas kernels, gathered(): pl.pallas_call(functools.partial(heads_kernel, length), grid=(blocks,), i...  4.57 us
    pallas_call x1, Pallas kernels, gathered(): pl.pallas_call(functools.partial(input_kernel, sections, tokens), grid=(s...  3.18 us
  transfers between devices with their start and end apart: 37, of which 12 were waited for; matrix products, arithmetic and copies ran while one was open for 0% of the time, Pallas kernels for 10%

profile of v4, /device:TPU:0, one launch (start us, length us, event | category | flops | bytes accessed | tf_op | source)
XLA Modules:
  0.0 134.9 jit_solution(12303871144671085485)
XLA Ops:
  0.6 1.5 %shard_map.84 = (bf16[2,64,1024]{2,1,0:T(8,128)(2,1)S(1)}, bf16[2,64,1024]{2,1,0:T(8,128)(2,1)S(1)}, bf16[2,64,1024]{2,1,0:T(8,128)(2,1)S(1)}, bf16[2,64,1024]{2...) custom-call(bf16[2,64,4096]{2,1,0:T(8,128)(2,1)} %bitcast.15, ...), custom_call_target="tpu_custom_call" | custom-call | tf_op jit(solution)/shard_map/pallas_call | solution.py:455
  2.1 3.1 %collective-permute-start.17 = (bf16[2,64,512]{2,1,0:T(8,128)(2,1)S(1)}, bf16[2,64,512]{2,1,0:T(8,128)(2,1)S(1)}, u32[]{:S(2)}, u32[]{:S(2)}) collective-permute-start(bf16[2,64,512]{2,1,0:T(8,128)(2,1)S(1)} %get-tuple-element.37), channel_id=1, source_target_pairs={{0,8},{4,12},{8,16},{12,20},{16,24},{20,28},{24,0},{28,4},{1,9},{5... | collective-permute-start | bytes 393224 | tf_op jit(solution)/shard_map/ppermute | solution.py:162
  5.2 2.2 %copy-done = bf16[1,2,2,4096,128]{4,3,2,1,0:T(8,128)(2,1)S(1)} copy-done((bf16[1,2,2,4096,128]{4,3,2,1,0:T(8,128)(2,1)S(1)}, bf16[1,2,2,4096,128]{4,3,2,1,0:T(8,128)(2,1)}, u32[]{:S(2)}) %copy-start) | copy-done | bytes 4194328
  7.4 1.2 copy-done.2
  8.6 1.2 copy-done.4
  12.1 4.6 %shard_map.81 = (bf16[192,128]{1,0:T(8,128)(2,1)S(1)}, bf16[320,128]{1,0:T(8,128)(2,1)S(1)}) custom-call(s32[2,2]{1,0:T(2,128)S(1)} %copy-done.7, bf16[2,64,4096]{2,1,0:T(8,128)(2,1)S(1)} %bitcast.16, bf16[2,64,4096]{2,1,0:T(8,128)(2,1)S(1)} %bitcast.13, bf16[2,2,4096,128]{3,2,1,0:T(8,128)(2,1)S(1)} %bitcast.9, bf16[2,64,128]{2,1,0:T(8,128)(2,1)S(1)} %bitcast.17, ...), custom_call_target="tpu_custom_call" | custom-call | tf_op jit(solution)/shard_map/pallas_call | solution.py:491
  16.6 2.5 %collective-permute-start.9 = (bf16[320,128]{1,0:T(8,128)(2,1)S(1)}, bf16[320,128]{1,0:T(8,128)(2,1)S(1)}, u32[]{:S(2)}, u32[]{:S(2)}) collective-permute-start(bf16[320,128]{1,0:T(8,128)(2,1)S(1)} %get-tuple-element.27.refs_4_), channel_id=1, source_target_pairs={{0,3},{1,2},{2,1},{3,0},{4,7},{5,6},{6,5},{7,4},{8,11},{9,10},{10,... | collective-permute-start | bytes 245768 | tf_op jit(solution)/shard_map/ppermute | solution.py:157
  19.1 2.6 %collective-permute-start.18 = (bf16[2,64,512]{2,1,0:T(8,128)(2,1)S(1)}, bf16[2,64,512]{2,1,0:T(8,128)(2,1)S(1)}, u32[]{:S(2)}, u32[]{:S(2)}) collective-permute-start(bf16[2,64,512]{2,1,0:T(8,128)(2,1)S(1)} %get-tuple-element.38), channel_id=1, source_target_pairs={{0,16},{4,20},{8,24},{12,28},{16,0},{20,4},{24,8},{28,12},{1,17},{... | collective-permute-start | bytes 393224 | tf_op jit(solution)/shard_map/ppermute | solution.py:162
  22.8 3.0 %collective-permute-done.7.refs_5_ = bf16[192,128]{1,0:T(8,128)(2,1)S(1)} collective-permute-done((bf16[192,128]{1,0:T(8,128)(2,1)S(1)}, bf16[192,128]{1,0:T(8,128)(2,1)S(1)}, u32[]{:S(2)}, u32[]{:S(2)}) %collective-permute-start.7) | collective-permute-done | bytes 49184 | tf_op jit(solution)/shard_map/ppermute | solution.py:157
  25.8 1.3 collective-permute-start.19
  27.2 1.4 %shard_map.78 = (bf16[4,512,128]{2,1,0:T(8,128)(2,1)S(1)}, bf16[4,512,128]{2,1,0:T(8,128)(2,1)S(1)}, bf16[4,512,128]{2,1,0:T(8,128)(2,1)S(1)}) custom-call(bf16[2,2,4,2,512,128]{5,4,3,2,1,0:T(8,128)(2,1)} %bitcast.8), custom_call_target="tpu_custom_call" | custom-call | tf_op jit(solution)/shard_map/pallas_call | solution.py:441
  29.7 2.4 %collective-permute-start.2 = (bf16[4,512,128]{2,1,0:T(8,128)(2,1)S(1)}, bf16[4,512,128]{2,1,0:T(8,128)(2,1)S(1)}, u32[]{:S(2)}, u32[]{:S(2)}) collective-permute-start(bf16[4,512,128]{2,1,0:T(8,128)(2,1)S(1)} %get-tuple-element.26), channel_id=1, source_target_pairs={{0,3},{1,2},{2,1},{3,0},{4,7},{5,6},{6,5},{7,4},{8,11},{9,10},{10,... | collective-permute-start | bytes 1572872 | tf_op jit(solution)/shard_map/ppermute | solution.py:157
  33.3 1.4 %collective-permute-start.35 = (bf16[512,128]{1,0:T(8,128)(2,1)S(1)}, bf16[512,128]{1,0:T(8,128)(2,1)S(1)}, u32[]{:S(2)}, u32[]{:S(2)}) collective-permute-start(bf16[512,128]{1,0:T(8,128)(2,1)S(1)} %get-tuple-element.43.refs_20_.refs_26_), channel_id=1, source_target_pairs={{1,0},{5,4},{9,8},{13,12},{17,16},{21,20},{25,24},{29,28}} | collective-permute-start | bytes 393224 | tf_op jit(solution)/shard_map/ppermute | solution.py:564
  34.7 19.5 %collective-permute-done.35.refs_24_ = bf16[512,128]{1,0:T(8,128)(2,1)S(1)} collective-permute-done((bf16[512,128]{1,0:T(8,128)(2,1)S(1)}, bf16[512,128]{1,0:T(8,128)(2,1)S(1)}, u32[]{:S(2)}, u32[]{:S(2)}) %collective-permute-start.35) | collective-permute-done | bytes 131104 | tf_op jit(solution)/shard_map/ppermute | solution.py:564
  54.6 2.6 %collective-permute-start.15 = (bf16[2,64,1024]{2,1,0:T(8,128)(2,1)S(1)}, bf16[2,64,1024]{2,1,0:T(8,128)(2,1)S(1)}, u32[]{:S(2)}, u32[]{:S(2)}) collective-permute-start(bf16[2,64,1024]{2,1,0:T(8,128)(2,1)S(1)} %get-tuple-element.35), channel_id=1, source_target_pairs={{0,24},{4,28},{8,0},{12,4},{16,8},{20,12},{24,16},{28,20},{1,25},{... | collective-permute-start | bytes 786440 | tf_op jit(solution)/shard_map/ppermute | solution.py:162
  57.9 9.1 %collective-permute-done.14.refs_2_ = bf16[2,64,1024]{2,1,0:T(8,128)(2,1)S(1)} collective-permute-done((bf16[2,64,1024]{2,1,0:T(8,128)(2,1)S(1)}, bf16[2,64,1024]{2,1,0:T(8,128)(2,1)S(1)}, u32[]{:S(2)}, u32[]{:S(2)}) %collective-permute-start.14) | collective-permute-done | bytes 262176 | tf_op jit(solution)/shard_map/ppermute | solution.py:162
  67.1 1.3 collective-permute-start.36
  68.5 2.7 %collective-permute-start.24 = (bf16[4,64,512]{2,1,0:T(8,128)(2,1)S(1)}, bf16[4,64,512]{2,1,0:T(8,128)(2,1)S(1)}, u32[]{:S(2)}, u32[]{:S(2)}) collective-permute-start(bf16[4,64,512]{2,1,0:T(8,128)(2,1)S(1)} %get-tuple-element.40.refs_2_), channel_id=1, source_target_pairs={{0,2},{1,3},{2,0},{3,1},{4,6},{5,7},{6,4},{7,5},{8,10},{9,11},{10,... | collective-permute-start | bytes 786440 | tf_op jit(solution)/shard_map/ppermute | solution.py:157
  72.7 2.6 %collective-permute-done.36.refs_25_ = bf16[512,128]{1,0:T(8,128)(2,1)S(1)} collective-permute-done((bf16[512,128]{1,0:T(8,128)(2,1)S(1)}, bf16[512,128]{1,0:T(8,128)(2,1)S(1)}, u32[]{:S(2)}, u32[]{:S(2)}) %collective-permute-start.36) | collective-permute-done | bytes 131104 | tf_op jit(solution)/shard_map/ppermute | solution.py:564
  75.8 3.6 %collective-permute-done.24.refs_8_ = bf16[4,64,512]{2,1,0:T(8,128)(2,1)S(1)} collective-permute-done((bf16[4,64,512]{2,1,0:T(8,128)(2,1)S(1)}, bf16[4,64,512]{2,1,0:T(8,128)(2,1)S(1)}, u32[]{:S(2)}, u32[]{:S(2)}) %collective-permute-start.24) | collective-permute-done | bytes 262176 | tf_op jit(solution)/shard_map/ppermute | solution.py:157
  80.8 1.8 %collective-permute-start.4 = (bf16[3,128,128]{2,1,0:T(8,128)(2,1)S(1)}, bf16[3,128,128]{2,1,0:T(8,128)(2,1)S(1)}, u32[]{:S(2)}, u32[]{:S(2)}) collective-permute-start(bf16[3,128,128]{2,1,0:T(8,128)(2,1)S(1)} %shard_map.80.refs_0_), channel_id=1, source_target_pairs={{0,1},{1,0},{2,3},{3,2},{4,5},{5,4},{6,7},{7,6},{8,9},{9,8},{10,11... | collective-permute-start | bytes 294920 | tf_op jit(solution)/shard_map/ppermute | solution.py:157
  82.7 1.7 %collective-permute-start.5 = (bf16[3,128,128]{2,1,0:T(8,128)(2,1)S(1)}, bf16[3,128,128]{2,1,0:T(8,128)(2,1)S(1)}, u32[]{:S(2)}, u32[]{:S(2)}) collective-permute-start(bf16[3,128,128]{2,1,0:T(8,128)(2,1)S(1)} %shard_map.80.refs_0_), channel_id=1, source_target_pairs={{0,2},{1,3},{2,0},{3,1},{4,6},{5,7},{6,4},{7,5},{8,10},{9,11},{10,... | collective-permute-start | bytes 294920 | tf_op jit(solution)/shard_map/ppermute | solution.py:157
  84.4 13.1 %collective-permute-done.4.refs_1_ = bf16[3,128,128]{2,1,0:T(8,128)(2,1)S(1)} collective-permute-done((bf16[3,128,128]{2,1,0:T(8,128)(2,1)S(1)}, bf16[3,128,128]{2,1,0:T(8,128)(2,1)S(1)}, u32[]{:S(2)}, u32[]{:S(2)}) %collective-permute-start.4) | collective-permute-done | bytes 98336 | tf_op jit(solution)/shard_map/ppermute | solution.py:157
  98.5 1.3 collective-permute-done.6.refs_3_
  99.8 1.6 %shard_map.82 = (bf16[2,5,64,128]{3,2,1,0:T(8,128)(2,1)S(1)}, bf16[128,384]{1,0:T(8,128)(2,1)S(1)}, bf16[2,64,128]{2,1,0:T(8,128)(2,1)S(1)}) custom-call(bf16[3,128,128]{2,1,0:T(8,128)(2,1)S(1)} %shard_map.80.refs_0_, bf16[3,128,128]{2,1,0:T(8,128)(2,1)S(1)} %collective-permute-done.4.refs_1_, bf16[3,128,128]{2,1,0:T(8,128)(2,1)S(1)} %collective-permute-done.5.refs_2_, ...), custom_call_target="tpu_custom_call" | custom-call | tf_op jit(solution)/shard_map/pallas_call | solution.py:566
  101.4 3.4 %collective-permute-start.28 = (bf16[2,5,64,128]{3,2,1,0:T(8,128)(2,1)S(1)}, bf16[2,5,64,128]{3,2,1,0:T(8,128)(2,1)S(1)}, u32[]{:S(2)}, u32[]{:S(2)}) collective-permute-start(bf16[2,5,64,128]{3,2,1,0:T(8,128)(2,1)S(1)} %get-tuple-element.42.refs_12_), channel_id=1, source_target_pairs={{0,8},{4,12},{8,16},{12,20},{16,24},{20,28},{24,0},{28,4},{1,9},{5... | collective-permute-start | bytes 491528 | tf_op jit(solution)/shard_map/ppermute | solution.py:162
  105.0 7.5 %collective-permute-done.28.refs_13_ = bf16[2,5,64,128]{3,2,1,0:T(8,128)(2,1)S(1)} collective-permute-done((bf16[2,5,64,128]{3,2,1,0:T(8,128)(2,1)S(1)}, bf16[2,5,64,128]{3,2,1,0:T(8,128)(2,1)S(1)}, u32[]{:S(2)}, u32[]{:S(2)}) %collective-permute-start.28) | collective-permute-done | bytes 163872 | tf_op jit(solution)/shard_map/ppermute | solution.py:162
  112.5 9.3 %collective-permute-done.29.refs_14_ = bf16[2,5,64,128]{3,2,1,0:T(8,128)(2,1)S(1)} collective-permute-done((bf16[2,5,64,128]{3,2,1,0:T(8,128)(2,1)S(1)}, bf16[2,5,64,128]{3,2,1,0:T(8,128)(2,1)S(1)}, u32[]{:S(2)}, u32[]{:S(2)}) %collective-permute-start.29) | collective-permute-done | bytes 163872 | tf_op jit(solution)/shard_map/ppermute | solution.py:162
  121.8 2.4 %collective-permute-start.30 = (bf16[2,5,64,128]{3,2,1,0:T(8,128)(2,1)S(1)}, bf16[2,5,64,128]{3,2,1,0:T(8,128)(2,1)S(1)}, u32[]{:S(2)}, u32[]{:S(2)}) collective-permute-start(bf16[2,5,64,128]{3,2,1,0:T(8,128)(2,1)S(1)} %get-tuple-element.42.refs_12_), channel_id=1, source_target_pairs={{0,24},{4,28},{8,0},{12,4},{16,8},{20,12},{24,16},{28,20},{1,25},{... | collective-permute-start | bytes 491528 | tf_op jit(solution)/shard_map/ppermute | solution.py:162
  124.1 3.8 %collective-permute-done.30.refs_15_ = bf16[2,5,64,128]{3,2,1,0:T(8,128)(2,1)S(1)} collective-permute-done((bf16[2,5,64,128]{3,2,1,0:T(8,128)(2,1)S(1)}, bf16[2,5,64,128]{3,2,1,0:T(8,128)(2,1)S(1)}, u32[]{:S(2)}, u32[]{:S(2)}) %collective-permute-start.30) | collective-permute-done | bytes 163872 | tf_op jit(solution)/shard_map/ppermute | solution.py:162
  128.9 3.2 %shard_map.83 = bf16[2,64,4096]{2,1,0:T(8,128)(2,1)} custom-call(bf16[2,64,4096]{2,1,0:T(8,128)(2,1)S(1)} %bitcast.14, bf16[128,384]{1,0:T(8,128)(2,1)S(1)} %get-tuple-element.29.steer, bf16[2,64,128]{2,1,0:T(8,128)(2,1)S(1)} %get-tuple-element.30.own, bf16[2,4096,128]{2,1,0:T(8,128)(2,1)S(1)} %get-tuple-element.31.held, ...), custom_call_target="tpu_custom_call" | custom-call | tf_op jit(solution)/shard_map/pallas_call | solution.py:585
  132.1 2.8 %shard_map.88 = f32[2,512,128]{2,1,0:T(8,128)} custom-call(bf16[4,64,1024]{2,1,0:T(8,128)(2,1)S(1)} %shard_map.85.refs_0_, bf16[4,64,1024]{2,1,0:T(8,128)(2,1)S(1)} %collective-permute-done.16.refs_1_, bf16[4,64,512]{2,1,0:T(8,128)(2,1)S(1)} %get-tuple-element.40.refs_2_, bf16[4,64,512]{2,1,0:T(8,128)(2,1)S(1)} %get-tuple-element.41.refs_3_, ...), custom_call_target="tpu_custom_call" | custom-call | tf_op jit(solution)/shard_map/pallas_call | solution.py:601
  (70 shorter events, 12.3 us)
Async XLA Ops:
  2.1 27.6 %collective-permute-start.17 = (bf16[2,64,512]{2,1,0:T(8,128)(2,1)S(1)}, bf16[2,64,512]{2,1,0:T(8,128)(2,1)S(1)}, u32[]{:S(2)}, u32[]{:S(2)}) collective-permute-start(bf16[2,64,512]{2,1,0:T(8,128)(2,1)S(1)} %get-tuple-element.37), channel_id=1, source_target_pairs={{0,8},{4,12},{8,16},{12,20},{16,24},{20,28},{24,0},{28,4},{1,9},{5... | collective-permute-start | bytes 393224 | tf_op jit(solution)/shard_map/ppermute | solution.py:162
  16.6 12.5 %collective-permute-start.9 = (bf16[320,128]{1,0:T(8,128)(2,1)S(1)}, bf16[320,128]{1,0:T(8,128)(2,1)S(1)}, u32[]{:S(2)}, u32[]{:S(2)}) collective-permute-start(bf16[320,128]{1,0:T(8,128)(2,1)S(1)} %get-tuple-element.27.refs_4_), channel_id=1, source_target_pairs={{0,3},{1,2},{2,1},{3,0},{4,7},{5,6},{6,5},{7,4},{8,11},{9,10},{10,... | collective-permute-start | bytes 245768 | tf_op jit(solution)/shard_map/ppermute | solution.py:157
  19.1 13.0 %collective-permute-start.18 = (bf16[2,64,512]{2,1,0:T(8,128)(2,1)S(1)}, bf16[2,64,512]{2,1,0:T(8,128)(2,1)S(1)}, u32[]{:S(2)}, u32[]{:S(2)}) collective-permute-start(bf16[2,64,512]{2,1,0:T(8,128)(2,1)S(1)} %get-tuple-element.38), channel_id=1, source_target_pairs={{0,16},{4,20},{8,24},{12,28},{16,0},{20,4},{24,8},{28,12},{1,17},{... | collective-permute-start | bytes 393224 | tf_op jit(solution)/shard_map/ppermute | solution.py:162
  22.3 6.3 %collective-permute-start.8 = (bf16[192,128]{1,0:T(8,128)(2,1)S(1)}, bf16[192,128]{1,0:T(8,128)(2,1)S(1)}, u32[]{:S(2)}, u32[]{:S(2)}) collective-permute-start(bf16[192,128]{1,0:T(8,128)(2,1)S(1)} %get-tuple-element.28), channel_id=1, source_target_pairs={{0,2},{1,3},{2,0},{3,1},{4,6},{5,7},{6,4},{7,5},{8,10},{9,11},{10,... | collective-permute-start | bytes 147464 | tf_op jit(solution)/shard_map/ppermute | solution.py:157
  25.8 7.5 %collective-permute-start.19 = (bf16[2,64,512]{2,1,0:T(8,128)(2,1)S(1)}, bf16[2,64,512]{2,1,0:T(8,128)(2,1)S(1)}, u32[]{:S(2)}, u32[]{:S(2)}) collective-permute-start(bf16[2,64,512]{2,1,0:T(8,128)(2,1)S(1)} %get-tuple-element.39), channel_id=1, source_target_pairs={{0,24},{4,28},{8,0},{12,4},{16,8},{20,12},{24,16},{28,20},{1,25},{... | collective-permute-start | bytes 393224 | tf_op jit(solution)/shard_map/ppermute | solution.py:162
  28.6 39.8 %collective-permute-start = (bf16[4,512,128]{2,1,0:T(8,128)(2,1)S(1)}, bf16[4,512,128]{2,1,0:T(8,128)(2,1)S(1)}, u32[]{:S(2)}, u32[]{:S(2)}) collective-permute-start(bf16[4,512,128]{2,1,0:T(8,128)(2,1)S(1)} %get-tuple-element.24), channel_id=1, source_target_pairs={{0,1},{1,0},{2,3},{3,2},{4,5},{5,4},{6,7},{7,6},{8,9},{9,8},{10,11... | collective-permute-start | bytes 1572872 | tf_op jit(solution)/shard_map/ppermute | solution.py:157
  29.2 39.3 %collective-permute-start.1 = (bf16[4,512,128]{2,1,0:T(8,128)(2,1)S(1)}, bf16[4,512,128]{2,1,0:T(8,128)(2,1)S(1)}, u32[]{:S(2)}, u32[]{:S(2)}) collective-permute-start(bf16[4,512,128]{2,1,0:T(8,128)(2,1)S(1)} %get-tuple-element.25), channel_id=1, source_target_pairs={{0,2},{1,3},{2,0},{3,1},{4,6},{5,7},{6,4},{7,5},{8,10},{9,11},{10,... | collective-permute-start | bytes 1572872 | tf_op jit(solution)/shard_map/ppermute | solution.py:157
  29.7 41.4 %collective-permute-start.2 = (bf16[4,512,128]{2,1,0:T(8,128)(2,1)S(1)}, bf16[4,512,128]{2,1,0:T(8,128)(2,1)S(1)}, u32[]{:S(2)}, u32[]{:S(2)}) collective-permute-start(bf16[4,512,128]{2,1,0:T(8,128)(2,1)S(1)} %get-tuple-element.26), channel_id=1, source_target_pairs={{0,3},{1,2},{2,1},{3,0},{4,7},{5,6},{6,5},{7,4},{8,11},{9,10},{10,... | collective-permute-start | bytes 1572872 | tf_op jit(solution)/shard_map/ppermute | solution.py:157
  32.2 22.4 %collective-permute-start.13 = (bf16[2,64,1024]{2,1,0:T(8,128)(2,1)S(1)}, bf16[2,64,1024]{2,1,0:T(8,128)(2,1)S(1)}, u32[]{:S(2)}, u32[]{:S(2)}) collective-permute-start(bf16[2,64,1024]{2,1,0:T(8,128)(2,1)S(1)} %get-tuple-element.33), channel_id=1, source_target_pairs={{0,8},{4,12},{8,16},{12,20},{16,24},{20,28},{24,0},{28,4},{1,9},{5... | collective-permute-start | bytes 786440 | tf_op jit(solution)/shard_map/ppermute | solution.py:162
  33.3 20.9 %collective-permute-start.35 = (bf16[512,128]{1,0:T(8,128)(2,1)S(1)}, bf16[512,128]{1,0:T(8,128)(2,1)S(1)}, u32[]{:S(2)}, u32[]{:S(2)}) collective-permute-start(bf16[512,128]{1,0:T(8,128)(2,1)S(1)} %get-tuple-element.43.refs_20_.refs_26_), channel_id=1, source_target_pairs={{1,0},{5,4},{9,8},{13,12},{17,16},{21,20},{25,24},{29,28}} | collective-permute-start | bytes 393224 | tf_op jit(solution)/shard_map/ppermute | solution.py:564
  54.2 12.9 %collective-permute-start.14 = (bf16[2,64,1024]{2,1,0:T(8,128)(2,1)S(1)}, bf16[2,64,1024]{2,1,0:T(8,128)(2,1)S(1)}, u32[]{:S(2)}, u32[]{:S(2)}) collective-permute-start(bf16[2,64,1024]{2,1,0:T(8,128)(2,1)S(1)} %get-tuple-element.34), channel_id=1, source_target_pairs={{0,16},{4,20},{8,24},{12,28},{16,0},{20,4},{24,8},{28,12},{1,17},{... | collective-permute-start | bytes 786440 | tf_op jit(solution)/shard_map/ppermute | solution.py:162
  54.6 17.2 %collective-permute-start.15 = (bf16[2,64,1024]{2,1,0:T(8,128)(2,1)S(1)}, bf16[2,64,1024]{2,1,0:T(8,128)(2,1)S(1)}, u32[]{:S(2)}, u32[]{:S(2)}) collective-permute-start(bf16[2,64,1024]{2,1,0:T(8,128)(2,1)S(1)} %get-tuple-element.35), channel_id=1, source_target_pairs={{0,24},{4,28},{8,0},{12,4},{16,8},{20,12},{24,16},{28,20},{1,25},{... | collective-permute-start | bytes 786440 | tf_op jit(solution)/shard_map/ppermute | solution.py:162
  67.1 8.2 %collective-permute-start.36 = (bf16[512,128]{1,0:T(8,128)(2,1)S(1)}, bf16[512,128]{1,0:T(8,128)(2,1)S(1)}, u32[]{:S(2)}, u32[]{:S(2)}) collective-permute-start(bf16[512,128]{1,0:T(8,128)(2,1)S(1)} %get-tuple-element.43.refs_20_.refs_26_), channel_id=1, source_target_pairs={{2,0},{6,4},{10,8},{14,12},{18,16},{22,20},{26,24},{30,28}} | collective-permute-start | bytes 393224 | tf_op jit(solution)/shard_map/ppermute | solution.py:564
  68.4 7.0 %collective-permute-start.20 = (bf16[4,64,512]{2,1,0:T(8,128)(2,1)S(1)}, bf16[4,64,512]{2,1,0:T(8,128)(2,1)S(1)}, u32[]{:S(2)}, u32[]{:S(2)}) collective-permute-start(bf16[4,64,512]{2,1,0:T(8,128)(2,1)S(1)} %get-tuple-element.40.refs_2_), channel_id=1, source_target_pairs={{0,4},{4,0},{8,12},{12,8},{16,20},{20,16},{24,28},{28,24},{1,5},{5... | collective-permute-start | bytes 786440 | tf_op jit(solution)/shard_map/ppermute | solution.py:157
  68.5 11.0 %collective-permute-start.24 = (bf16[4,64,512]{2,1,0:T(8,128)(2,1)S(1)}, bf16[4,64,512]{2,1,0:T(8,128)(2,1)S(1)}, u32[]{:S(2)}, u32[]{:S(2)}) collective-permute-start(bf16[4,64,512]{2,1,0:T(8,128)(2,1)S(1)} %get-tuple-element.40.refs_2_), channel_id=1, source_target_pairs={{0,2},{1,3},{2,0},{3,1},{4,6},{5,7},{6,4},{7,5},{8,10},{9,11},{10,... | collective-permute-start | bytes 786440 | tf_op jit(solution)/shard_map/ppermute | solution.py:157
  71.2 8.4 %collective-permute-start.25 = (bf16[4,64,512]{2,1,0:T(8,128)(2,1)S(1)}, bf16[4,64,512]{2,1,0:T(8,128)(2,1)S(1)}, u32[]{:S(2)}, u32[]{:S(2)}) collective-permute-start(bf16[4,64,512]{2,1,0:T(8,128)(2,1)S(1)} %get-tuple-element.41.refs_3_), channel_id=1, source_target_pairs={{0,1},{1,0},{2,3},{3,2},{4,5},{5,4},{6,7},{7,6},{8,9},{9,8},{10,11... | collective-permute-start | bytes 786440 | tf_op jit(solution)/shard_map/ppermute | solution.py:157
  71.8 8.9 %collective-permute-start.3 = (f32[3,128,128]{2,1,0:T(8,128)S(1)}, f32[3,128,128]{2,1,0:T(8,128)S(1)}, u32[]{:S(2)}, u32[]{:S(2)}) collective-permute-start(f32[3,128,128]{2,1,0:T(8,128)S(1)} %shard_map.79.near), channel_id=1, source_target_pairs={{0,4},{4,0},{8,12},{12,8},{16,20},{20,16},{24,28},{28,24},{1,5},{5... | collective-permute-start | bytes 589832 | tf_op jit(solution)/shard_map/ppermute | solution.py:157
  75.3 26.1 %collective-permute-start.16 = (bf16[4,64,1024]{2,1,0:T(8,128)(2,1)S(1)}, bf16[4,64,1024]{2,1,0:T(8,128)(2,1)S(1)}, u32[]{:S(2)}, u32[]{:S(2)}) collective-permute-start(bf16[4,64,1024]{2,1,0:T(8,128)(2,1)S(1)} %shard_map.85.refs_0_), channel_id=1, source_target_pairs={{0,4},{4,0},{8,12},{12,8},{16,20},{20,16},{24,28},{28,24},{1,5},{5... | collective-permute-start | bytes 1572872 | tf_op jit(solution)/shard_map/ppermute | solution.py:157
  75.3 5.5 %collective-permute-start.21 = (bf16[4,64,512]{2,1,0:T(8,128)(2,1)S(1)}, bf16[4,64,512]{2,1,0:T(8,128)(2,1)S(1)}, u32[]{:S(2)}, u32[]{:S(2)}) collective-permute-start(bf16[4,64,512]{2,1,0:T(8,128)(2,1)S(1)} %get-tuple-element.41.refs_3_), channel_id=1, source_target_pairs={{0,4},{4,0},{8,12},{12,8},{16,20},{20,16},{24,28},{28,24},{1,5},{5... | collective-permute-start | bytes 786440 | tf_op jit(solution)/shard_map/ppermute | solution.py:157
  79.5 4.8 %collective-permute-start.27 = (bf16[4,64,512]{2,1,0:T(8,128)(2,1)S(1)}, bf16[4,64,512]{2,1,0:T(8,128)(2,1)S(1)}, u32[]{:S(2)}, u32[]{:S(2)}) collective-permute-start(bf16[4,64,512]{2,1,0:T(8,128)(2,1)S(1)} %collective-permute-done.25.refs_9_), channel_id=1, source_target_pairs={{0,4},{4,0},{8,12},{12,8},{16,20},{20,16},{24,28},{28,24},{1,5},{5... | collective-permute-start | bytes 786440 | tf_op jit(solution)/shard_map/ppermute | solution.py:157
  80.7 24.1 %collective-permute-start.22 = (bf16[4,64,1024]{2,1,0:T(8,128)(2,1)S(1)}, bf16[4,64,1024]{2,1,0:T(8,128)(2,1)S(1)}, u32[]{:S(2)}, u32[]{:S(2)}) collective-permute-start(bf16[4,64,1024]{2,1,0:T(8,128)(2,1)S(1)} %shard_map.87), channel_id=1, source_target_pairs={{0,3},{1,2},{2,1},{3,0},{4,7},{5,6},{6,5},{7,4},{8,11},{9,10},{10,... | collective-permute-start | bytes 1572872 | tf_op jit(solution)/shard_map/ppermute | solution.py:157
  80.8 16.7 %collective-permute-start.4 = (bf16[3,128,128]{2,1,0:T(8,128)(2,1)S(1)}, bf16[3,128,128]{2,1,0:T(8,128)(2,1)S(1)}, u32[]{:S(2)}, u32[]{:S(2)}) collective-permute-start(bf16[3,128,128]{2,1,0:T(8,128)(2,1)S(1)} %shard_map.80.refs_0_), channel_id=1, source_target_pairs={{0,1},{1,0},{2,3},{3,2},{4,5},{5,4},{6,7},{7,6},{8,9},{9,8},{10,11... | collective-permute-start | bytes 294920 | tf_op jit(solution)/shard_map/ppermute | solution.py:157
  82.7 15.9 %collective-permute-start.5 = (bf16[3,128,128]{2,1,0:T(8,128)(2,1)S(1)}, bf16[3,128,128]{2,1,0:T(8,128)(2,1)S(1)}, u32[]{:S(2)}, u32[]{:S(2)}) collective-permute-start(bf16[3,128,128]{2,1,0:T(8,128)(2,1)S(1)} %shard_map.80.refs_0_), channel_id=1, source_target_pairs={{0,2},{1,3},{2,0},{3,1},{4,6},{5,7},{6,4},{7,5},{8,10},{9,11},{10,... | collective-permute-start | bytes 294920 | tf_op jit(solution)/shard_map/ppermute | solution.py:157
  84.3 15.4 %collective-permute-start.6 = (bf16[3,128,128]{2,1,0:T(8,128)(2,1)S(1)}, bf16[3,128,128]{2,1,0:T(8,128)(2,1)S(1)}, u32[]{:S(2)}, u32[]{:S(2)}) collective-permute-start(bf16[3,128,128]{2,1,0:T(8,128)(2,1)S(1)} %shard_map.80.refs_0_), channel_id=1, source_target_pairs={{0,3},{1,2},{2,1},{3,0},{4,7},{5,6},{6,5},{7,4},{8,11},{9,10},{10,... | collective-permute-start | bytes 294920 | tf_op jit(solution)/shard_map/ppermute | solution.py:157
  97.5 30.4 %collective-permute-start.10 = (bf16[4,512,128]{2,1,0:T(8,128)(2,1)S(1)}, bf16[4,512,128]{2,1,0:T(8,128)(2,1)S(1)}, u32[]{:S(2)}, u32[]{:S(2)}) collective-permute-start(bf16[4,512,128]{2,1,0:T(8,128)(2,1)S(1)} %collective-permute-done.refs_0_.refs_21_), channel_id=1, source_target_pairs={{0,4},{4,0},{8,12},{12,8},{16,20},{20,16},{24,28},{28,24},{1,5},{5... | collective-permute-start | bytes 1572872 | tf_op jit(solution)/shard_map/ppermute | solution.py:157
  98.5 29.9 %collective-permute-start.11 = (bf16[4,512,128]{2,1,0:T(8,128)(2,1)S(1)}, bf16[4,512,128]{2,1,0:T(8,128)(2,1)S(1)}, u32[]{:S(2)}, u32[]{:S(2)}) collective-permute-start(bf16[4,512,128]{2,1,0:T(8,128)(2,1)S(1)} %collective-permute-done.1.refs_1_.refs_22_), channel_id=1, source_target_pairs={{0,4},{4,0},{8,12},{12,8},{16,20},{20,16},{24,28},{28,24},{1,5},{5... | collective-permute-start | bytes 1572872 | tf_op jit(solution)/shard_map/ppermute | solution.py:157
  99.8 28.7 %collective-permute-start.12 = (bf16[4,512,128]{2,1,0:T(8,128)(2,1)S(1)}, bf16[4,512,128]{2,1,0:T(8,128)(2,1)S(1)}, u32[]{:S(2)}, u32[]{:S(2)}) collective-permute-start(bf16[4,512,128]{2,1,0:T(8,128)(2,1)S(1)} %collective-permute-done.2.refs_2_.refs_23_), channel_id=1, source_target_pairs={{0,4},{4,0},{8,12},{12,8},{16,20},{20,16},{24,28},{28,24},{1,5},{5... | collective-permute-start | bytes 1572872 | tf_op jit(solution)/shard_map/ppermute | solution.py:157
  101.4 11.1 %collective-permute-start.28 = (bf16[2,5,64,128]{3,2,1,0:T(8,128)(2,1)S(1)}, bf16[2,5,64,128]{3,2,1,0:T(8,128)(2,1)S(1)}, u32[]{:S(2)}, u32[]{:S(2)}) collective-permute-start(bf16[2,5,64,128]{3,2,1,0:T(8,128)(2,1)S(1)} %get-tuple-element.42.refs_12_), channel_id=1, source_target_pairs={{0,8},{4,12},{8,16},{12,20},{16,24},{20,28},{24,0},{28,4},{1,9},{5... | collective-permute-start | bytes 491528 | tf_op jit(solution)/shard_map/ppermute | solution.py:162
  104.8 27.3 %collective-permute-start.23 = (bf16[4,64,1024]{2,1,0:T(8,128)(2,1)S(1)}, bf16[4,64,1024]{2,1,0:T(8,128)(2,1)S(1)}, u32[]{:S(2)}, u32[]{:S(2)}) collective-permute-start(bf16[4,64,1024]{2,1,0:T(8,128)(2,1)S(1)} %collective-permute-done.22.refs_6_), channel_id=1, source_target_pairs={{0,4},{4,0},{8,12},{12,8},{16,20},{20,16},{24,28},{28,24},{1,5},{5... | collective-permute-start | bytes 1572872 | tf_op jit(solution)/shard_map/ppermute | solution.py:157
  112.5 9.3 %collective-permute-start.29 = (bf16[2,5,64,128]{3,2,1,0:T(8,128)(2,1)S(1)}, bf16[2,5,64,128]{3,2,1,0:T(8,128)(2,1)S(1)}, u32[]{:S(2)}, u32[]{:S(2)}) collective-permute-start(bf16[2,5,64,128]{3,2,1,0:T(8,128)(2,1)S(1)} %get-tuple-element.42.refs_12_), channel_id=1, source_target_pairs={{0,16},{4,20},{8,24},{12,28},{16,0},{20,4},{24,8},{28,12},{1,17},{... | collective-permute-start | bytes 491528 | tf_op jit(solution)/shard_map/ppermute | solution.py:162
  121.8 6.1 %collective-permute-start.30 = (bf16[2,5,64,128]{3,2,1,0:T(8,128)(2,1)S(1)}, bf16[2,5,64,128]{3,2,1,0:T(8,128)(2,1)S(1)}, u32[]{:S(2)}, u32[]{:S(2)}) collective-permute-start(bf16[2,5,64,128]{3,2,1,0:T(8,128)(2,1)S(1)} %get-tuple-element.42.refs_12_), channel_id=1, source_target_pairs={{0,24},{4,28},{8,0},{12,4},{16,8},{20,12},{24,16},{28,20},{1,25},{... | collective-permute-start | bytes 491528 | tf_op jit(solution)/shard_map/ppermute | solution.py:162
  127.9 4.2 %collective-permute-start.31 = (bf16[2,5,64,128]{3,2,1,0:T(8,128)(2,1)S(1)}, bf16[2,5,64,128]{3,2,1,0:T(8,128)(2,1)S(1)}, u32[]{:S(2)}, u32[]{:S(2)}) collective-permute-start(bf16[2,5,64,128]{3,2,1,0:T(8,128)(2,1)S(1)} %get-tuple-element.42.refs_12_), channel_id=1, source_target_pairs={{0,4},{4,0},{8,12},{12,8},{16,20},{20,16},{24,28},{28,24},{1,5},{5... | collective-permute-start | bytes 491528 | tf_op jit(solution)/shard_map/ppermute | solution.py:157
  (13 other events, 142.1 us)

commit v5 on v4

--- a/solution.py
+++ b/solution.py
@@ -360,16 +360,37 @@
         out[mask - 1] = total
 
 
+def assemble_kernel(steps, tokens, *refs):
+    place = position()
+    columns, halves, mirrored, lent, outs = refs[:2], refs[2:6], refs[6:8], refs[8:12], refs[12:]
+    width = outs[0].shape[-1]
+    every = 2 * steps * tokens
+    lanes = pl.ds(pl.multiple_of(place[1] * width, 128), width)
+    for index in range(2 * steps):
+        rows = slice(index * tokens, (index + 1) * tokens)
+        outs[0][rows, :] = columns[index // steps][index % steps, :, lanes]
+        rows = slice(every + index * tokens, every + (index + 1) * tokens)
+        outs[0][rows, :] = mirrored[index // steps][index % steps, :, lanes]
+        for way in range(2):
+            both = slice(way * every + index * tokens, way * every + (index + 1) * tokens)
+
+            @pl.when(place[3 + way] == place[1])
+            def _():
+                outs[1][both, :] = halves[2 * (index // steps) + way][index % steps]
+
+            @pl.when(place[3 + way] != place[1])
+            def _():
+                outs[1][both, :] = lent[2 * (index // steps) + way][index % steps]
+
+
 def weight_kernel(sections, steps, tokens, *refs):
     place = position()
-    columns, halves, refs = refs[:2], refs[2:6], refs[6:]
-    mirrored, lent, refs = refs[:2], refs[2:6], refs[6:]
+    inputs, cots, refs = refs[0], refs[1], refs[2:]
     sent, refs = refs[: 2 * steps], refs[2 * steps :]
     own_slice, fetched, lent_slices = refs[0], refs[:sections], refs[sections - 1 :]
     out, lefts, rights, steers = refs[2 * sections - 1 :]
-    width, head = out.shape[1:]
+    _, head = out.shape[1:]
     every = 2 * steps * tokens
-    lanes = pl.ds(pl.multiple_of(place[1] * width, 128), width)
     for index in range(2 * steps):
         rows = slice(index * tokens, (index + 1) * tokens)
         for way in range(2):
@@ -378,21 +399,7 @@
             both = slice(way * every + index * tokens, way * every + (index + 1) * tokens)
             lefts[0, both, :] = sent[index][way, 0]
             lefts[1, both, :] = sent[index][way, sections]
-        rights[rows, :] = columns[index // steps][index % steps, :, lanes]
-        rows = slice(every + index * tokens, every + (index + 1) * tokens)
-        rights[rows, :] = mirrored[index // steps][index % steps, :, lanes]
-    out[0] = contract(lefts[0], rights[...], 0, 0).T
-    for index in range(2 * steps):
-        for way in range(2):
-            both = slice(way * every + index * tokens, way * every + (index + 1) * tokens)
-
-            @pl.when(place[3 + way] == place[1])
-            def _():
-                rights[both, :] = halves[2 * (index // steps) + way][index % steps]
-
-            @pl.when(place[3 + way] != place[1])
-            def _():
-                rights[both, :] = lent[2 * (index // steps) + way][index % steps]
+    out[0] = contract(lefts[0], inputs[...], 0, 0).T
 
     def corrected(here, way):
         rows = slice(way * every, (way + 1) * every)
@@ -407,7 +414,11 @@
                 blocks.append(fetched[holder ^ here][place[2]])
         steer = steers[way, :, : len(blocks) * head]
         total = contract(steer, jnp.concatenate(blocks, axis=1), 1, 1)
-        rights[rows, :] = (rights[rows, :].astype(jnp.float32) + total).astype(jnp.bfloat16)
+        rights[rows, :] = (cots[rows, :].astype(jnp.float32) + total).astype(jnp.bfloat16)
+
+    @pl.when(place[0] == sections - 1)
+    def _():
+        rights[...] = cots[...]
 
     for here in range(sections - 1):
 
@@ -598,9 +609,25 @@
     )(cot, steer, own, own_values, *fetched[1:], *lent_back[1:])
 
     every = replicas * tokens
+    assembled = pl.pallas_call(
+        functools.partial(assemble_kernel, steps, tokens),
+        in_specs=[memory] * 12,
+        out_specs=[memory] * 2,
+        out_shape=[jax.ShapeDtypeStruct((2 * every, width), jnp.bfloat16)] * 2,
+        compiler_params=pltpu.CompilerParams(vmem_limit_bytes=12 << 20),
+    )(
+        downward,
+        far_columns,
+        *sideways,
+        *far_halves,
+        near_mirror,
+        far_mirror,
+        *near_aside,
+        *far_aside,
+    )
     weight_grads = pl.pallas_call(
         functools.partial(weight_kernel, sections, steps, tokens),
-        in_specs=[memory] * (2 * steps + 2 * sections + 11),
+        in_specs=[memory] * (2 * steps + 2 * sections + 1),
         out_specs=memory,
         out_shape=jax.ShapeDtypeStruct((2, width, head), jnp.float32),
         scratch_shapes=[
@@ -610,14 +637,7 @@
         ],
         compiler_params=pltpu.CompilerParams(vmem_limit_bytes=20 << 20),
     )(
-        downward,
-        far_columns,
-        *sideways,
-        *far_halves,
-        near_mirror,
-        far_mirror,
-        *near_aside,
-        *far_aside,
+        *assembled,
         *near_sent,
         *far_sent,
         own_slice,

time: 135 us -> 116 us (0.86)
  waiting for transfers between devices: 73.9 us -> 57.4 us
  starting transfers between devices: 35.1 us -> 32.2 us
    ppermute x2, waiting for transfers between devices: 22.1 us -> 4.98 us  [gathered(): lent.append(lax.ppermute(own_slice, SECTION, route) if route else own_slice)]
    ppermute x9, waiting for transfers between devices: 29.6 us -> 36.5 us  [shifted(): lax.ppermute(block, 'dp', [(i, (i + 2 * distance) % count) for i in range...]
    ppermute x26, waiting for transfers between devices: 22.2 us -> 15.9 us  [swapped(): lax.ppermute(block, axis, [(i, i ^ mask) for i in range(lax.axis_size(axi...]
    ppermute x9, starting transfers between devices: 16.5 us -> 12.8 us  [shifted(): lax.ppermute(block, 'dp', [(i, (i + 2 * distance) % count) for i in range...]
  transfers between devices with their start and end apart: 37 -> 37, of which waited for: 12 -> 14; matrix products, arithmetic and copies ran while one was open for 0% -> 0% of each run, Pallas kernels for 10% -> 12%
where the time goes in v5:
time: 116 us; the launch traced here: 115 us
  waiting for transfers between devices  57.4 us (49%)
  starting transfers between devices  32.2 us (28%)
  Pallas kernels  18.2 us (16%)
  local copies, waits for them, and re-layouts  6.84 us (6%)
    ppermute x9, waiting for transfers between devices, shifted(): lax.ppermute(block, 'dp', [(i, (i + 2 * distance) % count) for i in range...  36.5 us
    ppermute x26, starting transfers between devices, swapped(): lax.ppermute(block, axis, [(i, i ^ mask) for i in range(lax.axis_size(axi...  16.6 us
    ppermute x26, waiting for transfers between devices, swapped(): lax.ppermute(block, axis, [(i, i ^ mask) for i in range(lax.axis_size(axi...  15.9 us
    ppermute x9, starting transfers between devices, shifted(): lax.ppermute(block, 'dp', [(i, (i + 2 * distance) % count) for i in range...  12.8 us
    unnamed x16, local copies, waits for them, and re-layouts  6.84 us
    ppermute x2, waiting for transfers between devices, gathered(): lent.append(lax.ppermute(own_slice, SECTION, route) if route else own_slice)  4.98 us
    pallas_call x1, Pallas kernels, gathered(): pl.pallas_call(functools.partial(heads_kernel, length), grid=(blocks,), i...  4.57 us
    pallas_call x1, Pallas kernels, gathered(): pl.pallas_call(functools.partial(input_kernel, sections, tokens), grid=(s...  3.2 us
  transfers between devices with their start and end apart: 37, of which 14 were waited for; matrix products, arithmetic and copies ran while one was open for 0% of the time, Pallas kernels for 12%

profile of v5, /device:TPU:0, one launch (start us, length us, event | category | flops | bytes accessed | tf_op | source)
XLA Modules:
  0.0 115.5 jit_solution(14774388086424819408)
XLA Ops:
  0.6 1.5 %shard_map.84 = (bf16[2,64,1024]{2,1,0:T(8,128)(2,1)S(1)}, bf16[2,64,1024]{2,1,0:T(8,128)(2,1)S(1)}, bf16[2,64,1024]{2,1,0:T(8,128)(2,1)S(1)}, bf16[2,64,1024]{2...) custom-call(bf16[2,64,4096]{2,1,0:T(8,128)(2,1)} %bitcast.15, ...), custom_call_target="tpu_custom_call" | custom-call | tf_op jit(solution)/shard_map/pallas_call | solution.py:466
  2.1 3.1 %collective-permute-start.17 = (bf16[2,64,512]{2,1,0:T(8,128)(2,1)S(1)}, bf16[2,64,512]{2,1,0:T(8,128)(2,1)S(1)}, u32[]{:S(2)}, u32[]{:S(2)}) collective-permute-start(bf16[2,64,512]{2,1,0:T(8,128)(2,1)S(1)} %get-tuple-element.39), channel_id=1, source_target_pairs={{0,8},{4,12},{8,16},{12,20},{16,24},{20,28},{24,0},{28,4},{1,9},{5... | collective-permute-start | bytes 393224 | tf_op jit(solution)/shard_map/ppermute | solution.py:162
  5.2 2.2 %copy-done = bf16[1,2,2,4096,128]{4,3,2,1,0:T(8,128)(2,1)S(1)} copy-done((bf16[1,2,2,4096,128]{4,3,2,1,0:T(8,128)(2,1)S(1)}, bf16[1,2,2,4096,128]{4,3,2,1,0:T(8,128)(2,1)}, u32[]{:S(2)}) %copy-start) | copy-done | bytes 4194328
  7.4 1.2 %copy-done.2 = bf16[2,2,32,4096]{3,2,1,0:T(8,128)(2,1)S(1)} copy-done((bf16[2,2,32,4096]{3,2,1,0:T(8,128)(2,1)S(1)}, bf16[2,2,32,4096]{3,2,1,0:T(8,128)(2,1)}, u32[]{:S(2)}) %copy-start.2) | copy-done | bytes 1048600
  8.6 1.2 %copy-done.4 = bf16[1,2,2,32,4096]{4,3,2,1,0:T(8,128)(2,1)S(1)} copy-done((bf16[1,2,2,32,4096]{4,3,2,1,0:T(8,128)(2,1)S(1)}, bf16[1,2,2,32,4096]{4,3,2,1,0:T(8,128)(2,1)}, u32[]{:S(2)}) %copy-start.4) | copy-done | bytes 1048600
  12.1 4.6 %shard_map.81 = (bf16[192,128]{1,0:T(8,128)(2,1)S(1)}, bf16[320,128]{1,0:T(8,128)(2,1)S(1)}) custom-call(s32[2,2]{1,0:T(2,128)S(1)} %copy-done.7, bf16[2,64,4096]{2,1,0:T(8,128)(2,1)S(1)} %bitcast.16, bf16[2,64,4096]{2,1,0:T(8,128)(2,1)S(1)} %bitcast.13, bf16[2,2,4096,128]{3,2,1,0:T(8,128)(2,1)S(1)} %bitcast.9, bf16[2,64,128]{2,1,0:T(8,128)(2,1)S(1)} %bitcast.17, ...), custom_call_target="tpu_custom_call" | custom-call | tf_op jit(solution)/shard_map/pallas_call | solution.py:502
  16.6 2.5 %collective-permute-start.9 = (bf16[320,128]{1,0:T(8,128)(2,1)S(1)}, bf16[320,128]{1,0:T(8,128)(2,1)S(1)}, u32[]{:S(2)}, u32[]{:S(2)}) collective-permute-start(bf16[320,128]{1,0:T(8,128)(2,1)S(1)} %get-tuple-element.29.refs_4_), channel_id=1, source_target_pairs={{0,3},{1,2},{2,1},{3,0},{4,7},{5,6},{6,5},{7,4},{8,11},{9,10},{10,... | collective-permute-start | bytes 245768 | tf_op jit(solution)/shard_map/ppermute | solution.py:157
  19.1 2.6 %collective-permute-start.18 = (bf16[2,64,512]{2,1,0:T(8,128)(2,1)S(1)}, bf16[2,64,512]{2,1,0:T(8,128)(2,1)S(1)}, u32[]{:S(2)}, u32[]{:S(2)}) collective-permute-start(bf16[2,64,512]{2,1,0:T(8,128)(2,1)S(1)} %get-tuple-element.40), channel_id=1, source_target_pairs={{0,16},{4,20},{8,24},{12,28},{16,0},{20,4},{24,8},{28,12},{1,17},{... | collective-permute-start | bytes 393224 | tf_op jit(solution)/shard_map/ppermute | solution.py:162
  22.8 1.4 %shard_map.78 = (bf16[4,512,128]{2,1,0:T(8,128)(2,1)S(1)}, bf16[4,512,128]{2,1,0:T(8,128)(2,1)S(1)}, bf16[4,512,128]{2,1,0:T(8,128)(2,1)S(1)}) custom-call(bf16[2,2,4,2,512,128]{5,4,3,2,1,0:T(8,128)(2,1)} %bitcast.8), custom_call_target="tpu_custom_call" | custom-call | tf_op jit(solution)/shard_map/pallas_call | solution.py:452
  24.2 1.6 %collective-permute-done.7.refs_5_ = bf16[192,128]{1,0:T(8,128)(2,1)S(1)} collective-permute-done((bf16[192,128]{1,0:T(8,128)(2,1)S(1)}, bf16[192,128]{1,0:T(8,128)(2,1)S(1)}, u32[]{:S(2)}, u32[]{:S(2)}) %collective-permute-start.7) | collective-permute-done | bytes 49184 | tf_op jit(solution)/shard_map/ppermute | solution.py:157
  26.4 1.3 %collective-permute-start.19 = (bf16[2,64,512]{2,1,0:T(8,128)(2,1)S(1)}, bf16[2,64,512]{2,1,0:T(8,128)(2,1)S(1)}, u32[]{:S(2)}, u32[]{:S(2)}) collective-permute-start(bf16[2,64,512]{2,1,0:T(8,128)(2,1)S(1)} %get-tuple-element.41), channel_id=1, source_target_pairs={{0,24},{4,28},{8,0},{12,4},{16,8},{20,12},{24,16},{28,20},{1,25},{... | collective-permute-start | bytes 393224 | tf_op jit(solution)/shard_map/ppermute | solution.py:162
  27.7 0.9 collective-permute-start.1
  28.7 2.0 %collective-permute-start.2 = (bf16[4,512,128]{2,1,0:T(8,128)(2,1)S(1)}, bf16[4,512,128]{2,1,0:T(8,128)(2,1)S(1)}, u32[]{:S(2)}, u32[]{:S(2)}) collective-permute-start(bf16[4,512,128]{2,1,0:T(8,128)(2,1)S(1)} %get-tuple-element.28), channel_id=1, source_target_pairs={{0,3},{1,2},{2,1},{3,0},{4,7},{5,6},{6,5},{7,4},{8,11},{9,10},{10,... | collective-permute-start | bytes 1572872 | tf_op jit(solution)/shard_map/ppermute | solution.py:157
  31.7 10.0 %collective-permute-done.13.refs_1_ = bf16[2,64,1024]{2,1,0:T(8,128)(2,1)S(1)} collective-permute-done((bf16[2,64,1024]{2,1,0:T(8,128)(2,1)S(1)}, bf16[2,64,1024]{2,1,0:T(8,128)(2,1)S(1)}, u32[]{:S(2)}, u32[]{:S(2)}) %collective-permute-start.13) | collective-permute-done | bytes 262176 | tf_op jit(solution)/shard_map/ppermute | solution.py:162
  42.5 6.3 %collective-permute-done.14.refs_2_ = bf16[2,64,1024]{2,1,0:T(8,128)(2,1)S(1)} collective-permute-done((bf16[2,64,1024]{2,1,0:T(8,128)(2,1)S(1)}, bf16[2,64,1024]{2,1,0:T(8,128)(2,1)S(1)}, u32[]{:S(2)}, u32[]{:S(2)}) %collective-permute-start.14) | collective-permute-done | bytes 262176 | tf_op jit(solution)/shard_map/ppermute | solution.py:162
  48.8 1.3 %collective-permute-start.24 = (bf16[4,64,512]{2,1,0:T(8,128)(2,1)S(1)}, bf16[4,64,512]{2,1,0:T(8,128)(2,1)S(1)}, u32[]{:S(2)}, u32[]{:S(2)}) collective-permute-start(bf16[4,64,512]{2,1,0:T(8,128)(2,1)S(1)} %get-tuple-element.42.refs_2_), channel_id=1, source_target_pairs={{0,2},{1,3},{2,0},{3,1},{4,6},{5,7},{6,4},{7,5},{8,10},{9,11},{10,... | collective-permute-start | bytes 786440 | tf_op jit(solution)/shard_map/ppermute | solution.py:157
  50.5 1.4 %collective-permute-start.35 = (bf16[512,128]{1,0:T(8,128)(2,1)S(1)}, bf16[512,128]{1,0:T(8,128)(2,1)S(1)}, u32[]{:S(2)}, u32[]{:S(2)}) collective-permute-start(bf16[512,128]{1,0:T(8,128)(2,1)S(1)} %get-tuple-element.47.refs_10_.refs_16_), channel_id=1, source_target_pairs={{1,0},{5,4},{9,8},{13,12},{17,16},{21,20},{25,24},{29,28}} | collective-permute-start | bytes 393224 | tf_op jit(solution)/shard_map/ppermute | solution.py:575
  51.9 2.7 %collective-permute-start.25 = (bf16[4,64,512]{2,1,0:T(8,128)(2,1)S(1)}, bf16[4,64,512]{2,1,0:T(8,128)(2,1)S(1)}, u32[]{:S(2)}, u32[]{:S(2)}) collective-permute-start(bf16[4,64,512]{2,1,0:T(8,128)(2,1)S(1)} %get-tuple-element.43.refs_3_), channel_id=1, source_target_pairs={{0,1},{1,0},{2,3},{3,2},{4,5},{5,4},{6,7},{7,6},{8,9},{9,8},{10,11... | collective-permute-start | bytes 786440 | tf_op jit(solution)/shard_map/ppermute | solution.py:157
  56.6 2.3 %collective-permute-done.35.refs_14_ = bf16[512,128]{1,0:T(8,128)(2,1)S(1)} collective-permute-done((bf16[512,128]{1,0:T(8,128)(2,1)S(1)}, bf16[512,128]{1,0:T(8,128)(2,1)S(1)}, u32[]{:S(2)}, u32[]{:S(2)}) %collective-permute-start.35) | collective-permute-done | bytes 131104 | tf_op jit(solution)/shard_map/ppermute | solution.py:575
  59.7 4.8 %collective-permute-done.25.refs_9_ = bf16[4,64,512]{2,1,0:T(8,128)(2,1)S(1)} collective-permute-done((bf16[4,64,512]{2,1,0:T(8,128)(2,1)S(1)}, bf16[4,64,512]{2,1,0:T(8,128)(2,1)S(1)}, u32[]{:S(2)}, u32[]{:S(2)}) %collective-permute-start.25) | collective-permute-done | bytes 262176 | tf_op jit(solution)/shard_map/ppermute | solution.py:157
  66.8 2.7 %collective-permute-start.6 = (bf16[3,128,128]{2,1,0:T(8,128)(2,1)S(1)}, bf16[3,128,128]{2,1,0:T(8,128)(2,1)S(1)}, u32[]{:S(2)}, u32[]{:S(2)}) collective-permute-start(bf16[3,128,128]{2,1,0:T(8,128)(2,1)S(1)} %shard_map.80.refs_0_), channel_id=1, source_target_pairs={{0,3},{1,2},{2,1},{3,0},{4,7},{5,6},{6,5},{7,4},{8,11},{9,10},{10,... | collective-permute-start | bytes 294920 | tf_op jit(solution)/shard_map/ppermute | solution.py:157
  69.5 7.8 %collective-permute-done.4.refs_1_ = bf16[3,128,128]{2,1,0:T(8,128)(2,1)S(1)} collective-permute-done((bf16[3,128,128]{2,1,0:T(8,128)(2,1)S(1)}, bf16[3,128,128]{2,1,0:T(8,128)(2,1)S(1)}, u32[]{:S(2)}, u32[]{:S(2)}) %collective-permute-start.4) | collective-permute-done | bytes 98336 | tf_op jit(solution)/shard_map/ppermute | solution.py:157
  77.9 1.6 %shard_map.82 = (bf16[2,5,64,128]{3,2,1,0:T(8,128)(2,1)S(1)}, bf16[128,384]{1,0:T(8,128)(2,1)S(1)}, bf16[2,64,128]{2,1,0:T(8,128)(2,1)S(1)}) custom-call(bf16[3,128,128]{2,1,0:T(8,128)(2,1)S(1)} %shard_map.80.refs_0_, bf16[3,128,128]{2,1,0:T(8,128)(2,1)S(1)} %collective-permute-done.4.refs_1_, bf16[3,128,128]{2,1,0:T(8,128)(2,1)S(1)} %collective-permute-done.5.refs_2_, ...), custom_call_target="tpu_custom_call" | custom-call | tf_op jit(solution)/shard_map/pallas_call | solution.py:577
  79.5 2.6 %collective-permute-start.28 = (bf16[2,5,64,128]{3,2,1,0:T(8,128)(2,1)S(1)}, bf16[2,5,64,128]{3,2,1,0:T(8,128)(2,1)S(1)}, u32[]{:S(2)}, u32[]{:S(2)}) collective-permute-start(bf16[2,5,64,128]{3,2,1,0:T(8,128)(2,1)S(1)} %get-tuple-element.46.refs_2_), channel_id=1, source_target_pairs={{0,8},{4,12},{8,16},{12,20},{16,24},{20,28},{24,0},{28,4},{1,9},{5... | collective-permute-start | bytes 491528 | tf_op jit(solution)/shard_map/ppermute | solution.py:162
  82.2 7.3 %collective-permute-done.28.refs_3_ = bf16[2,5,64,128]{3,2,1,0:T(8,128)(2,1)S(1)} collective-permute-done((bf16[2,5,64,128]{3,2,1,0:T(8,128)(2,1)S(1)}, bf16[2,5,64,128]{3,2,1,0:T(8,128)(2,1)S(1)}, u32[]{:S(2)}, u32[]{:S(2)}) %collective-permute-start.28) | collective-permute-done | bytes 163872 | tf_op jit(solution)/shard_map/ppermute | solution.py:162
  89.5 8.9 %collective-permute-done.29.refs_4_ = bf16[2,5,64,128]{3,2,1,0:T(8,128)(2,1)S(1)} collective-permute-done((bf16[2,5,64,128]{3,2,1,0:T(8,128)(2,1)S(1)}, bf16[2,5,64,128]{3,2,1,0:T(8,128)(2,1)S(1)}, u32[]{:S(2)}, u32[]{:S(2)}) %collective-permute-start.29) | collective-permute-done | bytes 163872 | tf_op jit(solution)/shard_map/ppermute | solution.py:162
  98.4 2.4 %collective-permute-start.30 = (bf16[2,5,64,128]{3,2,1,0:T(8,128)(2,1)S(1)}, bf16[2,5,64,128]{3,2,1,0:T(8,128)(2,1)S(1)}, u32[]{:S(2)}, u32[]{:S(2)}) collective-permute-start(bf16[2,5,64,128]{3,2,1,0:T(8,128)(2,1)S(1)} %get-tuple-element.46.refs_2_), channel_id=1, source_target_pairs={{0,24},{4,28},{8,0},{12,4},{16,8},{20,12},{24,16},{28,20},{1,25},{... | collective-permute-start | bytes 491528 | tf_op jit(solution)/shard_map/ppermute | solution.py:162
  100.7 3.8 %collective-permute-done.30.refs_5_ = bf16[2,5,64,128]{3,2,1,0:T(8,128)(2,1)S(1)} collective-permute-done((bf16[2,5,64,128]{3,2,1,0:T(8,128)(2,1)S(1)}, bf16[2,5,64,128]{3,2,1,0:T(8,128)(2,1)S(1)}, u32[]{:S(2)}, u32[]{:S(2)}) %collective-permute-start.30) | collective-permute-done | bytes 163872 | tf_op jit(solution)/shard_map/ppermute | solution.py:162
  105.5 1.3 %collective-permute-start.36 = (bf16[512,128]{1,0:T(8,128)(2,1)S(1)}, bf16[512,128]{1,0:T(8,128)(2,1)S(1)}, u32[]{:S(2)}, u32[]{:S(2)}) collective-permute-start(bf16[512,128]{1,0:T(8,128)(2,1)S(1)} %get-tuple-element.47.refs_10_.refs_16_), channel_id=1, source_target_pairs={{2,0},{6,4},{10,8},{14,12},{18,16},{22,20},{26,24},{30,28}} | collective-permute-start | bytes 393224 | tf_op jit(solution)/shard_map/ppermute | solution.py:575
  106.8 3.2 %shard_map.83 = bf16[2,64,4096]{2,1,0:T(8,128)(2,1)} custom-call(bf16[2,64,4096]{2,1,0:T(8,128)(2,1)S(1)} %bitcast.14, bf16[128,384]{1,0:T(8,128)(2,1)S(1)} %get-tuple-element.31.steer, bf16[2,64,128]{2,1,0:T(8,128)(2,1)S(1)} %get-tuple-element.32.own, bf16[2,4096,128]{2,1,0:T(8,128)(2,1)S(1)} %get-tuple-element.33.held, ...), custom_call_target="tpu_custom_call" | custom-call | tf_op jit(solution)/shard_map/pallas_call | solution.py:596
  110.2 2.6 %collective-permute-done.36.refs_15_ = bf16[512,128]{1,0:T(8,128)(2,1)S(1)} collective-permute-done((bf16[512,128]{1,0:T(8,128)(2,1)S(1)}, bf16[512,128]{1,0:T(8,128)(2,1)S(1)}, u32[]{:S(2)}, u32[]{:S(2)}) %collective-permute-start.36) | collective-permute-done | bytes 131104 | tf_op jit(solution)/shard_map/ppermute | solution.py:575
  112.9 2.6 %shard_map.89 = f32[2,512,128]{2,1,0:T(8,128)} custom-call(bf16[1024,512]{1,0:T(8,128)(2,1)S(1)} %get-tuple-element.44.refs_0_, bf16[1024,512]{1,0:T(8,128)(2,1)S(1)} %get-tuple-element.45.refs_1_, bf16[2,5,64,128]{3,2,1,0:T(8,128)(2,1)S(1)} %get-tuple-element.46.refs_2_, bf16[2,5,64,128]{3,2,1,0:T(8,128)(2,1)S(1)} %collective-permute-done.28.refs_3_, ...), custom_call_target="tpu_custom_call" | custom-call | tf_op jit(solution)/shard_map/pallas_call | solution.py:628
  (71 shorter events, 12.7 us)
Async XLA Ops:
  2.1 26.5 %collective-permute-start.17 = (bf16[2,64,512]{2,1,0:T(8,128)(2,1)S(1)}, bf16[2,64,512]{2,1,0:T(8,128)(2,1)S(1)}, u32[]{:S(2)}, u32[]{:S(2)}) collective-permute-start(bf16[2,64,512]{2,1,0:T(8,128)(2,1)S(1)} %get-tuple-element.39), channel_id=1, source_target_pairs={{0,8},{4,12},{8,16},{12,20},{16,24},{20,28},{24,0},{28,4},{1,9},{5... | collective-permute-start | bytes 393224 | tf_op jit(solution)/shard_map/ppermute | solution.py:162
  16.6 11.1 %collective-permute-start.9 = (bf16[320,128]{1,0:T(8,128)(2,1)S(1)}, bf16[320,128]{1,0:T(8,128)(2,1)S(1)}, u32[]{:S(2)}, u32[]{:S(2)}) collective-permute-start(bf16[320,128]{1,0:T(8,128)(2,1)S(1)} %get-tuple-element.29.refs_4_), channel_id=1, source_target_pairs={{0,3},{1,2},{2,1},{3,0},{4,7},{5,6},{6,5},{7,4},{8,11},{9,10},{10,... | collective-permute-start | bytes 245768 | tf_op jit(solution)/shard_map/ppermute | solution.py:157
  19.1 11.5 %collective-permute-start.18 = (bf16[2,64,512]{2,1,0:T(8,128)(2,1)S(1)}, bf16[2,64,512]{2,1,0:T(8,128)(2,1)S(1)}, u32[]{:S(2)}, u32[]{:S(2)}) collective-permute-start(bf16[2,64,512]{2,1,0:T(8,128)(2,1)S(1)} %get-tuple-element.40), channel_id=1, source_target_pairs={{0,16},{4,20},{8,24},{12,28},{16,0},{20,4},{24,8},{28,12},{1,17},{... | collective-permute-start | bytes 393224 | tf_op jit(solution)/shard_map/ppermute | solution.py:162
  25.8 24.7 %collective-permute-start = (bf16[4,512,128]{2,1,0:T(8,128)(2,1)S(1)}, bf16[4,512,128]{2,1,0:T(8,128)(2,1)S(1)}, u32[]{:S(2)}, u32[]{:S(2)}) collective-permute-start(bf16[4,512,128]{2,1,0:T(8,128)(2,1)S(1)} %get-tuple-element.26), channel_id=1, source_target_pairs={{0,1},{1,0},{2,3},{3,2},{4,5},{5,4},{6,7},{7,6},{8,9},{9,8},{10,11... | collective-permute-start | bytes 1572872 | tf_op jit(solution)/shard_map/ppermute | solution.py:157
  26.4 5.2 %collective-permute-start.19 = (bf16[2,64,512]{2,1,0:T(8,128)(2,1)S(1)}, bf16[2,64,512]{2,1,0:T(8,128)(2,1)S(1)}, u32[]{:S(2)}, u32[]{:S(2)}) collective-permute-start(bf16[2,64,512]{2,1,0:T(8,128)(2,1)S(1)} %get-tuple-element.41), channel_id=1, source_target_pairs={{0,24},{4,28},{8,0},{12,4},{16,8},{20,12},{24,16},{28,20},{1,25},{... | collective-permute-start | bytes 393224 | tf_op jit(solution)/shard_map/ppermute | solution.py:162
  27.7 24.2 %collective-permute-start.1 = (bf16[4,512,128]{2,1,0:T(8,128)(2,1)S(1)}, bf16[4,512,128]{2,1,0:T(8,128)(2,1)S(1)}, u32[]{:S(2)}, u32[]{:S(2)}) collective-permute-start(bf16[4,512,128]{2,1,0:T(8,128)(2,1)S(1)} %get-tuple-element.27), channel_id=1, source_target_pairs={{0,2},{1,3},{2,0},{3,1},{4,6},{5,7},{6,4},{7,5},{8,10},{9,11},{10,... | collective-permute-start | bytes 1572872 | tf_op jit(solution)/shard_map/ppermute | solution.py:157
  28.7 26.0 %collective-permute-start.2 = (bf16[4,512,128]{2,1,0:T(8,128)(2,1)S(1)}, bf16[4,512,128]{2,1,0:T(8,128)(2,1)S(1)}, u32[]{:S(2)}, u32[]{:S(2)}) collective-permute-start(bf16[4,512,128]{2,1,0:T(8,128)(2,1)S(1)} %get-tuple-element.28), channel_id=1, source_target_pairs={{0,3},{1,2},{2,1},{3,0},{4,7},{5,6},{6,5},{7,4},{8,11},{9,10},{10,... | collective-permute-start | bytes 1572872 | tf_op jit(solution)/shard_map/ppermute | solution.py:157
  30.7 11.0 %collective-permute-start.13 = (bf16[2,64,1024]{2,1,0:T(8,128)(2,1)S(1)}, bf16[2,64,1024]{2,1,0:T(8,128)(2,1)S(1)}, u32[]{:S(2)}, u32[]{:S(2)}) collective-permute-start(bf16[2,64,1024]{2,1,0:T(8,128)(2,1)S(1)} %get-tuple-element.35), channel_id=1, source_target_pairs={{0,8},{4,12},{8,16},{12,20},{16,24},{20,28},{24,0},{28,4},{1,9},{5... | collective-permute-start | bytes 786440 | tf_op jit(solution)/shard_map/ppermute | solution.py:162
  31.6 17.2 %collective-permute-start.14 = (bf16[2,64,1024]{2,1,0:T(8,128)(2,1)S(1)}, bf16[2,64,1024]{2,1,0:T(8,128)(2,1)S(1)}, u32[]{:S(2)}, u32[]{:S(2)}) collective-permute-start(bf16[2,64,1024]{2,1,0:T(8,128)(2,1)S(1)} %get-tuple-element.36), channel_id=1, source_target_pairs={{0,16},{4,20},{8,24},{12,28},{16,0},{20,4},{24,8},{28,12},{1,17},{... | collective-permute-start | bytes 786440 | tf_op jit(solution)/shard_map/ppermute | solution.py:162
  41.7 13.6 %collective-permute-start.15 = (bf16[2,64,1024]{2,1,0:T(8,128)(2,1)S(1)}, bf16[2,64,1024]{2,1,0:T(8,128)(2,1)S(1)}, u32[]{:S(2)}, u32[]{:S(2)}) collective-permute-start(bf16[2,64,1024]{2,1,0:T(8,128)(2,1)S(1)} %get-tuple-element.37), channel_id=1, source_target_pairs={{0,24},{4,28},{8,0},{12,4},{16,8},{20,12},{24,16},{28,20},{1,25},{... | collective-permute-start | bytes 786440 | tf_op jit(solution)/shard_map/ppermute | solution.py:162
  48.8 10.8 %collective-permute-start.24 = (bf16[4,64,512]{2,1,0:T(8,128)(2,1)S(1)}, bf16[4,64,512]{2,1,0:T(8,128)(2,1)S(1)}, u32[]{:S(2)}, u32[]{:S(2)}) collective-permute-start(bf16[4,64,512]{2,1,0:T(8,128)(2,1)S(1)} %get-tuple-element.42.refs_2_), channel_id=1, source_target_pairs={{0,2},{1,3},{2,0},{3,1},{4,6},{5,7},{6,4},{7,5},{8,10},{9,11},{10,... | collective-permute-start | bytes 786440 | tf_op jit(solution)/shard_map/ppermute | solution.py:157
  50.5 8.4 %collective-permute-start.35 = (bf16[512,128]{1,0:T(8,128)(2,1)S(1)}, bf16[512,128]{1,0:T(8,128)(2,1)S(1)}, u32[]{:S(2)}, u32[]{:S(2)}) collective-permute-start(bf16[512,128]{1,0:T(8,128)(2,1)S(1)} %get-tuple-element.47.refs_10_.refs_16_), channel_id=1, source_target_pairs={{1,0},{5,4},{9,8},{13,12},{17,16},{21,20},{25,24},{29,28}} | collective-permute-start | bytes 393224 | tf_op jit(solution)/shard_map/ppermute | solution.py:575
  51.9 12.6 %collective-permute-start.25 = (bf16[4,64,512]{2,1,0:T(8,128)(2,1)S(1)}, bf16[4,64,512]{2,1,0:T(8,128)(2,1)S(1)}, u32[]{:S(2)}, u32[]{:S(2)}) collective-permute-start(bf16[4,64,512]{2,1,0:T(8,128)(2,1)S(1)} %get-tuple-element.43.refs_3_), channel_id=1, source_target_pairs={{0,1},{1,0},{2,3},{3,2},{4,5},{5,4},{6,7},{7,6},{8,9},{9,8},{10,11... | collective-permute-start | bytes 786440 | tf_op jit(solution)/shard_map/ppermute | solution.py:157
  54.6 9.9 %collective-permute-start.20 = (bf16[4,64,512]{2,1,0:T(8,128)(2,1)S(1)}, bf16[4,64,512]{2,1,0:T(8,128)(2,1)S(1)}, u32[]{:S(2)}, u32[]{:S(2)}) collective-permute-start(bf16[4,64,512]{2,1,0:T(8,128)(2,1)S(1)} %get-tuple-element.42.refs_2_), channel_id=1, source_target_pairs={{0,4},{4,0},{8,12},{12,8},{16,20},{20,16},{24,28},{28,24},{1,5},{5... | collective-permute-start | bytes 786440 | tf_op jit(solution)/shard_map/ppermute | solution.py:157
  55.3 9.7 %collective-permute-start.3 = (f32[3,128,128]{2,1,0:T(8,128)S(1)}, f32[3,128,128]{2,1,0:T(8,128)S(1)}, u32[]{:S(2)}, u32[]{:S(2)}) collective-permute-start(f32[3,128,128]{2,1,0:T(8,128)S(1)} %shard_map.79.near), channel_id=1, source_target_pairs={{0,4},{4,0},{8,12},{12,8},{16,20},{20,16},{24,28},{28,24},{1,5},{5... | collective-permute-start | bytes 589832 | tf_op jit(solution)/shard_map/ppermute | solution.py:157
  58.9 20.6 %collective-permute-start.22 = (bf16[4,64,1024]{2,1,0:T(8,128)(2,1)S(1)}, bf16[4,64,1024]{2,1,0:T(8,128)(2,1)S(1)}, u32[]{:S(2)}, u32[]{:S(2)}) collective-permute-start(bf16[4,64,1024]{2,1,0:T(8,128)(2,1)S(1)} %shard_map.87), channel_id=1, source_target_pairs={{0,3},{1,2},{2,1},{3,0},{4,7},{5,6},{6,5},{7,4},{8,11},{9,10},{10,... | collective-permute-start | bytes 1572872 | tf_op jit(solution)/shard_map/ppermute | solution.py:157
  59.6 22.6 %collective-permute-start.16 = (bf16[4,64,1024]{2,1,0:T(8,128)(2,1)S(1)}, bf16[4,64,1024]{2,1,0:T(8,128)(2,1)S(1)}, u32[]{:S(2)}, u32[]{:S(2)}) collective-permute-start(bf16[4,64,1024]{2,1,0:T(8,128)(2,1)S(1)} %shard_map.85.refs_0_), channel_id=1, source_target_pairs={{0,4},{4,0},{8,12},{12,8},{16,20},{20,16},{24,28},{28,24},{1,5},{5... | collective-permute-start | bytes 1572872 | tf_op jit(solution)/shard_map/ppermute | solution.py:157
  66.0 11.3 %collective-permute-start.4 = (bf16[3,128,128]{2,1,0:T(8,128)(2,1)S(1)}, bf16[3,128,128]{2,1,0:T(8,128)(2,1)S(1)}, u32[]{:S(2)}, u32[]{:S(2)}) collective-permute-start(bf16[3,128,128]{2,1,0:T(8,128)(2,1)S(1)} %shard_map.80.refs_0_), channel_id=1, source_target_pairs={{0,1},{1,0},{2,3},{3,2},{4,5},{5,4},{6,7},{7,6},{8,9},{9,8},{10,11... | collective-permute-start | bytes 294920 | tf_op jit(solution)/shard_map/ppermute | solution.py:157
  66.4 10.9 %collective-permute-start.5 = (bf16[3,128,128]{2,1,0:T(8,128)(2,1)S(1)}, bf16[3,128,128]{2,1,0:T(8,128)(2,1)S(1)}, u32[]{:S(2)}, u32[]{:S(2)}) collective-permute-start(bf16[3,128,128]{2,1,0:T(8,128)(2,1)S(1)} %shard_map.80.refs_0_), channel_id=1, source_target_pairs={{0,2},{1,3},{2,0},{3,1},{4,6},{5,7},{6,4},{7,5},{8,10},{9,11},{10,... | collective-permute-start | bytes 294920 | tf_op jit(solution)/shard_map/ppermute | solution.py:157
  66.8 11.0 %collective-permute-start.6 = (bf16[3,128,128]{2,1,0:T(8,128)(2,1)S(1)}, bf16[3,128,128]{2,1,0:T(8,128)(2,1)S(1)}, u32[]{:S(2)}, u32[]{:S(2)}) collective-permute-start(bf16[3,128,128]{2,1,0:T(8,128)(2,1)S(1)} %shard_map.80.refs_0_), channel_id=1, source_target_pairs={{0,3},{1,2},{2,1},{3,0},{4,7},{5,6},{6,5},{7,4},{8,11},{9,10},{10,... | collective-permute-start | bytes 294920 | tf_op jit(solution)/shard_map/ppermute | solution.py:157
  77.3 27.2 %collective-permute-start.10 = (bf16[4,512,128]{2,1,0:T(8,128)(2,1)S(1)}, bf16[4,512,128]{2,1,0:T(8,128)(2,1)S(1)}, u32[]{:S(2)}, u32[]{:S(2)}) collective-permute-start(bf16[4,512,128]{2,1,0:T(8,128)(2,1)S(1)} %collective-permute-done.refs_0_.refs_11_), channel_id=1, source_target_pairs={{0,4},{4,0},{8,12},{12,8},{16,20},{20,16},{24,28},{28,24},{1,5},{5... | collective-permute-start | bytes 1572872 | tf_op jit(solution)/shard_map/ppermute | solution.py:157
  77.3 27.7 %collective-permute-start.11 = (bf16[4,512,128]{2,1,0:T(8,128)(2,1)S(1)}, bf16[4,512,128]{2,1,0:T(8,128)(2,1)S(1)}, u32[]{:S(2)}, u32[]{:S(2)}) collective-permute-start(bf16[4,512,128]{2,1,0:T(8,128)(2,1)S(1)} %collective-permute-done.1.refs_1_.refs_12_), channel_id=1, source_target_pairs={{0,4},{4,0},{8,12},{12,8},{16,20},{20,16},{24,28},{28,24},{1,5},{5... | collective-permute-start | bytes 1572872 | tf_op jit(solution)/shard_map/ppermute | solution.py:157
  77.8 27.2 %collective-permute-start.12 = (bf16[4,512,128]{2,1,0:T(8,128)(2,1)S(1)}, bf16[4,512,128]{2,1,0:T(8,128)(2,1)S(1)}, u32[]{:S(2)}, u32[]{:S(2)}) collective-permute-start(bf16[4,512,128]{2,1,0:T(8,128)(2,1)S(1)} %collective-permute-done.2.refs_2_.refs_13_), channel_id=1, source_target_pairs={{0,4},{4,0},{8,12},{12,8},{16,20},{20,16},{24,28},{28,24},{1,5},{5... | collective-permute-start | bytes 1572872 | tf_op jit(solution)/shard_map/ppermute | solution.py:157
  79.5 9.9 %collective-permute-start.28 = (bf16[2,5,64,128]{3,2,1,0:T(8,128)(2,1)S(1)}, bf16[2,5,64,128]{3,2,1,0:T(8,128)(2,1)S(1)}, u32[]{:S(2)}, u32[]{:S(2)}) collective-permute-start(bf16[2,5,64,128]{3,2,1,0:T(8,128)(2,1)S(1)} %get-tuple-element.46.refs_2_), channel_id=1, source_target_pairs={{0,8},{4,12},{8,16},{12,20},{16,24},{20,28},{24,0},{28,4},{1,9},{5... | collective-permute-start | bytes 491528 | tf_op jit(solution)/shard_map/ppermute | solution.py:162
  82.2 23.3 %collective-permute-start.23 = (bf16[4,64,1024]{2,1,0:T(8,128)(2,1)S(1)}, bf16[4,64,1024]{2,1,0:T(8,128)(2,1)S(1)}, u32[]{:S(2)}, u32[]{:S(2)}) collective-permute-start(bf16[4,64,1024]{2,1,0:T(8,128)(2,1)S(1)} %collective-permute-done.22.refs_6_), channel_id=1, source_target_pairs={{0,4},{4,0},{8,12},{12,8},{16,20},{20,16},{24,28},{28,24},{1,5},{5... | collective-permute-start | bytes 1572872 | tf_op jit(solution)/shard_map/ppermute | solution.py:157
  89.5 8.9 %collective-permute-start.29 = (bf16[2,5,64,128]{3,2,1,0:T(8,128)(2,1)S(1)}, bf16[2,5,64,128]{3,2,1,0:T(8,128)(2,1)S(1)}, u32[]{:S(2)}, u32[]{:S(2)}) collective-permute-start(bf16[2,5,64,128]{3,2,1,0:T(8,128)(2,1)S(1)} %get-tuple-element.46.refs_2_), channel_id=1, source_target_pairs={{0,16},{4,20},{8,24},{12,28},{16,0},{20,4},{24,8},{28,12},{1,17},{... | collective-permute-start | bytes 491528 | tf_op jit(solution)/shard_map/ppermute | solution.py:162
  98.4 6.1 %collective-permute-start.30 = (bf16[2,5,64,128]{3,2,1,0:T(8,128)(2,1)S(1)}, bf16[2,5,64,128]{3,2,1,0:T(8,128)(2,1)S(1)}, u32[]{:S(2)}, u32[]{:S(2)}) collective-permute-start(bf16[2,5,64,128]{3,2,1,0:T(8,128)(2,1)S(1)} %get-tuple-element.46.refs_2_), channel_id=1, source_target_pairs={{0,24},{4,28},{8,0},{12,4},{16,8},{20,12},{24,16},{28,20},{1,25},{... | collective-permute-start | bytes 491528 | tf_op jit(solution)/shard_map/ppermute | solution.py:162
  104.5 8.4 %collective-permute-start.31 = (bf16[2,5,64,128]{3,2,1,0:T(8,128)(2,1)S(1)}, bf16[2,5,64,128]{3,2,1,0:T(8,128)(2,1)S(1)}, u32[]{:S(2)}, u32[]{:S(2)}) collective-permute-start(bf16[2,5,64,128]{3,2,1,0:T(8,128)(2,1)S(1)} %get-tuple-element.46.refs_2_), channel_id=1, source_target_pairs={{0,4},{4,0},{8,12},{12,8},{16,20},{20,16},{24,28},{28,24},{1,5},{5... | collective-permute-start | bytes 491528 | tf_op jit(solution)/shard_map/ppermute | solution.py:157
  104.5 8.4 %collective-permute-start.32 = (bf16[2,5,64,128]{3,2,1,0:T(8,128)(2,1)S(1)}, bf16[2,5,64,128]{3,2,1,0:T(8,128)(2,1)S(1)}, u32[]{:S(2)}, u32[]{:S(2)}) collective-permute-start(bf16[2,5,64,128]{3,2,1,0:T(8,128)(2,1)S(1)} %collective-permute-done.28.refs_3_), channel_id=1, source_target_pairs={{0,4},{4,0},{8,12},{12,8},{16,20},{20,16},{24,28},{28,24},{1,5},{5... | collective-permute-start | bytes 491528 | tf_op jit(solution)/shard_map/ppermute | solution.py:157
  105.0 7.9 %collective-permute-start.33 = (bf16[2,5,64,128]{3,2,1,0:T(8,128)(2,1)S(1)}, bf16[2,5,64,128]{3,2,1,0:T(8,128)(2,1)S(1)}, u32[]{:S(2)}, u32[]{:S(2)}) collective-permute-start(bf16[2,5,64,128]{3,2,1,0:T(8,128)(2,1)S(1)} %collective-permute-done.29.refs_4_), channel_id=1, source_target_pairs={{0,4},{4,0},{8,12},{12,8},{16,20},{20,16},{24,28},{28,24},{1,5},{5... | collective-permute-start | bytes 491528 | tf_op jit(solution)/shard_map/ppermute | solution.py:157
  105.1 7.8 %collective-permute-start.34 = (bf16[2,5,64,128]{3,2,1,0:T(8,128)(2,1)S(1)}, bf16[2,5,64,128]{3,2,1,0:T(8,128)(2,1)S(1)}, u32[]{:S(2)}, u32[]{:S(2)}) collective-permute-start(bf16[2,5,64,128]{3,2,1,0:T(8,128)(2,1)S(1)} %collective-permute-done.30.refs_5_), channel_id=1, source_target_pairs={{0,4},{4,0},{8,12},{12,8},{16,20},{20,16},{24,28},{28,24},{1,5},{5... | collective-permute-start | bytes 491528 | tf_op jit(solution)/shard_map/ppermute | solution.py:157
  105.5 7.4 %collective-permute-start.36 = (bf16[512,128]{1,0:T(8,128)(2,1)S(1)}, bf16[512,128]{1,0:T(8,128)(2,1)S(1)}, u32[]{:S(2)}, u32[]{:S(2)}) collective-permute-start(bf16[512,128]{1,0:T(8,128)(2,1)S(1)} %get-tuple-element.47.refs_10_.refs_16_), channel_id=1, source_target_pairs={{2,0},{6,4},{10,8},{14,12},{18,16},{22,20},{26,24},{30,28}} | collective-permute-start | bytes 393224 | tf_op jit(solution)/shard_map/ppermute | solution.py:575
  (13 other events, 114.6 us)
